TPU v7x, 32 devices: a whole 2x2x4 slice. The times are simulated.
32 devices in a mesh: dp: 16 (over z, x, core), tp: 2 (over y).
Axes of the slice: x: 2, y: 2, z: 4, core: 2. Of those that a mesh axis runs over, the one named last changes fastest.
Arguments:
- stash_values: bfloat16 [4096, 8192], P(('dp', 'tp')), may hold values from -127 to 127
- stash_scales: bfloat16 [4096, 64], P(('dp', 'tp')), may hold values from 0.001 to 0.13
- value_grad: bfloat16 [4096, 256], P('dp', 'tp'), may hold values from -19 to 19
Outputs:
- clipped_grad: float32 [8192, 256], P('dp', 'tp')
All inputs are finite; a program needn't handle non-finite values.
Results may differ from a plain program's by a relative error of at most 0.0019.
Values may be sent and summed in bfloat16 or wider, within the bound.
No kernel may reach another device: no remote copies, remote signals or barrier semaphores. Data moves between devices by JAX's collectives and lax.ppermute only.
A program may use at most 64 MiB of HBM per device.

v0:
```python
import jax
import jax.numpy as jnp
from jax import lax
from jax.sharding import PartitionSpec as P


def block_dequantize(values, scales):
    rows = values.shape[0]
    blocks = scales.shape[1]
    scaled = (
        values.astype(jnp.float32).reshape(rows, blocks, values.shape[1] // blocks)
        * scales.astype(jnp.float32)[:, :, None]
    )
    return scaled.reshape(rows, values.shape[1]).astype(jnp.bfloat16)


def body(stash_values, stash_scales, value_grad):
    width = stash_values.shape[1]
    columns = value_grad.shape[1]
    dp_count = lax.axis_size("dp")
    tp_count = lax.axis_size("tp")
    own_tokens = stash_values.shape[0]
    sub_rows = width // (dp_count * tp_count)
    inputs = block_dequantize(stash_values, stash_scales)
    inputs = inputs.reshape(own_tokens, dp_count, tp_count, sub_rows)
    features = lax.all_to_all(inputs, "tp", split_axis=2, concat_axis=0, tiled=True)
    features = features.reshape(own_tokens * tp_count, dp_count * sub_rows)
    all_heads = lax.dot_general(
        features,
        lax.all_gather(value_grad, "tp", axis=1, tiled=True),
        (((0,), (0,)), ((), ())),
        preferred_element_type=jnp.float32,
    )
    summed = lax.psum_scatter(all_heads, "dp", scatter_dimension=0, tiled=True)
    local = lax.all_to_all(summed, "tp", split_axis=1, concat_axis=0, tiled=True)
    total = lax.psum(jnp.sum(summed * summed), ("dp", "tp"))
    limit = jnp.sqrt(jnp.float32(width * columns * lax.axis_size("tp")))
    return local * jnp.minimum(jnp.float32(1.0), limit / jnp.sqrt(total))


def solution(mesh):
    placed = (P(("dp", "tp"), None), P(("dp", "tp"), None), P("dp", "tp"))
    return jax.shard_map(body, mesh=mesh, in_specs=placed, out_specs=P("dp", "tp"), check_vma=False)
```

profile of v0, /device:TPU:0, one launch (start us, length us, event | category | flops | bytes accessed | tf_op | source)
XLA Modules:
  0.0 181.6 jit_solution(3500669515704277287)
XLA Ops:
  6.5 0.8 copy.9
  7.3 0.0 copy-start
  7.4 1.1 mul.26
  8.5 0.4 copy-done
  8.9 3.8 %fusion = bf16[128,8192]{1,0:T(8,128)(2,1)} fusion(f32[16,8,64,128]{3,2,1,0:T(8,128)S(1)} %bitcast.22, bf16[128,8192]{1,0:T(8,128)(2,1)S(1)} %copy-done), kind=kLoop, calls=%fused_computation.1 | loop fusion | flops 3145728 | bytes 8388608 | tf_op jit(solution)/shard_map/convert_element_type | solution.py:14
  12.7 3.3 %reshape.16 = bf16[128,16,2,256]{3,2,1,0:T(2,128)(2,1)S(1)} reshape(bf16[128,8192]{1,0:T(8,128)(2,1)} %fusion) | data formatting | bytes 4194304 | tf_op jit(solution)/shard_map/reshape | solution.py:25
  16.0 1.7 copy.10
  17.7 0.0 copy-start.1
  17.7 4.4 %all-to-all-start = ((bf16[128,16,2,256]{3,1,0,2:T(8,128)(2,1)}), bf16[128,16,2,256]{3,1,0,2:T(8,128)(2,1)S(1)}, u32[]{:S(2)}, u32[]{:S(2)}) async-start(bf16[128,16,2,256]{3,1,0,2:T(8,128)(2,1)} %copy.10), calls=%async_computation | async-start | bytes 4194304 | tf_op jit(solution)/shard_map/all_to_all | solution.py:26
  22.1 0.0 reduce-scatter.2.cloned.1.call-start
  22.1 0.0 copy-done.1
  22.1 27.3 %all_gather.3 = bf16[256,256]{1,0:T(8,128)(2,1)S(1)} all-gather(bf16[256,128]{1,0:T(8,128)(2,1)S(1)} %copy-done.1), channel_id=1, replica_groups=mesh['dp'=16,'tp'=2] {'tp'}, dimensions={1}, use_global_device_ids=true | all-gather | bytes 196608 | tf_op jit(solution)/shard_map/all_gather | solution.py:30
  49.4 0.0 all-to-all-done
  49.4 0.9 copy.14
  50.3 2.7 %fusion.1 = f32[4096,256]{1,0:T(8,128)} fusion(bf16[256,4096]{1,0:T(8,128)(2,1)S(1)} %bitcast.23, bf16[256,256]{1,0:T(8,128)(2,1)S(1)} %all_gather.3), kind=kOutput, calls=%fused_computation.5 | convolution fusion | flops 536870912 | bytes 6422528 | tf_op jit(solution)/shard_map/dot_general | solution.py:28
  53.0 0.0 reduce-scatter.2.cloned.1.call-update
  53.1 73.4 %reduce-scatter.2.cloned.1.call-done = f32[256,256]{1,0:T(8,128)} async-done(((f32[4096,256]{1,0:T(8,128)}), f32[256,256]{1,0:T(8,128)}) %reduce-scatter.2.cloned.1.call-update) | async-done | bytes 262160 | tf_op jit(solution)/shard_map/reduce_scatter | solution.py:34
  126.5 1.7 copy_bitcast_fusion
  128.2 3.4 %all-to-all-start.1 = ((f32[256,2,128]{2,0,1:T(8,128)}), f32[256,2,128]{2,0,1:T(8,128)S(1)}, u32[]{:S(2)}, u32[]{:S(2)}) async-start(f32[256,2,128]{2,0,1:T(8,128)} %copy_bitcast_fusion), calls=%async_computation.2 | async-start | bytes 524288 | tf_op jit(solution)/shard_map/all_to_all | solution.py:35
  131.6 1.6 multiply_reduce_fusion
  133.2 40.2 %psum.7 = f32[]{:T(128)} all-reduce(f32[]{:T(128)} %multiply_reduce_fusion), channel_id=1, replica_groups=mesh['dp'=16,'tp'=2] {'dp','tp'}, use_global_device_ids=true, to_apply=%region_2.0 | all-reduce | flops 1 | bytes 8 | tf_op jit(solution)/shard_map/psum | solution.py:36
  174.0 0.0 all-to-all-done.1
  174.1 0.7 broadcast_multiply_fusion
Async XLA Ops:
  7.3 1.6 copy-start
  17.7 4.4 %copy-start.1 = (bf16[256,128]{1,0:T(8,128)(2,1)S(1)}, bf16[256,128]{1,0:T(8,128)(2,1)}, u32[]{:S(2)}) copy-start(bf16[256,128]{1,0:T(8,128)(2,1)} %param.5) | copy-start | bytes 196612
  17.7 31.7 %all-to-all-start = ((bf16[128,16,2,256]{3,1,0,2:T(8,128)(2,1)}), bf16[128,16,2,256]{3,1,0,2:T(8,128)(2,1)S(1)}, u32[]{:S(2)}, u32[]{:S(2)}) async-start(bf16[128,16,2,256]{3,1,0,2:T(8,128)(2,1)} %copy.10), calls=%async_computation | async-start | bytes 4194304 | tf_op jit(solution)/shard_map/all_to_all | solution.py:26
  22.1 104.4 %reduce-scatter.2.cloned.1.call-start = ((), (), s32[]{:S(2)}) async-start(), calls=%async_computation.3 | async-start | bytes 4456448 | tf_op jit(solution)/shard_map/reduce_scatter | solution.py:34
  128.2 45.9 %all-to-all-start.1 = ((f32[256,2,128]{2,0,1:T(8,128)}), f32[256,2,128]{2,0,1:T(8,128)S(1)}, u32[]{:S(2)}, u32[]{:S(2)}) async-start(f32[256,2,128]{2,0,1:T(8,128)} %copy_bitcast_fusion), calls=%async_computation.2 | async-start | bytes 524288 | tf_op jit(solution)/shard_map/all_to_all | solution.py:35
Sparse Core Ops, SparseCore 0:
  53.2 73.2 reduce-scatter.1
where the time goes:
time: 182 us
  waiting for transfers between devices  73.4 us (40%)
  blocking collectives  67.5 us (37%)
  between operations  14 us (8%)
  local copies, waits for them, and re-layouts  9.97 us (5%)
  starting transfers between devices  7.84 us (4%)
  other arithmetic  6.12 us (3%)
  matrix products  2.71 us (1%)
    reduce_scatter x1, waiting for transfers between devices, body(): summed = lax.psum_scatter(all_heads, 'dp', scatter_dimension=0, tiled=True)  73.4 us
    psum x1, blocking collectives, body(): total = lax.psum(jnp.sum(summed * summed), ('dp', 'tp'))  40.2 us
    all_gather x1, blocking collectives, body(): lax.all_gather(value_grad, 'tp', axis=1, tiled=True)  27.3 us
    reshape x2, local copies, waits for them, and re-layouts, body(): inputs = inputs.reshape(own_tokens, dp_count, tp_count, sub_rows)  4.97 us
    all_to_all x1, starting transfers between devices, body(): lax.all_to_all(inputs, 'tp', split_axis=2, concat_axis=0, tiled=True)  4.39 us
    convert_element_type x1, other arithmetic, block_dequantize(): return scaled.reshape(rows, values.shape[1]).astype(jnp.bfloat16)  3.79 us
  transfers between devices with their start and end apart: 3, of which 1 were waited for; matrix products, arithmetic and copies ran while one was open for 1% of the time, Pallas kernels for 0%

commit v1 on v0

--- a/solution.py
+++ b/solution.py
@@ -1,7 +1,246 @@
+import functools
+
 import jax
 import jax.numpy as jnp
 from jax import lax
+from jax.experimental import pallas as pl
+from jax.experimental.pallas import tpu as pltpu
 from jax.sharding import PartitionSpec as P
+
+
+AXES = ("dp", "tp")
+VMEM = pl.BlockSpec(memory_space=pltpu.VMEM)
+
+
+def params(limit=16 * 1024 * 1024):
+    return pltpu.CompilerParams(vmem_limit_bytes=limit)
+
+
+def cost(flops, moved):
+    return pl.CostEstimate(flops=flops, bytes_accessed=moved, transcendentals=0)
+
+
+def dequantize(values, scales, first, sub, block):
+    blocks = scales.shape[0]
+    row = lax.broadcasted_iota(jnp.int32, (blocks, sub), 0)
+    lane = lax.broadcasted_iota(jnp.int32, (blocks, sub), 1) // block
+    pick = (row == lane + first).astype(jnp.bfloat16)
+    spread = lax.dot_general(scales, pick, (((0,), (0,)), ((), ())), preferred_element_type=jnp.float32)
+    return (values.astype(jnp.float32) * spread).astype(jnp.bfloat16)
+
+
+def pack_kernel(n_tp, plane, planes, keys, core, sub, block, load, x_ref, s_ref, *refs):
+    index = lax.axis_index("dp") * n_tp + lax.axis_index("tp")
+    base = 0
+    if load:
+        *outs, x_vmem, s_vmem, sems = refs
+        (j,) = planes
+        width = plane * sub
+        base = lax.bitwise_xor(index, jnp.int32(j * plane)) // plane * plane
+        copies = [
+            pltpu.make_async_copy(
+                x_ref.at[:, pl.ds(pl.multiple_of(base * sub, width), width)], x_vmem, sems.at[0]
+            ),
+            pltpu.make_async_copy(s_ref, s_vmem, sems.at[1]),
+        ]
+        for copy in copies:
+            copy.start()
+        for copy in copies:
+            copy.wait()
+        x_ref, s_ref = x_vmem, s_vmem
+    else:
+        outs = refs
+    scales = s_ref[...]
+    for n, j in enumerate(planes):
+        for m, key in enumerate(keys):
+            out = outs[n * len(keys) + m]
+            for h in range(2):
+                part = lax.bitwise_xor(index, jnp.int32((j * plane + key) ^ (h * core)))
+                values = x_ref[:, pl.ds(pl.multiple_of((part - base) * sub, sub), sub)]
+                out[:, h * sub:(h + 1) * sub] = dequantize(values, scales, part * (sub // block), sub, block)
+
+
+def pack(x, scales, n_tp, plane, planes, keys, core, sub, load):
+    rows = x.shape[0]
+    block = x.shape[1] // scales.shape[0]
+    outs = len(planes) * len(keys)
+    scratch = [
+        pltpu.VMEM((rows, plane * sub), x.dtype),
+        pltpu.VMEM(scales.shape, scales.dtype),
+        pltpu.SemaphoreType.DMA((2,)),
+    ]
+    return pl.pallas_call(
+        functools.partial(pack_kernel, n_tp, plane, planes, keys, core, sub, block, load),
+        out_shape=[jax.ShapeDtypeStruct((rows, 2 * sub), jnp.bfloat16)] * outs,
+        in_specs=[pl.BlockSpec(memory_space=pltpu.HBM)] * 2 if load else [VMEM] * 2,
+        out_specs=[VMEM] * outs,
+        scratch_shapes=scratch if load else [],
+        compiler_params=params(67_043_328 - x.size * 5 // 4) if load else params(),
+        cost_estimate=cost(4 * rows * sub * outs, 8 * rows * sub * outs),
+        name="pack",
+    )(x, scales)
+
+
+def grads_kernel(n_tp, rows, *refs):
+    *ins, out = refs
+    tp = lax.axis_index("tp")
+    hd = ins[0].shape[1]
+    for g in range(len(ins) // n_tp):
+        for kt in range(n_tp):
+            start = pl.multiple_of(lax.bitwise_xor(tp, jnp.int32(kt)) * rows, rows)
+            for h in range(n_tp):
+                piece = ins[g * n_tp + h][pl.ds(start, rows), :]
+                column = (g * n_tp + kt) * rows
+                out[h * hd:(h + 1) * hd, column:column + rows] = piece.T
+
+
+def grads(pieces, n_tp, rows):
+    hd = pieces[0].shape[1]
+    size = len(pieces) * rows * hd * n_tp
+    return pl.pallas_call(
+        functools.partial(grads_kernel, n_tp, rows),
+        out_shape=jax.ShapeDtypeStruct((n_tp * hd, len(pieces) * rows), jnp.bfloat16),
+        in_specs=[VMEM] * len(pieces),
+        out_specs=VMEM,
+        compiler_params=params(),
+        cost_estimate=cost(size, 4 * size),
+        name="grads",
+    )(*pieces)
+
+
+def matmul_kernel(sub, gt_ref, *refs):
+    *ins, mine, theirs = refs
+    gt = gt_ref[...]
+    x = jnp.concatenate([r[...] for r in ins], axis=0)
+    theirs[...] = jnp.dot(gt, x[:, sub:], preferred_element_type=jnp.float32)
+    mine[...] = jnp.dot(gt, x[:, :sub], preferred_element_type=jnp.float32)
+
+
+def matmul(gt, xs, sub):
+    columns, tokens = gt.shape
+    return pl.pallas_call(
+        functools.partial(matmul_kernel, sub),
+        out_shape=[jax.ShapeDtypeStruct((columns, sub), jnp.float32)] * 2,
+        in_specs=[VMEM] * (1 + len(xs)),
+        out_specs=[VMEM] * 2,
+        compiler_params=params(),
+        cost_estimate=cost(4 * columns * tokens * sub, 4 * tokens * sub),
+        name="matmul",
+    )(gt, *xs)
+
+
+def join_kernel(a, b, out):
+    out[...] = (a[...] + b[...]).astype(out.dtype)
+
+
+def join(a, b):
+    return pl.pallas_call(
+        join_kernel,
+        out_shape=jax.ShapeDtypeStruct(a.shape, jnp.bfloat16),
+        in_specs=[VMEM] * 2,
+        out_specs=VMEM,
+        compiler_params=params(),
+        cost_estimate=cost(a.size, 10 * a.size),
+        name="join",
+    )(a, b)
+
+
+def total_kernel(*refs):
+    *ins, own, other, squares = refs
+    total = ins[0][...]
+    for r in ins[1:]:
+        total = total + r[...].astype(jnp.float32)
+    half = own.shape[0]
+    own[...] = total[:half]
+    other[...] = total[half:]
+    squared = (total * total).reshape(-1, 8, total.shape[1]).sum(0)
+    squares[...] = sum(squared[:, n:n + 128] for n in range(128, squared.shape[1], 128)) + squared[:, :128]
+
+
+def totals(parts):
+    columns, sub = parts[0].shape
+    half = jax.ShapeDtypeStruct((columns // 2, sub), jnp.float32)
+    return pl.pallas_call(
+        total_kernel,
+        out_shape=[half, half, jax.ShapeDtypeStruct((8, 128), jnp.float32)],
+        in_specs=[VMEM] * len(parts),
+        out_specs=[VMEM] * 3,
+        compiler_params=params(),
+        cost_estimate=cost(8 * columns * sub, 8 * columns * sub),
+        name="totals",
+    )(*parts)
+
+
+def clip_kernel(limit_squared, own, other, *refs):
+    *squares, out = refs
+    tp = lax.axis_index("tp")
+    sub = own.shape[1]
+    total = jnp.sum(sum(r[...] for r in squares))
+    norm = jnp.sqrt(jnp.full((8, 128), total, jnp.float32))
+    factor = jnp.minimum(jnp.float32(1.0), jnp.sqrt(jnp.float32(limit_squared)) / norm)[:1]
+    out[pl.ds(pl.multiple_of(tp * sub, sub), sub), :] = own[...].T * factor
+    out[pl.ds(pl.multiple_of((1 - tp) * sub, sub), sub), :] = other[...].T * factor
+
+
+def clip(own, other, squares, limit_squared):
+    hd, sub = own.shape
+    return pl.pallas_call(
+        functools.partial(clip_kernel, limit_squared),
+        out_shape=jax.ShapeDtypeStruct((2 * sub, hd), jnp.float32),
+        in_specs=[VMEM] * (2 + len(squares)),
+        out_specs=VMEM,
+        compiler_params=params(),
+        cost_estimate=cost(4 * hd * sub, 16 * hd * sub),
+        name="clip",
+    )(own, other, *squares)
+
+
+INNER = 4
+
+
+def keys_of(n_tp):
+    far = INNER // 2 * n_tp
+    return [0] + list(range(1, n_tp)) + [far + k for k in range(n_tp)]
+
+
+def fast_body(stash_values, stash_scales, value_grad):
+    n_dp, n_tp = lax.axis_size("dp"), lax.axis_size("tp")
+    count = n_dp * n_tp
+    plane = INNER * n_tp
+    depth = count // plane
+    rows, width = stash_values.shape
+    sub = width // count
+    keys = keys_of(n_tp)
+    core = n_tp
+    scales = stash_scales.T
+
+    def send(value, distance):
+        return lax.ppermute(value, AXES, [(i, i ^ distance) for i in range(count)])
+
+    order = list(range(depth - 1, -1, -1))
+    packed = pack(stash_values, scales, n_tp, plane, order[:1], keys, core, sub, True)
+    packed += pack(stash_values, scales, n_tp, plane, order[1:], keys, core, sub, False)
+    near = [value_grad] + [send(value_grad, k) for k in keys[1:]]
+    gt = grads(near, n_tp, rows)
+    parts = []
+    for n, j in enumerate(order):
+        own, *away = packed[n * len(keys):(n + 1) * len(keys)]
+        arrived = [own] + [send(v, k) for k, v in zip(keys[1:], away)]
+        mine, theirs = matmul(gt, arrived, sub)
+        theirs = send(theirs, core)
+        if j:
+            parts.append(send(join(mine, theirs), j * plane))
+        else:
+            parts += [mine, theirs]
+    own, other, squares = totals(parts[::-1])
+    other = send(other, 1)
+
+    pieces = [squares]
+    for group in [(core,), keys[1:], [j * plane for j in range(1, depth)]]:
+        merged = sum(pieces[1:], pieces[0])
+        pieces = [merged] + [send(merged, k) for k in group]
+    columns = value_grad.shape[1] * n_tp
+    return clip(own, other, pieces, width * columns)
 
 
 def block_dequantize(values, scales):
@@ -21,6 +260,8 @@
     tp_count = lax.axis_size("tp")
     own_tokens = stash_values.shape[0]
     sub_rows = width // (dp_count * tp_count)
+    if tp_count == 2 and dp_count == 16 and sub_rows % 256 == 0 and own_tokens % 128 == 0 and columns == 128:
+        return fast_body(stash_values, stash_scales, value_grad)
     inputs = block_dequantize(stash_values, stash_scales)
     inputs = inputs.reshape(own_tokens, dp_count, tp_count, sub_rows)
     features = lax.all_to_all(inputs, "tp", split_axis=2, concat_axis=0, tiled=True)

time: 182 us -> 69.2 us (0.38)
  blocking collectives: 67.5 us -> 0 us
  waiting for transfers between devices: 73.4 us -> 20.1 us
  starting transfers between devices: 7.84 us -> 36.4 us
  between operations: 14 us -> 0.18 us
  other arithmetic: 6.12 us -> 0.01 us
  Pallas kernels: 0 us -> 5.7 us
  local copies, waits for them, and re-layouts: 9.97 us -> 6.56 us
  matrix products: 2.71 us -> 0 us
    reduce_scatter x1 -> x0, waiting for transfers between devices: 73.4 us -> none  [body(): summed = lax.psum_scatter(all_heads, 'dp', scatter_dimension=0, tiled=True)]
    psum x1 -> x0, blocking collectives: 40.2 us -> none  [body(): total = lax.psum(jnp.sum(summed * summed), ('dp', 'tp'))]
    ppermute x0 -> x30, starting transfers between devices: none -> 36.4 us  [send(): return lax.ppermute(value, AXES, [(i, i ^ distance) for i in range(count)])]
    all_gather x1 -> x0, blocking collectives: 27.3 us -> none  [body(): lax.all_gather(value_grad, 'tp', axis=1, tiled=True)]
    ppermute x0 -> x30, waiting for transfers between devices: none -> 20.1 us  [send(): return lax.ppermute(value, AXES, [(i, i ^ distance) for i in range(count)])]
    all_to_all x2 -> x0, starting transfers between devices: 7.84 us -> none  [the longest x1 4.39 us: body(): lax.all_to_all(inputs, 'tp', split_axis=2, concat_axis=0, tiled=True)]
    pallas_call x0 -> x12, Pallas kernels: none -> 5.7 us  [the longest x2 3.36 us: pack(): pl.pallas_call(functools.partial(pack_kernel, n_tp, plane, planes, keys,...]
    unnamed x5 -> x24, local copies, waits for them, and re-layouts: 1.38 us -> 6.56 us
  transfers between devices with their start and end apart: 3 -> 30, of which waited for: 1 -> 10; matrix products, arithmetic and copies ran while one was open for 1% -> 0% of each run, Pallas kernels for 0% -> 7%
where the time goes in v1:
time: 69.2 us; the launch traced here: 68.9 us
  starting transfers between devices  36.4 us (53%)
  waiting for transfers between devices  20.1 us (29%)
  local copies, waits for them, and re-layouts  6.56 us (9%)
  Pallas kernels  5.7 us (8%)
    ppermute x30, starting transfers between devices, send(): return lax.ppermute(value, AXES, [(i, i ^ distance) for i in range(count)])  36.4 us
    ppermute x30, waiting for transfers between devices, send(): return lax.ppermute(value, AXES, [(i, i ^ distance) for i in range(count)])  20.1 us
    unnamed x24, local copies, waits for them, and re-layouts  6.56 us
    pallas_call x2, Pallas kernels, pack(): pl.pallas_call(functools.partial(pack_kernel, n_tp, plane, planes, keys,...  3.36 us
  transfers between devices with their start and end apart: 30, of which 10 were waited for; matrix products, arithmetic and copies ran while one was open for 0% of the time, Pallas kernels for 7%

profile of v1, /device:TPU:0, one launch (start us, length us, event | category | flops | bytes accessed | tf_op | source)
XLA Modules:
  0.0 68.9 jit_solution(3314214018990995662)
XLA Ops:
  0.0 3.0 %collective-permute-start = (bf16[256,128]{1,0:T(8,128)(2,1)}, bf16[256,128]{1,0:T(8,128)(2,1)S(1)}, u32[]{:S(2)}, u32[]{:S(2)}) collective-permute-start(bf16[256,128]{1,0:T(8,128)(2,1)} %refs_0_.1), channel_id=1, source_target_pairs={{0,1},{1,0},{2,3},{3,2},{4,5},{5,4},{6,7},{7,6},{8,9},{9,8},{10,11... | collective-permute-start | bytes 196616 | tf_op jit(solution)/shard_map/ppermute | solution.py:218
  3.0 1.5 %collective-permute-start.1 = (bf16[256,128]{1,0:T(8,128)(2,1)}, bf16[256,128]{1,0:T(8,128)(2,1)S(1)}, u32[]{:S(2)}, u32[]{:S(2)}) collective-permute-start(bf16[256,128]{1,0:T(8,128)(2,1)} %refs_0_.1), channel_id=1, source_target_pairs={{0,4},{1,5},{2,6},{3,7},{4,0},{5,1},{6,2},{7,3},{8,12},{9,13},{10,... | collective-permute-start | bytes 196616 | tf_op jit(solution)/shard_map/ppermute | solution.py:218
  4.5 1.6 %copy-done = bf16[128,8192]{1,0:T(8,128)(2,1)S(1)} copy-done((bf16[128,8192]{1,0:T(8,128)(2,1)S(1)}, bf16[128,8192]{1,0:T(8,128)(2,1)}, u32[]{:S(2)}) %copy-start) | copy-done | bytes 2097176
  6.8 1.3 %pack.2 = (bf16[128,512]{1,0:T(8,128)(2,1)S(1)}, bf16[128,512]{1,0:T(8,128)(2,1)S(1)}, bf16[128,512]{1,0:T(8,128)(2,1)}, bf16[128,512]{1,0:T(8,128)(2,1)}, bf16[...) custom-call(bf16[128,8192]{1,0:T(8,128)(2,1)S(1)} %copy-done, ...), custom_call_target="tpu_custom_call" | custom-call | flops 1572864 | bytes 3145728 | tf_op jit(solution)/shard_map/pack/pallas_call | solution.py:72
  9.4 2.0 %collective-permute-start.12 = (bf16[128,512]{1,0:T(8,128)(2,1)S(1)}, bf16[128,512]{1,0:T(8,128)(2,1)S(1)}, u32[]{:S(2)}, u32[]{:S(2)}) collective-permute-start(bf16[128,512]{1,0:T(8,128)(2,1)S(1)} %get-tuple-element.45), channel_id=1, source_target_pairs={{0,1},{1,0},{2,3},{3,2},{4,5},{5,4},{6,7},{7,6},{8,9},{9,8},{10,11... | collective-permute-start | bytes 393224 | tf_op jit(solution)/shard_map/ppermute | solution.py:218
  11.4 1.5 %collective-permute-start.13 = (bf16[128,512]{1,0:T(8,128)(2,1)}, bf16[128,512]{1,0:T(8,128)(2,1)S(1)}, u32[]{:S(2)}, u32[]{:S(2)}) collective-permute-start(bf16[128,512]{1,0:T(8,128)(2,1)} %get-tuple-element.46), channel_id=1, source_target_pairs={{0,4},{1,5},{2,6},{3,7},{4,0},{5,1},{6,2},{7,3},{8,12},{9,13},{10,... | collective-permute-start | bytes 393224 | tf_op jit(solution)/shard_map/ppermute | solution.py:218
  14.2 1.4 %collective-permute-start.7 = (bf16[128,512]{1,0:T(8,128)(2,1)}, bf16[128,512]{1,0:T(8,128)(2,1)S(1)}, u32[]{:S(2)}, u32[]{:S(2)}) collective-permute-start(bf16[128,512]{1,0:T(8,128)(2,1)} %get-tuple-element.39), channel_id=1, source_target_pairs={{0,1},{1,0},{2,3},{3,2},{4,5},{5,4},{6,7},{7,6},{8,9},{9,8},{10,11... | collective-permute-start | bytes 393224 | tf_op jit(solution)/shard_map/ppermute | solution.py:218
  16.2 1.5 %collective-permute-start.8 = (bf16[128,512]{1,0:T(8,128)(2,1)}, bf16[128,512]{1,0:T(8,128)(2,1)S(1)}, u32[]{:S(2)}, u32[]{:S(2)}) collective-permute-start(bf16[128,512]{1,0:T(8,128)(2,1)} %get-tuple-element.40), channel_id=1, source_target_pairs={{0,4},{1,5},{2,6},{3,7},{4,0},{5,1},{6,2},{7,3},{8,12},{9,13},{10,... | collective-permute-start | bytes 393224 | tf_op jit(solution)/shard_map/ppermute | solution.py:218
  17.7 1.5 %collective-permute-start.9 = (bf16[128,512]{1,0:T(8,128)(2,1)}, bf16[128,512]{1,0:T(8,128)(2,1)S(1)}, u32[]{:S(2)}, u32[]{:S(2)}) collective-permute-start(bf16[128,512]{1,0:T(8,128)(2,1)} %get-tuple-element.41), channel_id=1, source_target_pairs={{0,5},{1,4},{2,7},{3,6},{4,1},{5,0},{6,3},{7,2},{8,13},{9,12},{10,... | collective-permute-start | bytes 393224 | tf_op jit(solution)/shard_map/ppermute | solution.py:218
  19.2 2.1 %pack.3 = (bf16[128,512]{1,0:T(8,128)(2,1)}, bf16[128,512]{1,0:T(8,128)(2,1)}, bf16[128,512]{1,0:T(8,128)(2,1)}, bf16[128,512]{1,0:T(8,128)(2,1)}) custom-call(bf16[128,8192]{1,0:T(8,128)(2,1)} %x_ref.3, bf16[64,128]{1,0:T(8,128)(2,1)} %bitcast.1), custom_call_target="tpu_custom_call" | custom-call | flops 524288 | bytes 1048576 | tf_op jit(solution)/shard_map/pack/pallas_call | solution.py:72
  21.8 1.5 %collective-permute-start.18 = (bf16[128,512]{1,0:T(8,128)(2,1)}, bf16[128,512]{1,0:T(8,128)(2,1)S(1)}, u32[]{:S(2)}, u32[]{:S(2)}) collective-permute-start(bf16[128,512]{1,0:T(8,128)(2,1)} %get-tuple-element.52), channel_id=1, source_target_pairs={{0,4},{1,5},{2,6},{3,7},{4,0},{5,1},{6,2},{7,3},{8,12},{9,13},{10,... | collective-permute-start | bytes 393224 | tf_op jit(solution)/shard_map/ppermute | solution.py:218
  23.3 1.5 %collective-permute-start.19 = (bf16[128,512]{1,0:T(8,128)(2,1)}, bf16[128,512]{1,0:T(8,128)(2,1)S(1)}, u32[]{:S(2)}, u32[]{:S(2)}) collective-permute-start(bf16[128,512]{1,0:T(8,128)(2,1)} %get-tuple-element.53), channel_id=1, source_target_pairs={{0,5},{1,4},{2,7},{3,6},{4,1},{5,0},{6,3},{7,2},{8,13},{9,12},{10,... | collective-permute-start | bytes 393224 | tf_op jit(solution)/shard_map/ppermute | solution.py:218
  27.4 1.6 %collective-permute-start.4 = (bf16[128,512]{1,0:T(8,128)(2,1)}, bf16[128,512]{1,0:T(8,128)(2,1)S(1)}, u32[]{:S(2)}, u32[]{:S(2)}) collective-permute-start(bf16[128,512]{1,0:T(8,128)(2,1)} %copy-done.10), channel_id=1, source_target_pairs={{0,4},{1,5},{2,6},{3,7},{4,0},{5,1},{6,2},{7,3},{8,12},{9,13},{10,... | collective-permute-start | bytes 393224 | tf_op jit(solution)/shard_map/ppermute | solution.py:218
  29.3 2.3 %collective-permute-start.5 = (bf16[128,512]{1,0:T(8,128)(2,1)S(1)}, bf16[128,512]{1,0:T(8,128)(2,1)S(1)}, u32[]{:S(2)}, u32[]{:S(2)}) collective-permute-start(bf16[128,512]{1,0:T(8,128)(2,1)S(1)} %copy-done.9), channel_id=1, source_target_pairs={{0,5},{1,4},{2,7},{3,6},{4,1},{5,0},{6,3},{7,2},{8,13},{9,12},{10,... | collective-permute-start | bytes 393224 | tf_op jit(solution)/shard_map/ppermute | solution.py:218
  33.2 1.1 %collective-permute-done.4.refs_2_ = bf16[128,512]{1,0:T(8,128)(2,1)S(1)} collective-permute-done((bf16[128,512]{1,0:T(8,128)(2,1)}, bf16[128,512]{1,0:T(8,128)(2,1)S(1)}, u32[]{:S(2)}, u32[]{:S(2)}) %collective-permute-start.4) | collective-permute-done | bytes 131104 | tf_op jit(solution)/shard_map/ppermute | solution.py:218
  34.3 1.8 %collective-permute-done.5.refs_3_ = bf16[128,512]{1,0:T(8,128)(2,1)S(1)} collective-permute-done((bf16[128,512]{1,0:T(8,128)(2,1)S(1)}, bf16[128,512]{1,0:T(8,128)(2,1)S(1)}, u32[]{:S(2)}, u32[]{:S(2)}) %collective-permute-start.5) | collective-permute-done | bytes 131104 | tf_op jit(solution)/shard_map/ppermute | solution.py:218
  36.5 2.7 %collective-permute-start.16 = (bf16[256,256]{1,0:T(8,128)(2,1)S(1)}, bf16[256,256]{1,0:T(8,128)(2,1)S(1)}, u32[]{:S(2)}, u32[]{:S(2)}) collective-permute-start(bf16[256,256]{1,0:T(8,128)(2,1)S(1)} %join.4), channel_id=1, source_target_pairs={{0,16},{1,17},{2,18},{3,19},{4,20},{5,21},{6,22},{7,23},{8,24},{9,... | collective-permute-start | bytes 393224 | tf_op jit(solution)/shard_map/ppermute | solution.py:218
  39.2 1.6 %collective-permute-start.11 = (bf16[256,256]{1,0:T(8,128)(2,1)S(1)}, bf16[256,256]{1,0:T(8,128)(2,1)S(1)}, u32[]{:S(2)}, u32[]{:S(2)}) collective-permute-start(bf16[256,256]{1,0:T(8,128)(2,1)S(1)} %join.3), channel_id=1, source_target_pairs={{0,8},{1,9},{2,10},{3,11},{4,12},{5,13},{6,14},{7,15},{8,0},{9,1},... | collective-permute-start | bytes 393224 | tf_op jit(solution)/shard_map/ppermute | solution.py:218
  41.2 5.5 %collective-permute-done.16.refs_3_ = bf16[256,256]{1,0:T(8,128)(2,1)S(1)} collective-permute-done((bf16[256,256]{1,0:T(8,128)(2,1)S(1)}, bf16[256,256]{1,0:T(8,128)(2,1)S(1)}, u32[]{:S(2)}, u32[]{:S(2)}) %collective-permute-start.16) | collective-permute-done | bytes 131104 | tf_op jit(solution)/shard_map/ppermute | solution.py:218
  46.7 3.5 %collective-permute-done.21.refs_4_ = bf16[256,256]{1,0:T(8,128)(2,1)S(1)} collective-permute-done((bf16[256,256]{1,0:T(8,128)(2,1)S(1)}, bf16[256,256]{1,0:T(8,128)(2,1)S(1)}, u32[]{:S(2)}, u32[]{:S(2)}) %collective-permute-start.21) | collective-permute-done | bytes 131104 | tf_op jit(solution)/shard_map/ppermute | solution.py:218
  50.3 1.2 %collective-permute-done.23 = f32[8,128]{1,0:T(8,128)S(1)} collective-permute-done((f32[8,128]{1,0:T(8,128)S(1)}, f32[8,128]{1,0:T(8,128)S(1)}, u32[]{:S(2)}, u32[]{:S(2)}) %collective-permute-start.23) | collective-permute-done | bytes 4128 | tf_op jit(solution)/shard_map/ppermute | solution.py:218
  51.5 1.1 %collective-permute-start.24 = (f32[8,128]{1,0:T(8,128)S(1)}, f32[8,128]{1,0:T(8,128)S(1)}, u32[]{:S(2)}, u32[]{:S(2)}) collective-permute-start(f32[8,128]{1,0:T(8,128)S(1)} %add.12), channel_id=1, source_target_pairs={{0,1},{1,0},{2,3},{3,2},{4,5},{5,4},{6,7},{7,6},{8,9},{9,8},{10,11... | collective-permute-start | bytes 12296 | tf_op jit(solution)/shard_map/ppermute | solution.py:218
  52.6 1.2 %collective-permute-start.25 = (f32[8,128]{1,0:T(8,128)S(1)}, f32[8,128]{1,0:T(8,128)S(1)}, u32[]{:S(2)}, u32[]{:S(2)}) collective-permute-start(f32[8,128]{1,0:T(8,128)S(1)} %add.12), channel_id=1, source_target_pairs={{0,4},{1,5},{2,6},{3,7},{4,0},{5,1},{6,2},{7,3},{8,12},{9,13},{10,... | collective-permute-start | bytes 12296 | tf_op jit(solution)/shard_map/ppermute | solution.py:218
  53.7 1.2 %collective-permute-start.26 = (f32[8,128]{1,0:T(8,128)S(1)}, f32[8,128]{1,0:T(8,128)S(1)}, u32[]{:S(2)}, u32[]{:S(2)}) collective-permute-start(f32[8,128]{1,0:T(8,128)S(1)} %add.12), channel_id=1, source_target_pairs={{0,5},{1,4},{2,7},{3,6},{4,1},{5,0},{6,3},{7,2},{8,13},{9,12},{10,... | collective-permute-start | bytes 12296 | tf_op jit(solution)/shard_map/ppermute | solution.py:218
  55.0 1.1 %collective-permute-start.22 = (f32[128,256]{1,0:T(8,128)S(1)}, f32[128,256]{1,0:T(8,128)S(1)}, u32[]{:S(2)}, u32[]{:S(2)}) collective-permute-start(f32[128,256]{1,0:T(8,128)S(1)} %get-tuple-element.57), channel_id=1, source_target_pairs={{0,1},{1,0},{2,3},{3,2},{4,5},{5,4},{6,7},{7,6},{8,9},{9,8},{10,11... | collective-permute-start | bytes 393224 | tf_op jit(solution)/shard_map/ppermute | solution.py:218
  56.2 2.2 %collective-permute-done.26 = f32[8,128]{1,0:T(8,128)S(1)} collective-permute-done((f32[8,128]{1,0:T(8,128)S(1)}, f32[8,128]{1,0:T(8,128)S(1)}, u32[]{:S(2)}, u32[]{:S(2)}) %collective-permute-start.26) | collective-permute-done | bytes 4128 | tf_op jit(solution)/shard_map/ppermute | solution.py:218
  58.4 2.3 %collective-permute-start.27 = (f32[8,128]{1,0:T(8,128)S(1)}, f32[8,128]{1,0:T(8,128)S(1)}, u32[]{:S(2)}, u32[]{:S(2)}) collective-permute-start(f32[8,128]{1,0:T(8,128)S(1)} %add_add_fusion.refs_0_), channel_id=1, source_target_pairs={{0,8},{1,9},{2,10},{3,11},{4,12},{5,13},{6,14},{7,15},{8,0},{9,1},... | collective-permute-start | bytes 12296 | tf_op jit(solution)/shard_map/ppermute | solution.py:218
  60.7 2.0 %collective-permute-start.28 = (f32[8,128]{1,0:T(8,128)S(1)}, f32[8,128]{1,0:T(8,128)S(1)}, u32[]{:S(2)}, u32[]{:S(2)}) collective-permute-start(f32[8,128]{1,0:T(8,128)S(1)} %add_add_fusion.refs_0_), channel_id=1, source_target_pairs={{0,16},{1,17},{2,18},{3,19},{4,20},{5,21},{6,22},{7,23},{8,24},{9,... | collective-permute-start | bytes 12296 | tf_op jit(solution)/shard_map/ppermute | solution.py:218
  62.7 1.4 %collective-permute-start.29 = (f32[8,128]{1,0:T(8,128)S(1)}, f32[8,128]{1,0:T(8,128)S(1)}, u32[]{:S(2)}, u32[]{:S(2)}) collective-permute-start(f32[8,128]{1,0:T(8,128)S(1)} %add_add_fusion.refs_0_), channel_id=1, source_target_pairs={{0,24},{1,25},{2,26},{3,27},{4,28},{5,29},{6,30},{7,31},{8,16},{9,... | collective-permute-start | bytes 12296 | tf_op jit(solution)/shard_map/ppermute | solution.py:218
  64.1 1.2 %collective-permute-done.28.refs_2_ = f32[8,128]{1,0:T(8,128)S(1)} collective-permute-done((f32[8,128]{1,0:T(8,128)S(1)}, f32[8,128]{1,0:T(8,128)S(1)}, u32[]{:S(2)}, u32[]{:S(2)}) %collective-permute-start.28) | collective-permute-done | bytes 4128 | tf_op jit(solution)/shard_map/ppermute | solution.py:218
  65.2 2.8 %collective-permute-done.29.refs_3_ = f32[8,128]{1,0:T(8,128)S(1)} collective-permute-done((f32[8,128]{1,0:T(8,128)S(1)}, f32[8,128]{1,0:T(8,128)S(1)}, u32[]{:S(2)}, u32[]{:S(2)}) %collective-permute-start.29) | collective-permute-done | bytes 4128 | tf_op jit(solution)/shard_map/ppermute | solution.py:218
  68.1 0.9 %clip.1 = f32[512,128]{1,0:T(8,128)} custom-call(f32[128,256]{1,0:T(8,128)S(1)} %get-tuple-element.56.own, f32[128,256]{1,0:T(8,128)S(1)} %collective-permute-done.22.other, f32[8,128]{1,0:T(8,128)S(1)} %add_add_fusion.refs_0_, f32[8,128]{1,0:T(8,128)S(1)} %collective-permute-done.27.refs_1_, f32[8,128]{1,0:T(8,128)S(1)} %collective-permute-done.28.refs_2_, ...), custom_call_target="tpu_custom_call" | custom-call | flops 131072 | bytes 524288 | tf_op jit(solution)/shard_map/clip/pallas_call | solution.py:187
  (66 shorter events, 9.9 us)
Async XLA Ops:
  0.0 12.9 %collective-permute-start = (bf16[256,128]{1,0:T(8,128)(2,1)}, bf16[256,128]{1,0:T(8,128)(2,1)S(1)}, u32[]{:S(2)}, u32[]{:S(2)}) collective-permute-start(bf16[256,128]{1,0:T(8,128)(2,1)} %refs_0_.1), channel_id=1, source_target_pairs={{0,1},{1,0},{2,3},{3,2},{4,5},{5,4},{6,7},{7,6},{8,9},{9,8},{10,11... | collective-permute-start | bytes 196616 | tf_op jit(solution)/shard_map/ppermute | solution.py:218
  3.0 10.5 %collective-permute-start.1 = (bf16[256,128]{1,0:T(8,128)(2,1)}, bf16[256,128]{1,0:T(8,128)(2,1)S(1)}, u32[]{:S(2)}, u32[]{:S(2)}) collective-permute-start(bf16[256,128]{1,0:T(8,128)(2,1)} %refs_0_.1), channel_id=1, source_target_pairs={{0,4},{1,5},{2,6},{3,7},{4,0},{5,1},{6,2},{7,3},{8,12},{9,13},{10,... | collective-permute-start | bytes 196616 | tf_op jit(solution)/shard_map/ppermute | solution.py:218
  4.5 11.0 %collective-permute-start.2 = (bf16[256,128]{1,0:T(8,128)(2,1)}, bf16[256,128]{1,0:T(8,128)(2,1)S(1)}, u32[]{:S(2)}, u32[]{:S(2)}) collective-permute-start(bf16[256,128]{1,0:T(8,128)(2,1)} %refs_0_.1), channel_id=1, source_target_pairs={{0,5},{1,4},{2,7},{3,6},{4,1},{5,0},{6,3},{7,2},{8,13},{9,12},{10,... | collective-permute-start | bytes 196616 | tf_op jit(solution)/shard_map/ppermute | solution.py:218
  6.8 18.5 %copy-start.3 = (bf16[256,128]{1,0:T(8,128)(2,1)S(1)}, bf16[256,128]{1,0:T(8,128)(2,1)}, u32[]{:S(2)}) copy-start(bf16[256,128]{1,0:T(8,128)(2,1)} %refs_0_.1) | copy-start | bytes 196612
  9.4 8.2 %collective-permute-start.12 = (bf16[128,512]{1,0:T(8,128)(2,1)S(1)}, bf16[128,512]{1,0:T(8,128)(2,1)S(1)}, u32[]{:S(2)}, u32[]{:S(2)}) collective-permute-start(bf16[128,512]{1,0:T(8,128)(2,1)S(1)} %get-tuple-element.45), channel_id=1, source_target_pairs={{0,1},{1,0},{2,3},{3,2},{4,5},{5,4},{6,7},{7,6},{8,9},{9,8},{10,11... | collective-permute-start | bytes 393224 | tf_op jit(solution)/shard_map/ppermute | solution.py:218
  11.4 9.9 %collective-permute-start.13 = (bf16[128,512]{1,0:T(8,128)(2,1)}, bf16[128,512]{1,0:T(8,128)(2,1)S(1)}, u32[]{:S(2)}, u32[]{:S(2)}) collective-permute-start(bf16[128,512]{1,0:T(8,128)(2,1)} %get-tuple-element.46), channel_id=1, source_target_pairs={{0,4},{1,5},{2,6},{3,7},{4,0},{5,1},{6,2},{7,3},{8,12},{9,13},{10,... | collective-permute-start | bytes 393224 | tf_op jit(solution)/shard_map/ppermute | solution.py:218
  12.9 8.9 %collective-permute-start.14 = (bf16[128,512]{1,0:T(8,128)(2,1)}, bf16[128,512]{1,0:T(8,128)(2,1)S(1)}, u32[]{:S(2)}, u32[]{:S(2)}) collective-permute-start(bf16[128,512]{1,0:T(8,128)(2,1)} %get-tuple-element.47), channel_id=1, source_target_pairs={{0,5},{1,4},{2,7},{3,6},{4,1},{5,0},{6,3},{7,2},{8,13},{9,12},{10,... | collective-permute-start | bytes 393224 | tf_op jit(solution)/shard_map/ppermute | solution.py:218
  14.2 9.2 %collective-permute-start.7 = (bf16[128,512]{1,0:T(8,128)(2,1)}, bf16[128,512]{1,0:T(8,128)(2,1)S(1)}, u32[]{:S(2)}, u32[]{:S(2)}) collective-permute-start(bf16[128,512]{1,0:T(8,128)(2,1)} %get-tuple-element.39), channel_id=1, source_target_pairs={{0,1},{1,0},{2,3},{3,2},{4,5},{5,4},{6,7},{7,6},{8,9},{9,8},{10,11... | collective-permute-start | bytes 393224 | tf_op jit(solution)/shard_map/ppermute | solution.py:218
  16.2 8.7 %collective-permute-start.8 = (bf16[128,512]{1,0:T(8,128)(2,1)}, bf16[128,512]{1,0:T(8,128)(2,1)S(1)}, u32[]{:S(2)}, u32[]{:S(2)}) collective-permute-start(bf16[128,512]{1,0:T(8,128)(2,1)} %get-tuple-element.40), channel_id=1, source_target_pairs={{0,4},{1,5},{2,6},{3,7},{4,0},{5,1},{6,2},{7,3},{8,12},{9,13},{10,... | collective-permute-start | bytes 393224 | tf_op jit(solution)/shard_map/ppermute | solution.py:218
  17.7 9.8 %collective-permute-start.9 = (bf16[128,512]{1,0:T(8,128)(2,1)}, bf16[128,512]{1,0:T(8,128)(2,1)S(1)}, u32[]{:S(2)}, u32[]{:S(2)}) collective-permute-start(bf16[128,512]{1,0:T(8,128)(2,1)} %get-tuple-element.41), channel_id=1, source_target_pairs={{0,5},{1,4},{2,7},{3,6},{4,1},{5,0},{6,3},{7,2},{8,13},{9,12},{10,... | collective-permute-start | bytes 393224 | tf_op jit(solution)/shard_map/ppermute | solution.py:218
  21.3 11.0 %copy-start.1 = (bf16[128,512]{1,0:T(8,128)(2,1)S(1)}, bf16[128,512]{1,0:T(8,128)(2,1)}, u32[]{:S(2)}) copy-start(bf16[128,512]{1,0:T(8,128)(2,1)} %get-tuple-element.50.refs_0_) | copy-start | bytes 393220
  21.3 8.0 %collective-permute-start.17 = (bf16[128,512]{1,0:T(8,128)(2,1)}, bf16[128,512]{1,0:T(8,128)(2,1)S(1)}, u32[]{:S(2)}, u32[]{:S(2)}) collective-permute-start(bf16[128,512]{1,0:T(8,128)(2,1)} %get-tuple-element.51), channel_id=1, source_target_pairs={{0,1},{1,0},{2,3},{3,2},{4,5},{5,4},{6,7},{7,6},{8,9},{9,8},{10,11... | collective-permute-start | bytes 393224 | tf_op jit(solution)/shard_map/ppermute | solution.py:218
  21.8 9.8 %collective-permute-start.18 = (bf16[128,512]{1,0:T(8,128)(2,1)}, bf16[128,512]{1,0:T(8,128)(2,1)S(1)}, u32[]{:S(2)}, u32[]{:S(2)}) collective-permute-start(bf16[128,512]{1,0:T(8,128)(2,1)} %get-tuple-element.52), channel_id=1, source_target_pairs={{0,4},{1,5},{2,6},{3,7},{4,0},{5,1},{6,2},{7,3},{8,12},{9,13},{10,... | collective-permute-start | bytes 393224 | tf_op jit(solution)/shard_map/ppermute | solution.py:218
  23.3 9.0 %collective-permute-start.19 = (bf16[128,512]{1,0:T(8,128)(2,1)}, bf16[128,512]{1,0:T(8,128)(2,1)S(1)}, u32[]{:S(2)}, u32[]{:S(2)}) collective-permute-start(bf16[128,512]{1,0:T(8,128)(2,1)} %get-tuple-element.53), channel_id=1, source_target_pairs={{0,5},{1,4},{2,7},{3,6},{4,1},{5,0},{6,3},{7,2},{8,13},{9,12},{10,... | collective-permute-start | bytes 393224 | tf_op jit(solution)/shard_map/ppermute | solution.py:218
  24.9 7.7 %collective-permute-start.3 = (bf16[128,512]{1,0:T(8,128)(2,1)}, bf16[128,512]{1,0:T(8,128)(2,1)S(1)}, u32[]{:S(2)}, u32[]{:S(2)}) collective-permute-start(bf16[128,512]{1,0:T(8,128)(2,1)} %copy-done.11), channel_id=1, source_target_pairs={{0,1},{1,0},{2,3},{3,2},{4,5},{5,4},{6,7},{7,6},{8,9},{9,8},{10,11... | collective-permute-start | bytes 393224 | tf_op jit(solution)/shard_map/ppermute | solution.py:218
  27.4 6.9 %collective-permute-start.4 = (bf16[128,512]{1,0:T(8,128)(2,1)}, bf16[128,512]{1,0:T(8,128)(2,1)S(1)}, u32[]{:S(2)}, u32[]{:S(2)}) collective-permute-start(bf16[128,512]{1,0:T(8,128)(2,1)} %copy-done.10), channel_id=1, source_target_pairs={{0,4},{1,5},{2,6},{3,7},{4,0},{5,1},{6,2},{7,3},{8,12},{9,13},{10,... | collective-permute-start | bytes 393224 | tf_op jit(solution)/shard_map/ppermute | solution.py:218
  29.3 6.8 %collective-permute-start.5 = (bf16[128,512]{1,0:T(8,128)(2,1)S(1)}, bf16[128,512]{1,0:T(8,128)(2,1)S(1)}, u32[]{:S(2)}, u32[]{:S(2)}) collective-permute-start(bf16[128,512]{1,0:T(8,128)(2,1)S(1)} %copy-done.9), channel_id=1, source_target_pairs={{0,5},{1,4},{2,7},{3,6},{4,1},{5,0},{6,3},{7,2},{8,13},{9,12},{10,... | collective-permute-start | bytes 393224 | tf_op jit(solution)/shard_map/ppermute | solution.py:218
  31.6 4.9 %collective-permute-start.15 = (f32[256,256]{1,0:T(8,128)S(1)}, f32[256,256]{1,0:T(8,128)S(1)}, u32[]{:S(2)}, u32[]{:S(2)}) collective-permute-start(f32[256,256]{1,0:T(8,128)S(1)} %get-tuple-element.49), channel_id=1, source_target_pairs={{0,2},{1,3},{2,0},{3,1},{4,6},{5,7},{6,4},{7,5},{8,10},{9,11},{10,... | collective-permute-start | bytes 786440 | tf_op jit(solution)/shard_map/ppermute | solution.py:218
  32.3 6.9 %collective-permute-start.10 = (f32[256,256]{1,0:T(8,128)S(1)}, f32[256,256]{1,0:T(8,128)S(1)}, u32[]{:S(2)}, u32[]{:S(2)}) collective-permute-start(f32[256,256]{1,0:T(8,128)S(1)} %get-tuple-element.43), channel_id=1, source_target_pairs={{0,2},{1,3},{2,0},{3,1},{4,6},{5,7},{6,4},{7,5},{8,10},{9,11},{10,... | collective-permute-start | bytes 786440 | tf_op jit(solution)/shard_map/ppermute | solution.py:218
  32.6 8.3 %collective-permute-start.20 = (f32[256,256]{1,0:T(8,128)S(1)}, f32[256,256]{1,0:T(8,128)S(1)}, u32[]{:S(2)}, u32[]{:S(2)}) collective-permute-start(f32[256,256]{1,0:T(8,128)S(1)} %get-tuple-element.55), channel_id=1, source_target_pairs={{0,2},{1,3},{2,0},{3,1},{4,6},{5,7},{6,4},{7,5},{8,10},{9,11},{10,... | collective-permute-start | bytes 786440 | tf_op jit(solution)/shard_map/ppermute | solution.py:218
  36.4 4.8 %collective-permute-start.6 = (f32[256,256]{1,0:T(8,128)S(1)}, f32[256,256]{1,0:T(8,128)S(1)}, u32[]{:S(2)}, u32[]{:S(2)}) collective-permute-start(f32[256,256]{1,0:T(8,128)S(1)} %get-tuple-element.36), channel_id=1, source_target_pairs={{0,2},{1,3},{2,0},{3,1},{4,6},{5,7},{6,4},{7,5},{8,10},{9,11},{10,... | collective-permute-start | bytes 786440 | tf_op jit(solution)/shard_map/ppermute | solution.py:218
  36.5 10.1 %collective-permute-start.16 = (bf16[256,256]{1,0:T(8,128)(2,1)S(1)}, bf16[256,256]{1,0:T(8,128)(2,1)S(1)}, u32[]{:S(2)}, u32[]{:S(2)}) collective-permute-start(bf16[256,256]{1,0:T(8,128)(2,1)S(1)} %join.4), channel_id=1, source_target_pairs={{0,16},{1,17},{2,18},{3,19},{4,20},{5,21},{6,22},{7,23},{8,24},{9,... | collective-permute-start | bytes 393224 | tf_op jit(solution)/shard_map/ppermute | solution.py:218
  39.2 7.5 %collective-permute-start.11 = (bf16[256,256]{1,0:T(8,128)(2,1)S(1)}, bf16[256,256]{1,0:T(8,128)(2,1)S(1)}, u32[]{:S(2)}, u32[]{:S(2)}) collective-permute-start(bf16[256,256]{1,0:T(8,128)(2,1)S(1)} %join.3), channel_id=1, source_target_pairs={{0,8},{1,9},{2,10},{3,11},{4,12},{5,13},{6,14},{7,15},{8,0},{9,1},... | collective-permute-start | bytes 393224 | tf_op jit(solution)/shard_map/ppermute | solution.py:218
  40.9 9.3 %collective-permute-start.21 = (bf16[256,256]{1,0:T(8,128)(2,1)S(1)}, bf16[256,256]{1,0:T(8,128)(2,1)S(1)}, u32[]{:S(2)}, u32[]{:S(2)}) collective-permute-start(bf16[256,256]{1,0:T(8,128)(2,1)S(1)} %join.5), channel_id=1, source_target_pairs={{0,24},{1,25},{2,26},{3,27},{4,28},{5,29},{6,30},{7,31},{8,16},{9,... | collective-permute-start | bytes 393224 | tf_op jit(solution)/shard_map/ppermute | solution.py:218
  50.3 1.2 %collective-permute-start.23 = (f32[8,128]{1,0:T(8,128)S(1)}, f32[8,128]{1,0:T(8,128)S(1)}, u32[]{:S(2)}, u32[]{:S(2)}) collective-permute-start(f32[8,128]{1,0:T(8,128)S(1)} %get-tuple-element.58), channel_id=1, source_target_pairs={{0,2},{1,3},{2,0},{3,1},{4,6},{5,7},{6,4},{7,5},{8,10},{9,11},{10,... | collective-permute-start | bytes 12296 | tf_op jit(solution)/shard_map/ppermute | solution.py:218
  51.5 4.6 %collective-permute-start.24 = (f32[8,128]{1,0:T(8,128)S(1)}, f32[8,128]{1,0:T(8,128)S(1)}, u32[]{:S(2)}, u32[]{:S(2)}) collective-permute-start(f32[8,128]{1,0:T(8,128)S(1)} %add.12), channel_id=1, source_target_pairs={{0,1},{1,0},{2,3},{3,2},{4,5},{5,4},{6,7},{7,6},{8,9},{9,8},{10,11... | collective-permute-start | bytes 12296 | tf_op jit(solution)/shard_map/ppermute | solution.py:218
  52.6 3.6 %collective-permute-start.25 = (f32[8,128]{1,0:T(8,128)S(1)}, f32[8,128]{1,0:T(8,128)S(1)}, u32[]{:S(2)}, u32[]{:S(2)}) collective-permute-start(f32[8,128]{1,0:T(8,128)S(1)} %add.12), channel_id=1, source_target_pairs={{0,4},{1,5},{2,6},{3,7},{4,0},{5,1},{6,2},{7,3},{8,12},{9,13},{10,... | collective-permute-start | bytes 12296 | tf_op jit(solution)/shard_map/ppermute | solution.py:218
  53.7 4.6 %collective-permute-start.26 = (f32[8,128]{1,0:T(8,128)S(1)}, f32[8,128]{1,0:T(8,128)S(1)}, u32[]{:S(2)}, u32[]{:S(2)}) collective-permute-start(f32[8,128]{1,0:T(8,128)S(1)} %add.12), channel_id=1, source_target_pairs={{0,5},{1,4},{2,7},{3,6},{4,1},{5,0},{6,3},{7,2},{8,13},{9,12},{10,... | collective-permute-start | bytes 12296 | tf_op jit(solution)/shard_map/ppermute | solution.py:218
  55.0 13.1 %collective-permute-start.22 = (f32[128,256]{1,0:T(8,128)S(1)}, f32[128,256]{1,0:T(8,128)S(1)}, u32[]{:S(2)}, u32[]{:S(2)}) collective-permute-start(f32[128,256]{1,0:T(8,128)S(1)} %get-tuple-element.57), channel_id=1, source_target_pairs={{0,1},{1,0},{2,3},{3,2},{4,5},{5,4},{6,7},{7,6},{8,9},{9,8},{10,11... | collective-permute-start | bytes 393224 | tf_op jit(solution)/shard_map/ppermute | solution.py:218
  58.4 5.7 %collective-permute-start.27 = (f32[8,128]{1,0:T(8,128)S(1)}, f32[8,128]{1,0:T(8,128)S(1)}, u32[]{:S(2)}, u32[]{:S(2)}) collective-permute-start(f32[8,128]{1,0:T(8,128)S(1)} %add_add_fusion.refs_0_), channel_id=1, source_target_pairs={{0,8},{1,9},{2,10},{3,11},{4,12},{5,13},{6,14},{7,15},{8,0},{9,1},... | collective-permute-start | bytes 12296 | tf_op jit(solution)/shard_map/ppermute | solution.py:218
  60.7 4.5 %collective-permute-start.28 = (f32[8,128]{1,0:T(8,128)S(1)}, f32[8,128]{1,0:T(8,128)S(1)}, u32[]{:S(2)}, u32[]{:S(2)}) collective-permute-start(f32[8,128]{1,0:T(8,128)S(1)} %add_add_fusion.refs_0_), channel_id=1, source_target_pairs={{0,16},{1,17},{2,18},{3,19},{4,20},{5,21},{6,22},{7,23},{8,24},{9,... | collective-permute-start | bytes 12296 | tf_op jit(solution)/shard_map/ppermute | solution.py:218
  62.7 5.4 %collective-permute-start.29 = (f32[8,128]{1,0:T(8,128)S(1)}, f32[8,128]{1,0:T(8,128)S(1)}, u32[]{:S(2)}, u32[]{:S(2)}) collective-permute-start(f32[8,128]{1,0:T(8,128)S(1)} %add_add_fusion.refs_0_), channel_id=1, source_target_pairs={{0,24},{1,25},{2,26},{3,27},{4,28},{5,29},{6,30},{7,31},{8,16},{9,... | collective-permute-start | bytes 12296 | tf_op jit(solution)/shard_map/ppermute | solution.py:218
  (10 other events, 10.9 us)

commit v2 on v1

--- a/solution.py
+++ b/solution.py
@@ -33,7 +33,7 @@
     index = lax.axis_index("dp") * n_tp + lax.axis_index("tp")
     base = 0
     if load:
-        *outs, x_vmem, s_vmem, sems = refs
+        g_ref, *outs, x_vmem, s_vmem, sems = refs
         (j,) = planes
         width = plane * sub
         base = lax.bitwise_xor(index, jnp.int32(j * plane)) // plane * plane
@@ -48,6 +48,11 @@
         for copy in copies:
             copy.wait()
         x_ref, s_ref = x_vmem, s_vmem
+        rows = x_vmem.shape[0]
+        for out in outs:
+            for h in range(n_tp):
+                hd = g_ref.shape[1]
+                out[:, 2 * sub + h * hd:2 * sub + (h + 1) * hd] = g_ref[h * rows:(h + 1) * rows, :]
     else:
         outs = refs
     scales = s_ref[...]
@@ -60,8 +65,9 @@
                 out[:, h * sub:(h + 1) * sub] = dequantize(values, scales, part * (sub // block), sub, block)
 
 
-def pack(x, scales, n_tp, plane, planes, keys, core, sub, load):
+def pack(x, scales, n_tp, plane, planes, keys, core, sub, *load):
     rows = x.shape[0]
+    extra = load[0].size // rows if load else 0
     block = x.shape[1] // scales.shape[0]
     outs = len(planes) * len(keys)
     scratch = [
@@ -70,35 +76,34 @@
         pltpu.SemaphoreType.DMA((2,)),
     ]
     return pl.pallas_call(
-        functools.partial(pack_kernel, n_tp, plane, planes, keys, core, sub, block, load),
-        out_shape=[jax.ShapeDtypeStruct((rows, 2 * sub), jnp.bfloat16)] * outs,
-        in_specs=[pl.BlockSpec(memory_space=pltpu.HBM)] * 2 if load else [VMEM] * 2,
+        functools.partial(pack_kernel, n_tp, plane, planes, keys, core, sub, block, bool(load)),
+        out_shape=[jax.ShapeDtypeStruct((rows, 2 * sub + extra), jnp.bfloat16)] * outs,
+        in_specs=[pl.BlockSpec(memory_space=pltpu.HBM)] * 2 + [VMEM] if load else [VMEM] * 2,
         out_specs=[VMEM] * outs,
         scratch_shapes=scratch if load else [],
-        compiler_params=params(67_043_328 - x.size * 5 // 4) if load else params(),
+        compiler_params=params(FIRST_LIMIT) if load else params(),
         cost_estimate=cost(4 * rows * sub * outs, 8 * rows * sub * outs),
         name="pack",
-    )(x, scales)
-
-
-def grads_kernel(n_tp, rows, *refs):
+    )(x, scales, *load)
+
+
+def grads_kernel(n_tp, rows, hd, base, *refs):
     *ins, out = refs
     tp = lax.axis_index("tp")
-    hd = ins[0].shape[1]
     for g in range(len(ins) // n_tp):
         for kt in range(n_tp):
-            start = pl.multiple_of(lax.bitwise_xor(tp, jnp.int32(kt)) * rows, rows)
+            start = pl.multiple_of(base + lax.bitwise_xor(tp, jnp.int32(kt)) * hd, hd)
             for h in range(n_tp):
-                piece = ins[g * n_tp + h][pl.ds(start, rows), :]
+                piece = ins[g * n_tp + h][:, pl.ds(start, hd)]
                 column = (g * n_tp + kt) * rows
                 out[h * hd:(h + 1) * hd, column:column + rows] = piece.T
 
 
-def grads(pieces, n_tp, rows):
-    hd = pieces[0].shape[1]
+def grads(pieces, n_tp, hd, base):
+    rows = pieces[0].shape[0]
     size = len(pieces) * rows * hd * n_tp
     return pl.pallas_call(
-        functools.partial(grads_kernel, n_tp, rows),
+        functools.partial(grads_kernel, n_tp, rows, hd, base),
         out_shape=jax.ShapeDtypeStruct((n_tp * hd, len(pieces) * rows), jnp.bfloat16),
         in_specs=[VMEM] * len(pieces),
         out_specs=VMEM,
@@ -111,7 +116,7 @@
 def matmul_kernel(sub, gt_ref, *refs):
     *ins, mine, theirs = refs
     gt = gt_ref[...]
-    x = jnp.concatenate([r[...] for r in ins], axis=0)
+    x = jnp.concatenate([r[:, :2 * sub] for r in ins], axis=0)
     theirs[...] = jnp.dot(gt, x[:, sub:], preferred_element_type=jnp.float32)
     mine[...] = jnp.dot(gt, x[:, :sub], preferred_element_type=jnp.float32)
 
@@ -195,6 +200,7 @@
     )(own, other, *squares)
 
 
+FIRST_LIMIT = 54_000_000
 INNER = 4
 
 
@@ -208,7 +214,7 @@
     count = n_dp * n_tp
     plane = INNER * n_tp
     depth = count // plane
-    rows, width = stash_values.shape
+    _, width = stash_values.shape
     sub = width // count
     keys = keys_of(n_tp)
     core = n_tp
@@ -218,14 +224,14 @@
         return lax.ppermute(value, AXES, [(i, i ^ distance) for i in range(count)])
 
     order = list(range(depth - 1, -1, -1))
-    packed = pack(stash_values, scales, n_tp, plane, order[:1], keys, core, sub, True)
-    packed += pack(stash_values, scales, n_tp, plane, order[1:], keys, core, sub, False)
-    near = [value_grad] + [send(value_grad, k) for k in keys[1:]]
-    gt = grads(near, n_tp, rows)
+    packed = pack(stash_values, scales, n_tp, plane, order[:1], keys, core, sub, value_grad)
+    packed += pack(stash_values, scales, n_tp, plane, order[1:], keys, core, sub)
     parts = []
     for n, j in enumerate(order):
         own, *away = packed[n * len(keys):(n + 1) * len(keys)]
         arrived = [own] + [send(v, k) for k, v in zip(keys[1:], away)]
+        if n == 0:
+            gt = grads(arrived, n_tp, value_grad.shape[1], 2 * sub)
         mine, theirs = matmul(gt, arrived, sub)
         theirs = send(theirs, core)
         if j:

time: 69.2 us -> 66.6 us (0.962)
  waiting for transfers between devices: 20.1 us -> 29 us
  starting transfers between devices: 36.4 us -> 31.2 us
  local copies, waits for them, and re-layouts: 6.56 us -> 1.71 us
  Pallas kernels: 5.7 us -> 4.33 us
    ppermute x30 -> x27, waiting for transfers between devices: 20.1 us -> 29 us  [send(): return lax.ppermute(value, AXES, [(i, i ^ distance) for i in range(count)])]
    ppermute x30 -> x27, starting transfers between devices: 36.4 us -> 31.2 us  [send(): return lax.ppermute(value, AXES, [(i, i ^ distance) for i in range(count)])]
    unnamed x24 -> x6, local copies, waits for them, and re-layouts: 6.56 us -> 1.71 us
    pallas_call x2, Pallas kernels: 3.36 us -> 2 us  [pack(): pl.pallas_call(functools.partial(pack_kernel, n_tp, plane, planes, keys,...]
  transfers between devices with their start and end apart: 30 -> 27, of which waited for: 10 -> 14; matrix products, arithmetic and copies ran while one was open for 0% -> 0% of each run, Pallas kernels for 7% -> 3%
where the time goes in v2:
time: 66.6 us; the launch traced here: 66.4 us
  starting transfers between devices  31.2 us (47%)
  waiting for transfers between devices  29 us (44%)
  Pallas kernels  4.33 us (7%)
  local copies, waits for them, and re-layouts  1.71 us (3%)
    ppermute x27, starting transfers between devices, send(): return lax.ppermute(value, AXES, [(i, i ^ distance) for i in range(count)])  31.2 us
    ppermute x27, waiting for transfers between devices, send(): return lax.ppermute(value, AXES, [(i, i ^ distance) for i in range(count)])  29 us
    pallas_call x2, Pallas kernels, pack(): pl.pallas_call(functools.partial(pack_kernel, n_tp, plane, planes, keys,...  2 us
    unnamed x6, local copies, waits for them, and re-layouts  1.71 us
  transfers between devices with their start and end apart: 27, of which 14 were waited for; matrix products, arithmetic and copies ran while one was open for 0% of the time, Pallas kernels for 3%

profile of v2, /device:TPU:0, one launch (start us, length us, event | category | flops | bytes accessed | tf_op | source)
XLA Modules:
  0.0 66.4 jit_solution(1433324022500316952)
XLA Ops:
  0.0 0.9 %copy-done.1 = bf16[128,64]{0,1:T(8,128)(2,1)S(1)} copy-done((bf16[128,64]{0,1:T(8,128)(2,1)S(1)}, bf16[128,64]{0,1:T(8,128)(2,1)}, u32[]{:S(2)}) %copy-start.1) | copy-done | bytes 16408
  0.9 0.8 %copy-done.2 = bf16[256,128]{1,0:T(8,128)(2,1)S(1)} copy-done((bf16[256,128]{1,0:T(8,128)(2,1)S(1)}, bf16[256,128]{1,0:T(8,128)(2,1)}, u32[]{:S(2)}) %copy-start.2) | copy-done | bytes 65560
  1.7 1.4 %pack.2 = (bf16[128,768]{1,0:T(8,128)(2,1)S(1)}, bf16[128,768]{1,0:T(8,128)(2,1)S(1)}, bf16[128,768]{1,0:T(8,128)(2,1)S(1)}, bf16[128,768]{1,0:T(8,128)(2,1)S(1)}) custom-call(bf16[128,8192]{1,0:T(8,128)(2,1)} %x_ref.3, bf16[64,128]{1,0:T(8,128)(2,1)S(1)} %bitcast.1, bf16[256,128]{1,0:T(8,128)(2,1)S(1)} %copy-done.2), custom_call_target="tpu_custom_call" | custom-call | flops 524288 | bytes 1048576 | tf_op jit(solution)/shard_map/pack/pallas_call | solution.py:78
  3.1 3.1 %collective-permute-start = (bf16[128,768]{1,0:T(8,128)(2,1)S(1)}, bf16[128,768]{1,0:T(8,128)(2,1)S(1)}, u32[]{:S(2)}, u32[]{:S(2)}) collective-permute-start(bf16[128,768]{1,0:T(8,128)(2,1)S(1)} %get-tuple-element.33), channel_id=1, source_target_pairs={{0,1},{1,0},{2,3},{3,2},{4,5},{5,4},{6,7},{7,6},{8,9},{9,8},{10,11... | collective-permute-start | bytes 589832 | tf_op jit(solution)/shard_map/ppermute | solution.py:224
  6.2 1.5 %collective-permute-start.1 = (bf16[128,768]{1,0:T(8,128)(2,1)S(1)}, bf16[128,768]{1,0:T(8,128)(2,1)S(1)}, u32[]{:S(2)}, u32[]{:S(2)}) collective-permute-start(bf16[128,768]{1,0:T(8,128)(2,1)S(1)} %get-tuple-element.34), channel_id=1, source_target_pairs={{0,4},{1,5},{2,6},{3,7},{4,0},{5,1},{6,2},{7,3},{8,12},{9,13},{10,... | collective-permute-start | bytes 589832 | tf_op jit(solution)/shard_map/ppermute | solution.py:224
  7.7 0.6 pack.3
  8.3 2.0 %collective-permute-start.12 = (bf16[128,512]{1,0:T(8,128)(2,1)S(1)}, bf16[128,512]{1,0:T(8,128)(2,1)S(1)}, u32[]{:S(2)}, u32[]{:S(2)}) collective-permute-start(bf16[128,512]{1,0:T(8,128)(2,1)S(1)} %get-tuple-element.49), channel_id=1, source_target_pairs={{0,1},{1,0},{2,3},{3,2},{4,5},{5,4},{6,7},{7,6},{8,9},{9,8},{10,11... | collective-permute-start | bytes 393224 | tf_op jit(solution)/shard_map/ppermute | solution.py:224
  10.3 1.5 %collective-permute-start.13 = (bf16[128,512]{1,0:T(8,128)(2,1)S(1)}, bf16[128,512]{1,0:T(8,128)(2,1)S(1)}, u32[]{:S(2)}, u32[]{:S(2)}) collective-permute-start(bf16[128,512]{1,0:T(8,128)(2,1)S(1)} %get-tuple-element.50), channel_id=1, source_target_pairs={{0,4},{1,5},{2,6},{3,7},{4,0},{5,1},{6,2},{7,3},{8,12},{9,13},{10,... | collective-permute-start | bytes 393224 | tf_op jit(solution)/shard_map/ppermute | solution.py:224
  11.8 6.3 %collective-permute-done.12.refs_1_ = bf16[128,512]{1,0:T(8,128)(2,1)S(1)} collective-permute-done((bf16[128,512]{1,0:T(8,128)(2,1)S(1)}, bf16[128,512]{1,0:T(8,128)(2,1)S(1)}, u32[]{:S(2)}, u32[]{:S(2)}) %collective-permute-start.12) | collective-permute-done | bytes 131104 | tf_op jit(solution)/shard_map/ppermute | solution.py:224
  18.1 2.7 %collective-permute-start.14 = (bf16[128,512]{1,0:T(8,128)(2,1)S(1)}, bf16[128,512]{1,0:T(8,128)(2,1)S(1)}, u32[]{:S(2)}, u32[]{:S(2)}) collective-permute-start(bf16[128,512]{1,0:T(8,128)(2,1)S(1)} %get-tuple-element.51), channel_id=1, source_target_pairs={{0,5},{1,4},{2,7},{3,6},{4,1},{5,0},{6,3},{7,2},{8,13},{9,12},{10,... | collective-permute-start | bytes 393224 | tf_op jit(solution)/shard_map/ppermute | solution.py:224
  21.6 2.7 %collective-permute-start.9 = (bf16[128,512]{1,0:T(8,128)(2,1)S(1)}, bf16[128,512]{1,0:T(8,128)(2,1)S(1)}, u32[]{:S(2)}, u32[]{:S(2)}) collective-permute-start(bf16[128,512]{1,0:T(8,128)(2,1)S(1)} %get-tuple-element.45), channel_id=1, source_target_pairs={{0,5},{1,4},{2,7},{3,6},{4,1},{5,0},{6,3},{7,2},{8,13},{9,12},{10,... | collective-permute-start | bytes 393224 | tf_op jit(solution)/shard_map/ppermute | solution.py:224
  25.2 2.0 %collective-permute-start.4 = (bf16[128,512]{1,0:T(8,128)(2,1)S(1)}, bf16[128,512]{1,0:T(8,128)(2,1)S(1)}, u32[]{:S(2)}, u32[]{:S(2)}) collective-permute-start(bf16[128,512]{1,0:T(8,128)(2,1)S(1)} %get-tuple-element.38), channel_id=1, source_target_pairs={{0,4},{1,5},{2,6},{3,7},{4,0},{5,1},{6,2},{7,3},{8,12},{9,13},{10,... | collective-permute-start | bytes 393224 | tf_op jit(solution)/shard_map/ppermute | solution.py:224
  27.5 1.7 %collective-permute-done.7.refs_1_ = bf16[128,512]{1,0:T(8,128)(2,1)S(1)} collective-permute-done((bf16[128,512]{1,0:T(8,128)(2,1)S(1)}, bf16[128,512]{1,0:T(8,128)(2,1)S(1)}, u32[]{:S(2)}, u32[]{:S(2)}) %collective-permute-start.7) | collective-permute-done | bytes 131104 | tf_op jit(solution)/shard_map/ppermute | solution.py:224
  29.2 1.0 %collective-permute-start.5 = (bf16[128,512]{1,0:T(8,128)(2,1)S(1)}, bf16[128,512]{1,0:T(8,128)(2,1)S(1)}, u32[]{:S(2)}, u32[]{:S(2)}) collective-permute-start(bf16[128,512]{1,0:T(8,128)(2,1)S(1)} %get-tuple-element.39), channel_id=1, source_target_pairs={{0,5},{1,4},{2,7},{3,6},{4,1},{5,0},{6,3},{7,2},{8,13},{9,12},{10,... | collective-permute-start | bytes 393224 | tf_op jit(solution)/shard_map/ppermute | solution.py:224
  30.2 1.3 %collective-permute-done.9.refs_3_ = bf16[128,512]{1,0:T(8,128)(2,1)S(1)} collective-permute-done((bf16[128,512]{1,0:T(8,128)(2,1)S(1)}, bf16[128,512]{1,0:T(8,128)(2,1)S(1)}, u32[]{:S(2)}, u32[]{:S(2)}) %collective-permute-start.9) | collective-permute-done | bytes 131104 | tf_op jit(solution)/shard_map/ppermute | solution.py:224
  31.8 1.1 %collective-permute-done.3.refs_1_ = bf16[128,512]{1,0:T(8,128)(2,1)S(1)} collective-permute-done((bf16[128,512]{1,0:T(8,128)(2,1)S(1)}, bf16[128,512]{1,0:T(8,128)(2,1)S(1)}, u32[]{:S(2)}, u32[]{:S(2)}) %collective-permute-start.3) | collective-permute-done | bytes 131104 | tf_op jit(solution)/shard_map/ppermute | solution.py:224
  33.1 2.1 %collective-permute-done.5.refs_3_ = bf16[128,512]{1,0:T(8,128)(2,1)S(1)} collective-permute-done((bf16[128,512]{1,0:T(8,128)(2,1)S(1)}, bf16[128,512]{1,0:T(8,128)(2,1)S(1)}, u32[]{:S(2)}, u32[]{:S(2)}) %collective-permute-start.5) | collective-permute-done | bytes 131104 | tf_op jit(solution)/shard_map/ppermute | solution.py:224
  35.6 4.0 %collective-permute-start.18 = (bf16[256,256]{1,0:T(8,128)(2,1)S(1)}, bf16[256,256]{1,0:T(8,128)(2,1)S(1)}, u32[]{:S(2)}, u32[]{:S(2)}) collective-permute-start(bf16[256,256]{1,0:T(8,128)(2,1)S(1)} %join.5), channel_id=1, source_target_pairs={{0,24},{1,25},{2,26},{3,27},{4,28},{5,29},{6,30},{7,31},{8,16},{9,... | collective-permute-start | bytes 393224 | tf_op jit(solution)/shard_map/ppermute | solution.py:224
  39.8 0.6 collective-permute-start.11
  40.4 3.7 %collective-permute-done.18.refs_4_ = bf16[256,256]{1,0:T(8,128)(2,1)S(1)} collective-permute-done((bf16[256,256]{1,0:T(8,128)(2,1)S(1)}, bf16[256,256]{1,0:T(8,128)(2,1)S(1)}, u32[]{:S(2)}, u32[]{:S(2)}) %collective-permute-start.18) | collective-permute-done | bytes 131104 | tf_op jit(solution)/shard_map/ppermute | solution.py:224
  44.1 7.3 %collective-permute-done.16.refs_3_ = bf16[256,256]{1,0:T(8,128)(2,1)S(1)} collective-permute-done((bf16[256,256]{1,0:T(8,128)(2,1)S(1)}, bf16[256,256]{1,0:T(8,128)(2,1)S(1)}, u32[]{:S(2)}, u32[]{:S(2)}) %collective-permute-start.16) | collective-permute-done | bytes 131104 | tf_op jit(solution)/shard_map/ppermute | solution.py:224
  51.5 1.2 %collective-permute-done.20 = f32[8,128]{1,0:T(8,128)S(1)} collective-permute-done((f32[8,128]{1,0:T(8,128)S(1)}, f32[8,128]{1,0:T(8,128)S(1)}, u32[]{:S(2)}, u32[]{:S(2)}) %collective-permute-start.20) | collective-permute-done | bytes 4128 | tf_op jit(solution)/shard_map/ppermute | solution.py:224
  52.7 1.4 %collective-permute-start.23 = (f32[8,128]{1,0:T(8,128)S(1)}, f32[8,128]{1,0:T(8,128)S(1)}, u32[]{:S(2)}, u32[]{:S(2)}) collective-permute-start(f32[8,128]{1,0:T(8,128)S(1)} %add.12), channel_id=1, source_target_pairs={{0,5},{1,4},{2,7},{3,6},{4,1},{5,0},{6,3},{7,2},{8,13},{9,12},{10,... | collective-permute-start | bytes 12296 | tf_op jit(solution)/shard_map/ppermute | solution.py:224
  54.1 0.8 %collective-permute-start.22 = (f32[8,128]{1,0:T(8,128)S(1)}, f32[8,128]{1,0:T(8,128)S(1)}, u32[]{:S(2)}, u32[]{:S(2)}) collective-permute-start(f32[8,128]{1,0:T(8,128)S(1)} %add.12), channel_id=1, source_target_pairs={{0,4},{1,5},{2,6},{3,7},{4,0},{5,1},{6,2},{7,3},{8,12},{9,13},{10,... | collective-permute-start | bytes 12296 | tf_op jit(solution)/shard_map/ppermute | solution.py:224
  54.9 1.3 %collective-permute-start.21 = (f32[8,128]{1,0:T(8,128)S(1)}, f32[8,128]{1,0:T(8,128)S(1)}, u32[]{:S(2)}, u32[]{:S(2)}) collective-permute-start(f32[8,128]{1,0:T(8,128)S(1)} %add.12), channel_id=1, source_target_pairs={{0,1},{1,0},{2,3},{3,2},{4,5},{5,4},{6,7},{7,6},{8,9},{9,8},{10,11... | collective-permute-start | bytes 12296 | tf_op jit(solution)/shard_map/ppermute | solution.py:224
  56.2 0.8 %collective-permute-start.19 = (f32[128,256]{1,0:T(8,128)S(1)}, f32[128,256]{1,0:T(8,128)S(1)}, u32[]{:S(2)}, u32[]{:S(2)}) collective-permute-start(f32[128,256]{1,0:T(8,128)S(1)} %get-tuple-element.57), channel_id=1, source_target_pairs={{0,1},{1,0},{2,3},{3,2},{4,5},{5,4},{6,7},{7,6},{8,9},{9,8},{10,11... | collective-permute-start | bytes 393224 | tf_op jit(solution)/shard_map/ppermute | solution.py:224
  57.7 0.8 %collective-permute-done.21 = f32[8,128]{1,0:T(8,128)S(1)} collective-permute-done((f32[8,128]{1,0:T(8,128)S(1)}, f32[8,128]{1,0:T(8,128)S(1)}, u32[]{:S(2)}, u32[]{:S(2)}) %collective-permute-start.21) | collective-permute-done | bytes 4128 | tf_op jit(solution)/shard_map/ppermute | solution.py:224
  58.5 2.5 %collective-permute-start.26 = (f32[8,128]{1,0:T(8,128)S(1)}, f32[8,128]{1,0:T(8,128)S(1)}, u32[]{:S(2)}, u32[]{:S(2)}) collective-permute-start(f32[8,128]{1,0:T(8,128)S(1)} %add_add_fusion.refs_0_), channel_id=1, source_target_pairs={{0,24},{1,25},{2,26},{3,27},{4,28},{5,29},{6,30},{7,31},{8,16},{9,... | collective-permute-start | bytes 12296 | tf_op jit(solution)/shard_map/ppermute | solution.py:224
  61.0 1.9 %collective-permute-start.24 = (f32[8,128]{1,0:T(8,128)S(1)}, f32[8,128]{1,0:T(8,128)S(1)}, u32[]{:S(2)}, u32[]{:S(2)}) collective-permute-start(f32[8,128]{1,0:T(8,128)S(1)} %add_add_fusion.refs_0_), channel_id=1, source_target_pairs={{0,8},{1,9},{2,10},{3,11},{4,12},{5,13},{6,14},{7,15},{8,0},{9,1},... | collective-permute-start | bytes 12296 | tf_op jit(solution)/shard_map/ppermute | solution.py:224
  62.9 1.0 %collective-permute-done.26.refs_3_ = f32[8,128]{1,0:T(8,128)S(1)} collective-permute-done((f32[8,128]{1,0:T(8,128)S(1)}, f32[8,128]{1,0:T(8,128)S(1)}, u32[]{:S(2)}, u32[]{:S(2)}) %collective-permute-start.26) | collective-permute-done | bytes 4128 | tf_op jit(solution)/shard_map/ppermute | solution.py:224
  63.9 1.6 %collective-permute-done.25.refs_2_ = f32[8,128]{1,0:T(8,128)S(1)} collective-permute-done((f32[8,128]{1,0:T(8,128)S(1)}, f32[8,128]{1,0:T(8,128)S(1)}, u32[]{:S(2)}, u32[]{:S(2)}) %collective-permute-start.25) | collective-permute-done | bytes 4128 | tf_op jit(solution)/shard_map/ppermute | solution.py:224
  65.5 0.9 %clip.1 = f32[512,128]{1,0:T(8,128)} custom-call(f32[128,256]{1,0:T(8,128)S(1)} %get-tuple-element.56.own, f32[128,256]{1,0:T(8,128)S(1)} %collective-permute-done.19.other, f32[8,128]{1,0:T(8,128)S(1)} %add_add_fusion.refs_0_, f32[8,128]{1,0:T(8,128)S(1)} %collective-permute-done.24.refs_1_, f32[8,128]{1,0:T(8,128)S(1)} %collective-permute-done.25.refs_2_, ...), custom_call_target="tpu_custom_call" | custom-call | flops 131072 | bytes 524288 | tf_op jit(solution)/shard_map/clip/pallas_call | solution.py:192
  (42 shorter events, 4.2 us)
Async XLA Ops:
  0.0 7.7 %copy-start = (bf16[128,8192]{1,0:T(8,128)(2,1)S(1)}, bf16[128,8192]{1,0:T(8,128)(2,1)}, u32[]{:S(2)}) copy-start(bf16[128,8192]{1,0:T(8,128)(2,1)} %x_ref.3) | copy-start | bytes 6291460
  0.0 0.9 %copy-start.1 = (bf16[128,64]{0,1:T(8,128)(2,1)S(1)}, bf16[128,64]{0,1:T(8,128)(2,1)}, u32[]{:S(2)}) copy-start(bf16[128,64]{0,1:T(8,128)(2,1)} %param.4) | copy-start | bytes 49156
  0.9 0.8 %copy-start.2 = (bf16[256,128]{1,0:T(8,128)(2,1)S(1)}, bf16[256,128]{1,0:T(8,128)(2,1)}, u32[]{:S(2)}) copy-start(bf16[256,128]{1,0:T(8,128)(2,1)} %refs_0_.1) | copy-start | bytes 196612
  3.1 18.2 %collective-permute-start = (bf16[128,768]{1,0:T(8,128)(2,1)S(1)}, bf16[128,768]{1,0:T(8,128)(2,1)S(1)}, u32[]{:S(2)}, u32[]{:S(2)}) collective-permute-start(bf16[128,768]{1,0:T(8,128)(2,1)S(1)} %get-tuple-element.33), channel_id=1, source_target_pairs={{0,1},{1,0},{2,3},{3,2},{4,5},{5,4},{6,7},{7,6},{8,9},{9,8},{10,11... | collective-permute-start | bytes 589832 | tf_op jit(solution)/shard_map/ppermute | solution.py:224
  6.2 15.4 %collective-permute-start.1 = (bf16[128,768]{1,0:T(8,128)(2,1)S(1)}, bf16[128,768]{1,0:T(8,128)(2,1)S(1)}, u32[]{:S(2)}, u32[]{:S(2)}) collective-permute-start(bf16[128,768]{1,0:T(8,128)(2,1)S(1)} %get-tuple-element.34), channel_id=1, source_target_pairs={{0,4},{1,5},{2,6},{3,7},{4,0},{5,1},{6,2},{7,3},{8,12},{9,13},{10,... | collective-permute-start | bytes 589832 | tf_op jit(solution)/shard_map/ppermute | solution.py:224
  7.7 16.6 %collective-permute-start.2 = (bf16[128,768]{1,0:T(8,128)(2,1)S(1)}, bf16[128,768]{1,0:T(8,128)(2,1)S(1)}, u32[]{:S(2)}, u32[]{:S(2)}) collective-permute-start(bf16[128,768]{1,0:T(8,128)(2,1)S(1)} %get-tuple-element.35), channel_id=1, source_target_pairs={{0,5},{1,4},{2,7},{3,6},{4,1},{5,0},{6,3},{7,2},{8,13},{9,12},{10,... | collective-permute-start | bytes 589832 | tf_op jit(solution)/shard_map/ppermute | solution.py:224
  8.3 9.8 %collective-permute-start.12 = (bf16[128,512]{1,0:T(8,128)(2,1)S(1)}, bf16[128,512]{1,0:T(8,128)(2,1)S(1)}, u32[]{:S(2)}, u32[]{:S(2)}) collective-permute-start(bf16[128,512]{1,0:T(8,128)(2,1)S(1)} %get-tuple-element.49), channel_id=1, source_target_pairs={{0,1},{1,0},{2,3},{3,2},{4,5},{5,4},{6,7},{7,6},{8,9},{9,8},{10,11... | collective-permute-start | bytes 393224 | tf_op jit(solution)/shard_map/ppermute | solution.py:224
  10.3 10.4 %collective-permute-start.13 = (bf16[128,512]{1,0:T(8,128)(2,1)S(1)}, bf16[128,512]{1,0:T(8,128)(2,1)S(1)}, u32[]{:S(2)}, u32[]{:S(2)}) collective-permute-start(bf16[128,512]{1,0:T(8,128)(2,1)S(1)} %get-tuple-element.50), channel_id=1, source_target_pairs={{0,4},{1,5},{2,6},{3,7},{4,0},{5,1},{6,2},{7,3},{8,12},{9,13},{10,... | collective-permute-start | bytes 393224 | tf_op jit(solution)/shard_map/ppermute | solution.py:224
  18.1 7.1 %collective-permute-start.14 = (bf16[128,512]{1,0:T(8,128)(2,1)S(1)}, bf16[128,512]{1,0:T(8,128)(2,1)S(1)}, u32[]{:S(2)}, u32[]{:S(2)}) collective-permute-start(bf16[128,512]{1,0:T(8,128)(2,1)S(1)} %get-tuple-element.51), channel_id=1, source_target_pairs={{0,5},{1,4},{2,7},{3,6},{4,1},{5,0},{6,3},{7,2},{8,13},{9,12},{10,... | collective-permute-start | bytes 393224 | tf_op jit(solution)/shard_map/ppermute | solution.py:224
  20.8 8.4 %collective-permute-start.7 = (bf16[128,512]{1,0:T(8,128)(2,1)S(1)}, bf16[128,512]{1,0:T(8,128)(2,1)S(1)}, u32[]{:S(2)}, u32[]{:S(2)}) collective-permute-start(bf16[128,512]{1,0:T(8,128)(2,1)S(1)} %get-tuple-element.43), channel_id=1, source_target_pairs={{0,1},{1,0},{2,3},{3,2},{4,5},{5,4},{6,7},{7,6},{8,9},{9,8},{10,11... | collective-permute-start | bytes 393224 | tf_op jit(solution)/shard_map/ppermute | solution.py:224
  21.3 8.9 %collective-permute-start.8 = (bf16[128,512]{1,0:T(8,128)(2,1)S(1)}, bf16[128,512]{1,0:T(8,128)(2,1)S(1)}, u32[]{:S(2)}, u32[]{:S(2)}) collective-permute-start(bf16[128,512]{1,0:T(8,128)(2,1)S(1)} %get-tuple-element.44), channel_id=1, source_target_pairs={{0,4},{1,5},{2,6},{3,7},{4,0},{5,1},{6,2},{7,3},{8,12},{9,13},{10,... | collective-permute-start | bytes 393224 | tf_op jit(solution)/shard_map/ppermute | solution.py:224
  21.6 9.9 %collective-permute-start.9 = (bf16[128,512]{1,0:T(8,128)(2,1)S(1)}, bf16[128,512]{1,0:T(8,128)(2,1)S(1)}, u32[]{:S(2)}, u32[]{:S(2)}) collective-permute-start(bf16[128,512]{1,0:T(8,128)(2,1)S(1)} %get-tuple-element.45), channel_id=1, source_target_pairs={{0,5},{1,4},{2,7},{3,6},{4,1},{5,0},{6,3},{7,2},{8,13},{9,12},{10,... | collective-permute-start | bytes 393224 | tf_op jit(solution)/shard_map/ppermute | solution.py:224
  24.3 8.6 %collective-permute-start.3 = (bf16[128,512]{1,0:T(8,128)(2,1)S(1)}, bf16[128,512]{1,0:T(8,128)(2,1)S(1)}, u32[]{:S(2)}, u32[]{:S(2)}) collective-permute-start(bf16[128,512]{1,0:T(8,128)(2,1)S(1)} %get-tuple-element.37), channel_id=1, source_target_pairs={{0,1},{1,0},{2,3},{3,2},{4,5},{5,4},{6,7},{7,6},{8,9},{9,8},{10,11... | collective-permute-start | bytes 393224 | tf_op jit(solution)/shard_map/ppermute | solution.py:224
  25.2 7.9 %collective-permute-start.4 = (bf16[128,512]{1,0:T(8,128)(2,1)S(1)}, bf16[128,512]{1,0:T(8,128)(2,1)S(1)}, u32[]{:S(2)}, u32[]{:S(2)}) collective-permute-start(bf16[128,512]{1,0:T(8,128)(2,1)S(1)} %get-tuple-element.38), channel_id=1, source_target_pairs={{0,4},{1,5},{2,6},{3,7},{4,0},{5,1},{6,2},{7,3},{8,12},{9,13},{10,... | collective-permute-start | bytes 393224 | tf_op jit(solution)/shard_map/ppermute | solution.py:224
  29.2 6.0 %collective-permute-start.5 = (bf16[128,512]{1,0:T(8,128)(2,1)S(1)}, bf16[128,512]{1,0:T(8,128)(2,1)S(1)}, u32[]{:S(2)}, u32[]{:S(2)}) collective-permute-start(bf16[128,512]{1,0:T(8,128)(2,1)S(1)} %get-tuple-element.39), channel_id=1, source_target_pairs={{0,5},{1,4},{2,7},{3,6},{4,1},{5,0},{6,3},{7,2},{8,13},{9,12},{10,... | collective-permute-start | bytes 393224 | tf_op jit(solution)/shard_map/ppermute | solution.py:224
  30.2 5.4 %collective-permute-start.17 = (f32[256,256]{1,0:T(8,128)S(1)}, f32[256,256]{1,0:T(8,128)S(1)}, u32[]{:S(2)}, u32[]{:S(2)}) collective-permute-start(f32[256,256]{1,0:T(8,128)S(1)} %get-tuple-element.55), channel_id=1, source_target_pairs={{0,2},{1,3},{2,0},{3,1},{4,6},{5,7},{6,4},{7,5},{8,10},{9,11},{10,... | collective-permute-start | bytes 786440 | tf_op jit(solution)/shard_map/ppermute | solution.py:224
  31.5 8.1 %collective-permute-start.15 = (f32[256,256]{1,0:T(8,128)S(1)}, f32[256,256]{1,0:T(8,128)S(1)}, u32[]{:S(2)}, u32[]{:S(2)}) collective-permute-start(f32[256,256]{1,0:T(8,128)S(1)} %get-tuple-element.53), channel_id=1, source_target_pairs={{0,2},{1,3},{2,0},{3,1},{4,6},{5,7},{6,4},{7,5},{8,10},{9,11},{10,... | collective-permute-start | bytes 786440 | tf_op jit(solution)/shard_map/ppermute | solution.py:224
  32.9 6.8 %collective-permute-start.10 = (f32[256,256]{1,0:T(8,128)S(1)}, f32[256,256]{1,0:T(8,128)S(1)}, u32[]{:S(2)}, u32[]{:S(2)}) collective-permute-start(f32[256,256]{1,0:T(8,128)S(1)} %get-tuple-element.47), channel_id=1, source_target_pairs={{0,2},{1,3},{2,0},{3,1},{4,6},{5,7},{6,4},{7,5},{8,10},{9,11},{10,... | collective-permute-start | bytes 786440 | tf_op jit(solution)/shard_map/ppermute | solution.py:224
  35.5 4.9 %collective-permute-start.6 = (f32[256,256]{1,0:T(8,128)S(1)}, f32[256,256]{1,0:T(8,128)S(1)}, u32[]{:S(2)}, u32[]{:S(2)}) collective-permute-start(f32[256,256]{1,0:T(8,128)S(1)} %get-tuple-element.40), channel_id=1, source_target_pairs={{0,2},{1,3},{2,0},{3,1},{4,6},{5,7},{6,4},{7,5},{8,10},{9,11},{10,... | collective-permute-start | bytes 786440 | tf_op jit(solution)/shard_map/ppermute | solution.py:224
  35.6 8.4 %collective-permute-start.18 = (bf16[256,256]{1,0:T(8,128)(2,1)S(1)}, bf16[256,256]{1,0:T(8,128)(2,1)S(1)}, u32[]{:S(2)}, u32[]{:S(2)}) collective-permute-start(bf16[256,256]{1,0:T(8,128)(2,1)S(1)} %join.5), channel_id=1, source_target_pairs={{0,24},{1,25},{2,26},{3,27},{4,28},{5,29},{6,30},{7,31},{8,16},{9,... | collective-permute-start | bytes 393224 | tf_op jit(solution)/shard_map/ppermute | solution.py:224
  39.6 11.7 %collective-permute-start.16 = (bf16[256,256]{1,0:T(8,128)(2,1)S(1)}, bf16[256,256]{1,0:T(8,128)(2,1)S(1)}, u32[]{:S(2)}, u32[]{:S(2)}) collective-permute-start(bf16[256,256]{1,0:T(8,128)(2,1)S(1)} %join.4), channel_id=1, source_target_pairs={{0,16},{1,17},{2,18},{3,19},{4,20},{5,21},{6,22},{7,23},{8,24},{9,... | collective-permute-start | bytes 393224 | tf_op jit(solution)/shard_map/ppermute | solution.py:224
  39.8 11.6 %collective-permute-start.11 = (bf16[256,256]{1,0:T(8,128)(2,1)S(1)}, bf16[256,256]{1,0:T(8,128)(2,1)S(1)}, u32[]{:S(2)}, u32[]{:S(2)}) collective-permute-start(bf16[256,256]{1,0:T(8,128)(2,1)S(1)} %join.3), channel_id=1, source_target_pairs={{0,8},{1,9},{2,10},{3,11},{4,12},{5,13},{6,14},{7,15},{8,0},{9,1},... | collective-permute-start | bytes 393224 | tf_op jit(solution)/shard_map/ppermute | solution.py:224
  51.4 1.2 %collective-permute-start.20 = (f32[8,128]{1,0:T(8,128)S(1)}, f32[8,128]{1,0:T(8,128)S(1)}, u32[]{:S(2)}, u32[]{:S(2)}) collective-permute-start(f32[8,128]{1,0:T(8,128)S(1)} %get-tuple-element.58), channel_id=1, source_target_pairs={{0,2},{1,3},{2,0},{3,1},{4,6},{5,7},{6,4},{7,5},{8,10},{9,11},{10,... | collective-permute-start | bytes 12296 | tf_op jit(solution)/shard_map/ppermute | solution.py:224
  52.7 4.5 %collective-permute-start.23 = (f32[8,128]{1,0:T(8,128)S(1)}, f32[8,128]{1,0:T(8,128)S(1)}, u32[]{:S(2)}, u32[]{:S(2)}) collective-permute-start(f32[8,128]{1,0:T(8,128)S(1)} %add.12), channel_id=1, source_target_pairs={{0,5},{1,4},{2,7},{3,6},{4,1},{5,0},{6,3},{7,2},{8,13},{9,12},{10,... | collective-permute-start | bytes 12296 | tf_op jit(solution)/shard_map/ppermute | solution.py:224
  54.1 3.6 %collective-permute-start.22 = (f32[8,128]{1,0:T(8,128)S(1)}, f32[8,128]{1,0:T(8,128)S(1)}, u32[]{:S(2)}, u32[]{:S(2)}) collective-permute-start(f32[8,128]{1,0:T(8,128)S(1)} %add.12), channel_id=1, source_target_pairs={{0,4},{1,5},{2,6},{3,7},{4,0},{5,1},{6,2},{7,3},{8,12},{9,13},{10,... | collective-permute-start | bytes 12296 | tf_op jit(solution)/shard_map/ppermute | solution.py:224
  54.9 3.7 %collective-permute-start.21 = (f32[8,128]{1,0:T(8,128)S(1)}, f32[8,128]{1,0:T(8,128)S(1)}, u32[]{:S(2)}, u32[]{:S(2)}) collective-permute-start(f32[8,128]{1,0:T(8,128)S(1)} %add.12), channel_id=1, source_target_pairs={{0,1},{1,0},{2,3},{3,2},{4,5},{5,4},{6,7},{7,6},{8,9},{9,8},{10,11... | collective-permute-start | bytes 12296 | tf_op jit(solution)/shard_map/ppermute | solution.py:224
  56.2 9.4 %collective-permute-start.19 = (f32[128,256]{1,0:T(8,128)S(1)}, f32[128,256]{1,0:T(8,128)S(1)}, u32[]{:S(2)}, u32[]{:S(2)}) collective-permute-start(f32[128,256]{1,0:T(8,128)S(1)} %get-tuple-element.57), channel_id=1, source_target_pairs={{0,1},{1,0},{2,3},{3,2},{4,5},{5,4},{6,7},{7,6},{8,9},{9,8},{10,11... | collective-permute-start | bytes 393224 | tf_op jit(solution)/shard_map/ppermute | solution.py:224
  58.5 5.4 %collective-permute-start.26 = (f32[8,128]{1,0:T(8,128)S(1)}, f32[8,128]{1,0:T(8,128)S(1)}, u32[]{:S(2)}, u32[]{:S(2)}) collective-permute-start(f32[8,128]{1,0:T(8,128)S(1)} %add_add_fusion.refs_0_), channel_id=1, source_target_pairs={{0,24},{1,25},{2,26},{3,27},{4,28},{5,29},{6,30},{7,31},{8,16},{9,... | collective-permute-start | bytes 12296 | tf_op jit(solution)/shard_map/ppermute | solution.py:224
  61.0 4.5 %collective-permute-start.25 = (f32[8,128]{1,0:T(8,128)S(1)}, f32[8,128]{1,0:T(8,128)S(1)}, u32[]{:S(2)}, u32[]{:S(2)}) collective-permute-start(f32[8,128]{1,0:T(8,128)S(1)} %add_add_fusion.refs_0_), channel_id=1, source_target_pairs={{0,16},{1,17},{2,18},{3,19},{4,20},{5,21},{6,22},{7,23},{8,24},{9,... | collective-permute-start | bytes 12296 | tf_op jit(solution)/shard_map/ppermute | solution.py:224
  61.0 4.5 %collective-permute-start.24 = (f32[8,128]{1,0:T(8,128)S(1)}, f32[8,128]{1,0:T(8,128)S(1)}, u32[]{:S(2)}, u32[]{:S(2)}) collective-permute-start(f32[8,128]{1,0:T(8,128)S(1)} %add_add_fusion.refs_0_), channel_id=1, source_target_pairs={{0,8},{1,9},{2,10},{3,11},{4,12},{5,13},{6,14},{7,15},{8,0},{9,1},... | collective-permute-start | bytes 12296 | tf_op jit(solution)/shard_map/ppermute | solution.py:224

commit v3 on v2

--- a/solution.py
+++ b/solution.py
@@ -33,26 +33,22 @@
     index = lax.axis_index("dp") * n_tp + lax.axis_index("tp")
     base = 0
     if load:
-        g_ref, *outs, x_vmem, s_vmem, sems = refs
+        *outs, x_vmem, sem = refs
         (j,) = planes
         width = plane * sub
         base = lax.bitwise_xor(index, jnp.int32(j * plane)) // plane * plane
-        copies = [
-            pltpu.make_async_copy(
-                x_ref.at[:, pl.ds(pl.multiple_of(base * sub, width), width)], x_vmem, sems.at[0]
-            ),
-            pltpu.make_async_copy(s_ref, s_vmem, sems.at[1]),
-        ]
-        for copy in copies:
-            copy.start()
-        for copy in copies:
-            copy.wait()
-        x_ref, s_ref = x_vmem, s_vmem
+        copy = pltpu.make_async_copy(
+            x_ref.at[:, pl.ds(pl.multiple_of(base * sub, width), width)], x_vmem, sem
+        )
+        copy.start()
         rows = x_vmem.shape[0]
+        blocks = s_ref.shape[0] - n_tp * rows
         for out in outs:
             for h in range(n_tp):
-                hd = g_ref.shape[1]
-                out[:, 2 * sub + h * hd:2 * sub + (h + 1) * hd] = g_ref[h * rows:(h + 1) * rows, :]
+                hd = s_ref.shape[1]
+                out[:, 2 * sub + h * hd:2 * sub + (h + 1) * hd] = s_ref[blocks + h * rows:blocks + (h + 1) * rows, :]
+        copy.wait()
+        x_ref, s_ref = x_vmem, s_ref.at[:blocks]
     else:
         outs = refs
     scales = s_ref[...]
@@ -68,23 +64,22 @@
 def pack(x, scales, n_tp, plane, planes, keys, core, sub, *load):
     rows = x.shape[0]
     extra = load[0].size // rows if load else 0
-    block = x.shape[1] // scales.shape[0]
+    block = x.shape[1] // (scales.shape[0] - (load[0].shape[0] if load else 0))
     outs = len(planes) * len(keys)
     scratch = [
         pltpu.VMEM((rows, plane * sub), x.dtype),
-        pltpu.VMEM(scales.shape, scales.dtype),
-        pltpu.SemaphoreType.DMA((2,)),
+        pltpu.SemaphoreType.DMA,
     ]
     return pl.pallas_call(
         functools.partial(pack_kernel, n_tp, plane, planes, keys, core, sub, block, bool(load)),
         out_shape=[jax.ShapeDtypeStruct((rows, 2 * sub + extra), jnp.bfloat16)] * outs,
-        in_specs=[pl.BlockSpec(memory_space=pltpu.HBM)] * 2 + [VMEM] if load else [VMEM] * 2,
+        in_specs=[pl.BlockSpec(memory_space=pltpu.HBM) if load else VMEM, VMEM],
         out_specs=[VMEM] * outs,
         scratch_shapes=scratch if load else [],
         compiler_params=params(FIRST_LIMIT) if load else params(),
         cost_estimate=cost(4 * rows * sub * outs, 8 * rows * sub * outs),
         name="pack",
-    )(x, scales, *load)
+    )(x, scales)
 
 
 def grads_kernel(n_tp, rows, hd, base, *refs):
@@ -134,20 +129,22 @@
     )(gt, *xs)
 
 
-def join_kernel(a, b, out):
-    out[...] = (a[...] + b[...]).astype(out.dtype)
-
-
-def join(a, b):
+def join_kernel(*refs):
+    *ins, out = refs
+    out[...] = sum(r[...].astype(jnp.float32) for r in ins).astype(out.dtype)
+
+
+def join(*parts):
+    a = parts[0]
     return pl.pallas_call(
         join_kernel,
         out_shape=jax.ShapeDtypeStruct(a.shape, jnp.bfloat16),
-        in_specs=[VMEM] * 2,
+        in_specs=[VMEM] * len(parts),
         out_specs=VMEM,
         compiler_params=params(),
         cost_estimate=cost(a.size, 10 * a.size),
         name="join",
-    )(a, b)
+    )(*parts)
 
 
 def total_kernel(*refs):
@@ -224,23 +221,24 @@
         return lax.ppermute(value, AXES, [(i, i ^ distance) for i in range(count)])
 
     order = list(range(depth - 1, -1, -1))
-    packed = pack(stash_values, scales, n_tp, plane, order[:1], keys, core, sub, value_grad)
+    packed = pack(stash_values, jnp.concatenate([scales, value_grad]), n_tp, plane, order[:1], keys, core, sub, value_grad)
     packed += pack(stash_values, scales, n_tp, plane, order[1:], keys, core, sub)
-    parts = []
+    passed = {}
     for n, j in enumerate(order):
         own, *away = packed[n * len(keys):(n + 1) * len(keys)]
         arrived = [own] + [send(v, k) for k, v in zip(keys[1:], away)]
         if n == 0:
             gt = grads(arrived, n_tp, value_grad.shape[1], 2 * sub)
         mine, theirs = matmul(gt, arrived, sub)
-        theirs = send(theirs, core)
+        terms = [mine, send(theirs, core)]
         if j:
-            parts.append(send(join(mine, theirs), j * plane))
+            low = j
+            terms += passed.pop(j, [])
+            value = join(*terms)
+            passed.setdefault(j ^ low, []).append(send(value, low * plane))
         else:
-            parts += [mine, theirs]
-    own, other, squares = totals(parts[::-1])
+            own, other, squares = totals(terms + passed.pop(0))
     other = send(other, 1)
-
     pieces = [squares]
     for group in [(core,), keys[1:], [j * plane for j in range(1, depth)]]:
         merged = sum(pieces[1:], pieces[0])

time: 66.6 us -> 65.9 us (0.989)
  local copies, waits for them, and re-layouts: 1.71 us -> 0.01 us
  other arithmetic: 0.01 us -> 1.01 us
    unnamed x6 -> x4, local copies, waits for them, and re-layouts: 1.71 us -> 0.01 us
    concatenate x0 -> x1, other arithmetic: none -> 1 us  [fast_body(): jnp.concatenate([scales, value_grad])]
  transfers between devices with their start and end apart: 27 -> 27, of which waited for: 14 -> 15; matrix products, arithmetic and copies ran while one was open for 0% -> 0% of each run, Pallas kernels for 3% -> 3%
where the time goes in v3:
time: 65.9 us; the launch traced here: 65.7 us
  starting transfers between devices  31.2 us (47%)
  waiting for transfers between devices  29 us (44%)
  Pallas kernels  4.34 us (7%)
  other arithmetic  1.01 us (2%)
    ppermute x27, starting transfers between devices, send(): return lax.ppermute(value, AXES, [(i, i ^ distance) for i in range(count)])  31.2 us
    ppermute x27, waiting for transfers between devices, send(): return lax.ppermute(value, AXES, [(i, i ^ distance) for i in range(count)])  29 us
    pallas_call x2, Pallas kernels, pack(): pl.pallas_call(functools.partial(pack_kernel, n_tp, plane, planes, keys,...  2.01 us
  transfers between devices with their start and end apart: 27, of which 15 were waited for; matrix products, arithmetic and copies ran while one was open for 0% of the time, Pallas kernels for 3%

profile of v3, /device:TPU:0, one launch (start us, length us, event | category | flops | bytes accessed | tf_op | source)
XLA Modules:
  0.0 65.7 jit_solution(11758243501680333848)
XLA Ops:
  0.0 1.0 %pad_maximum_fusion.s_ref = bf16[320,128]{1,0:T(8,128)(2,1)S(1)} fusion(bf16[256,128]{1,0:T(8,128)(2,1)} %param.5, bf16[64,128]{1,0:T(8,128)(2,1)} %bitcast.1), kind=kLoop, calls=%fused_computation | loop fusion | flops 163840 | bytes 163840 | tf_op jit(solution)/shard_map/concatenate | solution.py:224
  1.0 1.4 %pack.2 = (bf16[128,768]{1,0:T(8,128)(2,1)S(1)}, bf16[128,768]{1,0:T(8,128)(2,1)S(1)}, bf16[128,768]{1,0:T(8,128)(2,1)S(1)}, bf16[128,768]{1,0:T(8,128)(2,1)S(1)}) custom-call(bf16[128,8192]{1,0:T(8,128)(2,1)} %x_ref.3, bf16[320,128]{1,0:T(8,128)(2,1)S(1)} %pad_maximum_fusion.s_ref), custom_call_target="tpu_custom_call" | custom-call | flops 524288 | bytes 1048576 | tf_op jit(solution)/shard_map/pack/pallas_call | solution.py:73
  2.4 3.1 %collective-permute-start = (bf16[128,768]{1,0:T(8,128)(2,1)S(1)}, bf16[128,768]{1,0:T(8,128)(2,1)S(1)}, u32[]{:S(2)}, u32[]{:S(2)}) collective-permute-start(bf16[128,768]{1,0:T(8,128)(2,1)S(1)} %get-tuple-element.33), channel_id=1, source_target_pairs={{0,1},{1,0},{2,3},{3,2},{4,5},{5,4},{6,7},{7,6},{8,9},{9,8},{10,11... | collective-permute-start | bytes 589832 | tf_op jit(solution)/shard_map/ppermute | solution.py:221
  5.5 1.5 %collective-permute-start.1 = (bf16[128,768]{1,0:T(8,128)(2,1)S(1)}, bf16[128,768]{1,0:T(8,128)(2,1)S(1)}, u32[]{:S(2)}, u32[]{:S(2)}) collective-permute-start(bf16[128,768]{1,0:T(8,128)(2,1)S(1)} %get-tuple-element.34), channel_id=1, source_target_pairs={{0,4},{1,5},{2,6},{3,7},{4,0},{5,1},{6,2},{7,3},{8,12},{9,13},{10,... | collective-permute-start | bytes 589832 | tf_op jit(solution)/shard_map/ppermute | solution.py:221
  7.0 0.6 pack.3
  7.6 2.0 %collective-permute-start.14 = (bf16[128,512]{1,0:T(8,128)(2,1)S(1)}, bf16[128,512]{1,0:T(8,128)(2,1)S(1)}, u32[]{:S(2)}, u32[]{:S(2)}) collective-permute-start(bf16[128,512]{1,0:T(8,128)(2,1)S(1)} %get-tuple-element.51), channel_id=1, source_target_pairs={{0,1},{1,0},{2,3},{3,2},{4,5},{5,4},{6,7},{7,6},{8,9},{9,8},{10,11... | collective-permute-start | bytes 393224 | tf_op jit(solution)/shard_map/ppermute | solution.py:221
  9.6 1.5 %collective-permute-start.15 = (bf16[128,512]{1,0:T(8,128)(2,1)S(1)}, bf16[128,512]{1,0:T(8,128)(2,1)S(1)}, u32[]{:S(2)}, u32[]{:S(2)}) collective-permute-start(bf16[128,512]{1,0:T(8,128)(2,1)S(1)} %get-tuple-element.52), channel_id=1, source_target_pairs={{0,4},{1,5},{2,6},{3,7},{4,0},{5,1},{6,2},{7,3},{8,12},{9,13},{10,... | collective-permute-start | bytes 393224 | tf_op jit(solution)/shard_map/ppermute | solution.py:221
  11.1 6.3 %collective-permute-done.14.refs_1_ = bf16[128,512]{1,0:T(8,128)(2,1)S(1)} collective-permute-done((bf16[128,512]{1,0:T(8,128)(2,1)S(1)}, bf16[128,512]{1,0:T(8,128)(2,1)S(1)}, u32[]{:S(2)}, u32[]{:S(2)}) %collective-permute-start.14) | collective-permute-done | bytes 131104 | tf_op jit(solution)/shard_map/ppermute | solution.py:221
  17.4 2.7 %collective-permute-start.16 = (bf16[128,512]{1,0:T(8,128)(2,1)S(1)}, bf16[128,512]{1,0:T(8,128)(2,1)S(1)}, u32[]{:S(2)}, u32[]{:S(2)}) collective-permute-start(bf16[128,512]{1,0:T(8,128)(2,1)S(1)} %get-tuple-element.53), channel_id=1, source_target_pairs={{0,5},{1,4},{2,7},{3,6},{4,1},{5,0},{6,3},{7,2},{8,13},{9,12},{10,... | collective-permute-start | bytes 393224 | tf_op jit(solution)/shard_map/ppermute | solution.py:221
  20.9 2.7 %collective-permute-start.11 = (bf16[128,512]{1,0:T(8,128)(2,1)S(1)}, bf16[128,512]{1,0:T(8,128)(2,1)S(1)}, u32[]{:S(2)}, u32[]{:S(2)}) collective-permute-start(bf16[128,512]{1,0:T(8,128)(2,1)S(1)} %get-tuple-element.47), channel_id=1, source_target_pairs={{0,5},{1,4},{2,7},{3,6},{4,1},{5,0},{6,3},{7,2},{8,13},{9,12},{10,... | collective-permute-start | bytes 393224 | tf_op jit(solution)/shard_map/ppermute | solution.py:221
  24.5 2.0 %collective-permute-start.4 = (bf16[128,512]{1,0:T(8,128)(2,1)S(1)}, bf16[128,512]{1,0:T(8,128)(2,1)S(1)}, u32[]{:S(2)}, u32[]{:S(2)}) collective-permute-start(bf16[128,512]{1,0:T(8,128)(2,1)S(1)} %get-tuple-element.38), channel_id=1, source_target_pairs={{0,4},{1,5},{2,6},{3,7},{4,0},{5,1},{6,2},{7,3},{8,12},{9,13},{10,... | collective-permute-start | bytes 393224 | tf_op jit(solution)/shard_map/ppermute | solution.py:221
  26.8 1.7 %collective-permute-done.9.refs_1_ = bf16[128,512]{1,0:T(8,128)(2,1)S(1)} collective-permute-done((bf16[128,512]{1,0:T(8,128)(2,1)S(1)}, bf16[128,512]{1,0:T(8,128)(2,1)S(1)}, u32[]{:S(2)}, u32[]{:S(2)}) %collective-permute-start.9) | collective-permute-done | bytes 131104 | tf_op jit(solution)/shard_map/ppermute | solution.py:221
  28.5 1.0 %collective-permute-start.5 = (bf16[128,512]{1,0:T(8,128)(2,1)S(1)}, bf16[128,512]{1,0:T(8,128)(2,1)S(1)}, u32[]{:S(2)}, u32[]{:S(2)}) collective-permute-start(bf16[128,512]{1,0:T(8,128)(2,1)S(1)} %get-tuple-element.39), channel_id=1, source_target_pairs={{0,5},{1,4},{2,7},{3,6},{4,1},{5,0},{6,3},{7,2},{8,13},{9,12},{10,... | collective-permute-start | bytes 393224 | tf_op jit(solution)/shard_map/ppermute | solution.py:221
  29.5 1.3 %collective-permute-done.11.refs_3_ = bf16[128,512]{1,0:T(8,128)(2,1)S(1)} collective-permute-done((bf16[128,512]{1,0:T(8,128)(2,1)S(1)}, bf16[128,512]{1,0:T(8,128)(2,1)S(1)}, u32[]{:S(2)}, u32[]{:S(2)}) %collective-permute-start.11) | collective-permute-done | bytes 131104 | tf_op jit(solution)/shard_map/ppermute | solution.py:221
  31.1 1.1 %collective-permute-done.3.refs_1_ = bf16[128,512]{1,0:T(8,128)(2,1)S(1)} collective-permute-done((bf16[128,512]{1,0:T(8,128)(2,1)S(1)}, bf16[128,512]{1,0:T(8,128)(2,1)S(1)}, u32[]{:S(2)}, u32[]{:S(2)}) %collective-permute-start.3) | collective-permute-done | bytes 131104 | tf_op jit(solution)/shard_map/ppermute | solution.py:221
  32.4 2.1 %collective-permute-done.5.refs_3_ = bf16[128,512]{1,0:T(8,128)(2,1)S(1)} collective-permute-done((bf16[128,512]{1,0:T(8,128)(2,1)S(1)}, bf16[128,512]{1,0:T(8,128)(2,1)S(1)}, u32[]{:S(2)}, u32[]{:S(2)}) %collective-permute-start.5) | collective-permute-done | bytes 131104 | tf_op jit(solution)/shard_map/ppermute | solution.py:221
  34.9 4.0 %collective-permute-start.8 = (bf16[256,256]{1,0:T(8,128)(2,1)S(1)}, bf16[256,256]{1,0:T(8,128)(2,1)S(1)}, u32[]{:S(2)}, u32[]{:S(2)}) collective-permute-start(bf16[256,256]{1,0:T(8,128)(2,1)S(1)} %join.3), channel_id=1, source_target_pairs={{0,24},{1,25},{2,26},{3,27},{4,28},{5,29},{6,30},{7,31},{8,16},{9,... | collective-permute-start | bytes 393224 | tf_op jit(solution)/shard_map/ppermute | solution.py:221
  39.1 0.6 collective-permute-start.13
  39.7 3.6 %collective-permute-done.8.refs_2_ = bf16[256,256]{1,0:T(8,128)(2,1)S(1)} collective-permute-done((bf16[256,256]{1,0:T(8,128)(2,1)S(1)}, bf16[256,256]{1,0:T(8,128)(2,1)S(1)}, u32[]{:S(2)}, u32[]{:S(2)}) %collective-permute-start.8) | collective-permute-done | bytes 131104 | tf_op jit(solution)/shard_map/ppermute | solution.py:221
  43.3 3.7 %collective-permute-done.18.refs_4_ = bf16[256,256]{1,0:T(8,128)(2,1)S(1)} collective-permute-done((bf16[256,256]{1,0:T(8,128)(2,1)S(1)}, bf16[256,256]{1,0:T(8,128)(2,1)S(1)}, u32[]{:S(2)}, u32[]{:S(2)}) %collective-permute-start.18) | collective-permute-done | bytes 131104 | tf_op jit(solution)/shard_map/ppermute | solution.py:221
  47.0 3.7 %collective-permute-done.13.refs_3_ = bf16[256,256]{1,0:T(8,128)(2,1)S(1)} collective-permute-done((bf16[256,256]{1,0:T(8,128)(2,1)S(1)}, bf16[256,256]{1,0:T(8,128)(2,1)S(1)}, u32[]{:S(2)}, u32[]{:S(2)}) %collective-permute-start.13) | collective-permute-done | bytes 131104 | tf_op jit(solution)/shard_map/ppermute | solution.py:221
  50.8 1.2 %collective-permute-done.20 = f32[8,128]{1,0:T(8,128)S(1)} collective-permute-done((f32[8,128]{1,0:T(8,128)S(1)}, f32[8,128]{1,0:T(8,128)S(1)}, u32[]{:S(2)}, u32[]{:S(2)}) %collective-permute-start.20) | collective-permute-done | bytes 4128 | tf_op jit(solution)/shard_map/ppermute | solution.py:221
  52.0 1.4 %collective-permute-start.23 = (f32[8,128]{1,0:T(8,128)S(1)}, f32[8,128]{1,0:T(8,128)S(1)}, u32[]{:S(2)}, u32[]{:S(2)}) collective-permute-start(f32[8,128]{1,0:T(8,128)S(1)} %add.12), channel_id=1, source_target_pairs={{0,5},{1,4},{2,7},{3,6},{4,1},{5,0},{6,3},{7,2},{8,13},{9,12},{10,... | collective-permute-start | bytes 12296 | tf_op jit(solution)/shard_map/ppermute | solution.py:221
  53.4 0.8 %collective-permute-start.22 = (f32[8,128]{1,0:T(8,128)S(1)}, f32[8,128]{1,0:T(8,128)S(1)}, u32[]{:S(2)}, u32[]{:S(2)}) collective-permute-start(f32[8,128]{1,0:T(8,128)S(1)} %add.12), channel_id=1, source_target_pairs={{0,4},{1,5},{2,6},{3,7},{4,0},{5,1},{6,2},{7,3},{8,12},{9,13},{10,... | collective-permute-start | bytes 12296 | tf_op jit(solution)/shard_map/ppermute | solution.py:221
  54.2 1.3 %collective-permute-start.21 = (f32[8,128]{1,0:T(8,128)S(1)}, f32[8,128]{1,0:T(8,128)S(1)}, u32[]{:S(2)}, u32[]{:S(2)}) collective-permute-start(f32[8,128]{1,0:T(8,128)S(1)} %add.12), channel_id=1, source_target_pairs={{0,1},{1,0},{2,3},{3,2},{4,5},{5,4},{6,7},{7,6},{8,9},{9,8},{10,11... | collective-permute-start | bytes 12296 | tf_op jit(solution)/shard_map/ppermute | solution.py:221
  55.4 0.8 %collective-permute-start.19 = (f32[128,256]{1,0:T(8,128)S(1)}, f32[128,256]{1,0:T(8,128)S(1)}, u32[]{:S(2)}, u32[]{:S(2)}) collective-permute-start(f32[128,256]{1,0:T(8,128)S(1)} %get-tuple-element.57), channel_id=1, source_target_pairs={{0,1},{1,0},{2,3},{3,2},{4,5},{5,4},{6,7},{7,6},{8,9},{9,8},{10,11... | collective-permute-start | bytes 393224 | tf_op jit(solution)/shard_map/ppermute | solution.py:221
  57.0 0.8 %collective-permute-done.21 = f32[8,128]{1,0:T(8,128)S(1)} collective-permute-done((f32[8,128]{1,0:T(8,128)S(1)}, f32[8,128]{1,0:T(8,128)S(1)}, u32[]{:S(2)}, u32[]{:S(2)}) %collective-permute-start.21) | collective-permute-done | bytes 4128 | tf_op jit(solution)/shard_map/ppermute | solution.py:221
  57.8 2.5 %collective-permute-start.26 = (f32[8,128]{1,0:T(8,128)S(1)}, f32[8,128]{1,0:T(8,128)S(1)}, u32[]{:S(2)}, u32[]{:S(2)}) collective-permute-start(f32[8,128]{1,0:T(8,128)S(1)} %add_add_fusion.refs_0_), channel_id=1, source_target_pairs={{0,24},{1,25},{2,26},{3,27},{4,28},{5,29},{6,30},{7,31},{8,16},{9,... | collective-permute-start | bytes 12296 | tf_op jit(solution)/shard_map/ppermute | solution.py:221
  60.3 1.9 %collective-permute-start.24 = (f32[8,128]{1,0:T(8,128)S(1)}, f32[8,128]{1,0:T(8,128)S(1)}, u32[]{:S(2)}, u32[]{:S(2)}) collective-permute-start(f32[8,128]{1,0:T(8,128)S(1)} %add_add_fusion.refs_0_), channel_id=1, source_target_pairs={{0,8},{1,9},{2,10},{3,11},{4,12},{5,13},{6,14},{7,15},{8,0},{9,1},... | collective-permute-start | bytes 12296 | tf_op jit(solution)/shard_map/ppermute | solution.py:221
  62.2 1.0 %collective-permute-done.26.refs_3_ = f32[8,128]{1,0:T(8,128)S(1)} collective-permute-done((f32[8,128]{1,0:T(8,128)S(1)}, f32[8,128]{1,0:T(8,128)S(1)}, u32[]{:S(2)}, u32[]{:S(2)}) %collective-permute-start.26) | collective-permute-done | bytes 4128 | tf_op jit(solution)/shard_map/ppermute | solution.py:221
  63.2 1.6 %collective-permute-done.25.refs_2_ = f32[8,128]{1,0:T(8,128)S(1)} collective-permute-done((f32[8,128]{1,0:T(8,128)S(1)}, f32[8,128]{1,0:T(8,128)S(1)}, u32[]{:S(2)}, u32[]{:S(2)}) %collective-permute-start.25) | collective-permute-done | bytes 4128 | tf_op jit(solution)/shard_map/ppermute | solution.py:221
  64.8 0.9 %clip.1 = f32[512,128]{1,0:T(8,128)} custom-call(f32[128,256]{1,0:T(8,128)S(1)} %get-tuple-element.56.own, f32[128,256]{1,0:T(8,128)S(1)} %collective-permute-done.19.other, f32[8,128]{1,0:T(8,128)S(1)} %add_add_fusion.refs_0_, f32[8,128]{1,0:T(8,128)S(1)} %collective-permute-done.24.refs_1_, f32[8,128]{1,0:T(8,128)S(1)} %collective-permute-done.25.refs_2_, ...), custom_call_target="tpu_custom_call" | custom-call | flops 131072 | bytes 524288 | tf_op jit(solution)/shard_map/clip/pallas_call | solution.py:189
  (41 shorter events, 4.1 us)
Async XLA Ops:
  0.0 7.0 %copy-start.1 = (bf16[128,64]{0,1:T(8,128)(2,1)S(1)}, bf16[128,64]{0,1:T(8,128)(2,1)}, u32[]{:S(2)}) copy-start(bf16[128,64]{0,1:T(8,128)(2,1)} %param.4) | copy-start | bytes 49156
  0.0 7.0 %copy-start = (bf16[128,8192]{1,0:T(8,128)(2,1)S(1)}, bf16[128,8192]{1,0:T(8,128)(2,1)}, u32[]{:S(2)}) copy-start(bf16[128,8192]{1,0:T(8,128)(2,1)} %x_ref.3) | copy-start | bytes 6291460
  2.4 18.2 %collective-permute-start = (bf16[128,768]{1,0:T(8,128)(2,1)S(1)}, bf16[128,768]{1,0:T(8,128)(2,1)S(1)}, u32[]{:S(2)}, u32[]{:S(2)}) collective-permute-start(bf16[128,768]{1,0:T(8,128)(2,1)S(1)} %get-tuple-element.33), channel_id=1, source_target_pairs={{0,1},{1,0},{2,3},{3,2},{4,5},{5,4},{6,7},{7,6},{8,9},{9,8},{10,11... | collective-permute-start | bytes 589832 | tf_op jit(solution)/shard_map/ppermute | solution.py:221
  5.5 15.4 %collective-permute-start.1 = (bf16[128,768]{1,0:T(8,128)(2,1)S(1)}, bf16[128,768]{1,0:T(8,128)(2,1)S(1)}, u32[]{:S(2)}, u32[]{:S(2)}) collective-permute-start(bf16[128,768]{1,0:T(8,128)(2,1)S(1)} %get-tuple-element.34), channel_id=1, source_target_pairs={{0,4},{1,5},{2,6},{3,7},{4,0},{5,1},{6,2},{7,3},{8,12},{9,13},{10,... | collective-permute-start | bytes 589832 | tf_op jit(solution)/shard_map/ppermute | solution.py:221
  7.0 16.6 %collective-permute-start.2 = (bf16[128,768]{1,0:T(8,128)(2,1)S(1)}, bf16[128,768]{1,0:T(8,128)(2,1)S(1)}, u32[]{:S(2)}, u32[]{:S(2)}) collective-permute-start(bf16[128,768]{1,0:T(8,128)(2,1)S(1)} %get-tuple-element.35), channel_id=1, source_target_pairs={{0,5},{1,4},{2,7},{3,6},{4,1},{5,0},{6,3},{7,2},{8,13},{9,12},{10,... | collective-permute-start | bytes 589832 | tf_op jit(solution)/shard_map/ppermute | solution.py:221
  7.6 9.8 %collective-permute-start.14 = (bf16[128,512]{1,0:T(8,128)(2,1)S(1)}, bf16[128,512]{1,0:T(8,128)(2,1)S(1)}, u32[]{:S(2)}, u32[]{:S(2)}) collective-permute-start(bf16[128,512]{1,0:T(8,128)(2,1)S(1)} %get-tuple-element.51), channel_id=1, source_target_pairs={{0,1},{1,0},{2,3},{3,2},{4,5},{5,4},{6,7},{7,6},{8,9},{9,8},{10,11... | collective-permute-start | bytes 393224 | tf_op jit(solution)/shard_map/ppermute | solution.py:221
  9.6 10.4 %collective-permute-start.15 = (bf16[128,512]{1,0:T(8,128)(2,1)S(1)}, bf16[128,512]{1,0:T(8,128)(2,1)S(1)}, u32[]{:S(2)}, u32[]{:S(2)}) collective-permute-start(bf16[128,512]{1,0:T(8,128)(2,1)S(1)} %get-tuple-element.52), channel_id=1, source_target_pairs={{0,4},{1,5},{2,6},{3,7},{4,0},{5,1},{6,2},{7,3},{8,12},{9,13},{10,... | collective-permute-start | bytes 393224 | tf_op jit(solution)/shard_map/ppermute | solution.py:221
  17.4 7.1 %collective-permute-start.16 = (bf16[128,512]{1,0:T(8,128)(2,1)S(1)}, bf16[128,512]{1,0:T(8,128)(2,1)S(1)}, u32[]{:S(2)}, u32[]{:S(2)}) collective-permute-start(bf16[128,512]{1,0:T(8,128)(2,1)S(1)} %get-tuple-element.53), channel_id=1, source_target_pairs={{0,5},{1,4},{2,7},{3,6},{4,1},{5,0},{6,3},{7,2},{8,13},{9,12},{10,... | collective-permute-start | bytes 393224 | tf_op jit(solution)/shard_map/ppermute | solution.py:221
  20.1 8.4 %collective-permute-start.9 = (bf16[128,512]{1,0:T(8,128)(2,1)S(1)}, bf16[128,512]{1,0:T(8,128)(2,1)S(1)}, u32[]{:S(2)}, u32[]{:S(2)}) collective-permute-start(bf16[128,512]{1,0:T(8,128)(2,1)S(1)} %get-tuple-element.45), channel_id=1, source_target_pairs={{0,1},{1,0},{2,3},{3,2},{4,5},{5,4},{6,7},{7,6},{8,9},{9,8},{10,11... | collective-permute-start | bytes 393224 | tf_op jit(solution)/shard_map/ppermute | solution.py:221
  20.6 8.9 %collective-permute-start.10 = (bf16[128,512]{1,0:T(8,128)(2,1)S(1)}, bf16[128,512]{1,0:T(8,128)(2,1)S(1)}, u32[]{:S(2)}, u32[]{:S(2)}) collective-permute-start(bf16[128,512]{1,0:T(8,128)(2,1)S(1)} %get-tuple-element.46), channel_id=1, source_target_pairs={{0,4},{1,5},{2,6},{3,7},{4,0},{5,1},{6,2},{7,3},{8,12},{9,13},{10,... | collective-permute-start | bytes 393224 | tf_op jit(solution)/shard_map/ppermute | solution.py:221
  20.9 9.9 %collective-permute-start.11 = (bf16[128,512]{1,0:T(8,128)(2,1)S(1)}, bf16[128,512]{1,0:T(8,128)(2,1)S(1)}, u32[]{:S(2)}, u32[]{:S(2)}) collective-permute-start(bf16[128,512]{1,0:T(8,128)(2,1)S(1)} %get-tuple-element.47), channel_id=1, source_target_pairs={{0,5},{1,4},{2,7},{3,6},{4,1},{5,0},{6,3},{7,2},{8,13},{9,12},{10,... | collective-permute-start | bytes 393224 | tf_op jit(solution)/shard_map/ppermute | solution.py:221
  23.6 8.6 %collective-permute-start.3 = (bf16[128,512]{1,0:T(8,128)(2,1)S(1)}, bf16[128,512]{1,0:T(8,128)(2,1)S(1)}, u32[]{:S(2)}, u32[]{:S(2)}) collective-permute-start(bf16[128,512]{1,0:T(8,128)(2,1)S(1)} %get-tuple-element.37), channel_id=1, source_target_pairs={{0,1},{1,0},{2,3},{3,2},{4,5},{5,4},{6,7},{7,6},{8,9},{9,8},{10,11... | collective-permute-start | bytes 393224 | tf_op jit(solution)/shard_map/ppermute | solution.py:221
  24.5 7.9 %collective-permute-start.4 = (bf16[128,512]{1,0:T(8,128)(2,1)S(1)}, bf16[128,512]{1,0:T(8,128)(2,1)S(1)}, u32[]{:S(2)}, u32[]{:S(2)}) collective-permute-start(bf16[128,512]{1,0:T(8,128)(2,1)S(1)} %get-tuple-element.38), channel_id=1, source_target_pairs={{0,4},{1,5},{2,6},{3,7},{4,0},{5,1},{6,2},{7,3},{8,12},{9,13},{10,... | collective-permute-start | bytes 393224 | tf_op jit(solution)/shard_map/ppermute | solution.py:221
  28.5 6.0 %collective-permute-start.5 = (bf16[128,512]{1,0:T(8,128)(2,1)S(1)}, bf16[128,512]{1,0:T(8,128)(2,1)S(1)}, u32[]{:S(2)}, u32[]{:S(2)}) collective-permute-start(bf16[128,512]{1,0:T(8,128)(2,1)S(1)} %get-tuple-element.39), channel_id=1, source_target_pairs={{0,5},{1,4},{2,7},{3,6},{4,1},{5,0},{6,3},{7,2},{8,13},{9,12},{10,... | collective-permute-start | bytes 393224 | tf_op jit(solution)/shard_map/ppermute | solution.py:221
  29.5 5.4 %collective-permute-start.7 = (f32[256,256]{1,0:T(8,128)S(1)}, f32[256,256]{1,0:T(8,128)S(1)}, u32[]{:S(2)}, u32[]{:S(2)}) collective-permute-start(f32[256,256]{1,0:T(8,128)S(1)} %get-tuple-element.43), channel_id=1, source_target_pairs={{0,2},{1,3},{2,0},{3,1},{4,6},{5,7},{6,4},{7,5},{8,10},{9,11},{10,... | collective-permute-start | bytes 786440 | tf_op jit(solution)/shard_map/ppermute | solution.py:221
  30.8 8.1 %collective-permute-start.17 = (f32[256,256]{1,0:T(8,128)S(1)}, f32[256,256]{1,0:T(8,128)S(1)}, u32[]{:S(2)}, u32[]{:S(2)}) collective-permute-start(f32[256,256]{1,0:T(8,128)S(1)} %get-tuple-element.55), channel_id=1, source_target_pairs={{0,2},{1,3},{2,0},{3,1},{4,6},{5,7},{6,4},{7,5},{8,10},{9,11},{10,... | collective-permute-start | bytes 786440 | tf_op jit(solution)/shard_map/ppermute | solution.py:221
  32.2 6.8 %collective-permute-start.12 = (f32[256,256]{1,0:T(8,128)S(1)}, f32[256,256]{1,0:T(8,128)S(1)}, u32[]{:S(2)}, u32[]{:S(2)}) collective-permute-start(f32[256,256]{1,0:T(8,128)S(1)} %get-tuple-element.49), channel_id=1, source_target_pairs={{0,2},{1,3},{2,0},{3,1},{4,6},{5,7},{6,4},{7,5},{8,10},{9,11},{10,... | collective-permute-start | bytes 786440 | tf_op jit(solution)/shard_map/ppermute | solution.py:221
  34.8 4.9 %collective-permute-start.6 = (f32[256,256]{1,0:T(8,128)S(1)}, f32[256,256]{1,0:T(8,128)S(1)}, u32[]{:S(2)}, u32[]{:S(2)}) collective-permute-start(f32[256,256]{1,0:T(8,128)S(1)} %get-tuple-element.41), channel_id=1, source_target_pairs={{0,2},{1,3},{2,0},{3,1},{4,6},{5,7},{6,4},{7,5},{8,10},{9,11},{10,... | collective-permute-start | bytes 786440 | tf_op jit(solution)/shard_map/ppermute | solution.py:221
  34.9 8.4 %collective-permute-start.8 = (bf16[256,256]{1,0:T(8,128)(2,1)S(1)}, bf16[256,256]{1,0:T(8,128)(2,1)S(1)}, u32[]{:S(2)}, u32[]{:S(2)}) collective-permute-start(bf16[256,256]{1,0:T(8,128)(2,1)S(1)} %join.3), channel_id=1, source_target_pairs={{0,24},{1,25},{2,26},{3,27},{4,28},{5,29},{6,30},{7,31},{8,16},{9,... | collective-permute-start | bytes 393224 | tf_op jit(solution)/shard_map/ppermute | solution.py:221
  38.9 8.0 %collective-permute-start.18 = (bf16[256,256]{1,0:T(8,128)(2,1)S(1)}, bf16[256,256]{1,0:T(8,128)(2,1)S(1)}, u32[]{:S(2)}, u32[]{:S(2)}) collective-permute-start(bf16[256,256]{1,0:T(8,128)(2,1)S(1)} %join.5), channel_id=1, source_target_pairs={{0,8},{1,9},{2,10},{3,11},{4,12},{5,13},{6,14},{7,15},{8,0},{9,1},... | collective-permute-start | bytes 393224 | tf_op jit(solution)/shard_map/ppermute | solution.py:221
  39.1 11.6 %collective-permute-start.13 = (bf16[256,256]{1,0:T(8,128)(2,1)S(1)}, bf16[256,256]{1,0:T(8,128)(2,1)S(1)}, u32[]{:S(2)}, u32[]{:S(2)}) collective-permute-start(bf16[256,256]{1,0:T(8,128)(2,1)S(1)} %join.4), channel_id=1, source_target_pairs={{0,16},{1,17},{2,18},{3,19},{4,20},{5,21},{6,22},{7,23},{8,24},{9,... | collective-permute-start | bytes 393224 | tf_op jit(solution)/shard_map/ppermute | solution.py:221
  50.7 1.2 %collective-permute-start.20 = (f32[8,128]{1,0:T(8,128)S(1)}, f32[8,128]{1,0:T(8,128)S(1)}, u32[]{:S(2)}, u32[]{:S(2)}) collective-permute-start(f32[8,128]{1,0:T(8,128)S(1)} %get-tuple-element.58), channel_id=1, source_target_pairs={{0,2},{1,3},{2,0},{3,1},{4,6},{5,7},{6,4},{7,5},{8,10},{9,11},{10,... | collective-permute-start | bytes 12296 | tf_op jit(solution)/shard_map/ppermute | solution.py:221
  52.0 4.5 %collective-permute-start.23 = (f32[8,128]{1,0:T(8,128)S(1)}, f32[8,128]{1,0:T(8,128)S(1)}, u32[]{:S(2)}, u32[]{:S(2)}) collective-permute-start(f32[8,128]{1,0:T(8,128)S(1)} %add.12), channel_id=1, source_target_pairs={{0,5},{1,4},{2,7},{3,6},{4,1},{5,0},{6,3},{7,2},{8,13},{9,12},{10,... | collective-permute-start | bytes 12296 | tf_op jit(solution)/shard_map/ppermute | solution.py:221
  53.4 3.6 %collective-permute-start.22 = (f32[8,128]{1,0:T(8,128)S(1)}, f32[8,128]{1,0:T(8,128)S(1)}, u32[]{:S(2)}, u32[]{:S(2)}) collective-permute-start(f32[8,128]{1,0:T(8,128)S(1)} %add.12), channel_id=1, source_target_pairs={{0,4},{1,5},{2,6},{3,7},{4,0},{5,1},{6,2},{7,3},{8,12},{9,13},{10,... | collective-permute-start | bytes 12296 | tf_op jit(solution)/shard_map/ppermute | solution.py:221
  54.2 3.6 %collective-permute-start.21 = (f32[8,128]{1,0:T(8,128)S(1)}, f32[8,128]{1,0:T(8,128)S(1)}, u32[]{:S(2)}, u32[]{:S(2)}) collective-permute-start(f32[8,128]{1,0:T(8,128)S(1)} %add.12), channel_id=1, source_target_pairs={{0,1},{1,0},{2,3},{3,2},{4,5},{5,4},{6,7},{7,6},{8,9},{9,8},{10,11... | collective-permute-start | bytes 12296 | tf_op jit(solution)/shard_map/ppermute | solution.py:221
  55.4 9.4 %collective-permute-start.19 = (f32[128,256]{1,0:T(8,128)S(1)}, f32[128,256]{1,0:T(8,128)S(1)}, u32[]{:S(2)}, u32[]{:S(2)}) collective-permute-start(f32[128,256]{1,0:T(8,128)S(1)} %get-tuple-element.57), channel_id=1, source_target_pairs={{0,1},{1,0},{2,3},{3,2},{4,5},{5,4},{6,7},{7,6},{8,9},{9,8},{10,11... | collective-permute-start | bytes 393224 | tf_op jit(solution)/shard_map/ppermute | solution.py:221
  57.8 5.4 %collective-permute-start.26 = (f32[8,128]{1,0:T(8,128)S(1)}, f32[8,128]{1,0:T(8,128)S(1)}, u32[]{:S(2)}, u32[]{:S(2)}) collective-permute-start(f32[8,128]{1,0:T(8,128)S(1)} %add_add_fusion.refs_0_), channel_id=1, source_target_pairs={{0,24},{1,25},{2,26},{3,27},{4,28},{5,29},{6,30},{7,31},{8,16},{9,... | collective-permute-start | bytes 12296 | tf_op jit(solution)/shard_map/ppermute | solution.py:221
  60.3 4.5 %collective-permute-start.25 = (f32[8,128]{1,0:T(8,128)S(1)}, f32[8,128]{1,0:T(8,128)S(1)}, u32[]{:S(2)}, u32[]{:S(2)}) collective-permute-start(f32[8,128]{1,0:T(8,128)S(1)} %add_add_fusion.refs_0_), channel_id=1, source_target_pairs={{0,16},{1,17},{2,18},{3,19},{4,20},{5,21},{6,22},{7,23},{8,24},{9,... | collective-permute-start | bytes 12296 | tf_op jit(solution)/shard_map/ppermute | solution.py:221
  60.3 4.5 %collective-permute-start.24 = (f32[8,128]{1,0:T(8,128)S(1)}, f32[8,128]{1,0:T(8,128)S(1)}, u32[]{:S(2)}, u32[]{:S(2)}) collective-permute-start(f32[8,128]{1,0:T(8,128)S(1)} %add_add_fusion.refs_0_), channel_id=1, source_target_pairs={{0,8},{1,9},{2,10},{3,11},{4,12},{5,13},{6,14},{7,15},{8,0},{9,1},... | collective-permute-start | bytes 12296 | tf_op jit(solution)/shard_map/ppermute | solution.py:221

commit v4 on v3

--- a/solution.py
+++ b/solution.py
@@ -54,32 +54,58 @@
     scales = s_ref[...]
     for n, j in enumerate(planes):
         for m, key in enumerate(keys):
-            out = outs[n * len(keys) + m]
             for h in range(2):
                 part = lax.bitwise_xor(index, jnp.int32((j * plane + key) ^ (h * core)))
                 values = x_ref[:, pl.ds(pl.multiple_of((part - base) * sub, sub), sub)]
-                out[:, h * sub:(h + 1) * sub] = dequantize(values, scales, part * (sub // block), sub, block)
+                values = dequantize(values, scales, part * (sub // block), sub, block)
+                if load:
+                    outs[m][:, h * sub:(h + 1) * sub] = values
+                else:
+                    column = (n * len(keys) + m) * sub
+                    outs[h][:, column:column + sub] = values
 
 
 def pack(x, scales, n_tp, plane, planes, keys, core, sub, *load):
     rows = x.shape[0]
     extra = load[0].size // rows if load else 0
     block = x.shape[1] // (scales.shape[0] - (load[0].shape[0] if load else 0))
-    outs = len(planes) * len(keys)
+    outs = len(keys) if load else 2
+    width = 2 * sub + extra if load else len(planes) * len(keys) * sub
     scratch = [
         pltpu.VMEM((rows, plane * sub), x.dtype),
         pltpu.SemaphoreType.DMA,
     ]
     return pl.pallas_call(
         functools.partial(pack_kernel, n_tp, plane, planes, keys, core, sub, block, bool(load)),
-        out_shape=[jax.ShapeDtypeStruct((rows, 2 * sub + extra), jnp.bfloat16)] * outs,
+        out_shape=[jax.ShapeDtypeStruct((rows, width), jnp.bfloat16)] * outs,
         in_specs=[pl.BlockSpec(memory_space=pltpu.HBM) if load else VMEM, VMEM],
         out_specs=[VMEM] * outs,
         scratch_shapes=scratch if load else [],
         compiler_params=params(FIRST_LIMIT) if load else params(),
-        cost_estimate=cost(4 * rows * sub * outs, 8 * rows * sub * outs),
+        cost_estimate=cost(2 * rows * width * outs, 4 * rows * width * outs),
         name="pack",
     )(x, scales)
+
+
+def merge_kernel(own, theirs, *outs):
+    rows = own.shape[0]
+    sub = outs[0].shape[1]
+    for n, out in enumerate(outs):
+        out[:rows, :] = own[:, n * sub:(n + 1) * sub]
+        out[rows:, :] = theirs[:, n * sub:(n + 1) * sub]
+
+
+def merge(own, theirs, sub):
+    rows, width = own.shape
+    return pl.pallas_call(
+        merge_kernel,
+        out_shape=[jax.ShapeDtypeStruct((2 * rows, sub), own.dtype)] * (width // sub),
+        in_specs=[VMEM] * 2,
+        out_specs=[VMEM] * (width // sub),
+        compiler_params=params(),
+        cost_estimate=cost(own.size, 8 * own.size),
+        name="merge",
+    )(own, theirs)
 
 
 def grads_kernel(n_tp, rows, hd, base, *refs):
@@ -129,6 +155,31 @@
     )(gt, *xs)
 
 
+def product_kernel(gt_a, gt_b, *refs):
+    *ins, out = refs
+    rows = ins[0].shape[0] // 2
+    own = jnp.concatenate([r[:rows, :] for r in ins], axis=0)
+    theirs = jnp.concatenate([r[rows:, :] for r in ins], axis=0)
+    total = jnp.dot(gt_a[...], own, preferred_element_type=jnp.float32)
+    total += jnp.dot(gt_b[...], theirs, preferred_element_type=jnp.float32)
+    out[...] = total.astype(out.dtype)
+
+
+def product(gts, xs, dtype):
+    columns = gts[0].shape[0]
+    sub = xs[0].shape[1]
+    size = sum(x.size for x in xs)
+    return pl.pallas_call(
+        product_kernel,
+        out_shape=jax.ShapeDtypeStruct((columns, sub), dtype),
+        in_specs=[VMEM] * (2 + len(xs)),
+        out_specs=VMEM,
+        compiler_params=params(),
+        cost_estimate=cost(2 * columns * size, 2 * size),
+        name="product",
+    )(*gts, *xs)
+
+
 def join_kernel(*refs):
     *ins, out = refs
     out[...] = sum(r[...].astype(jnp.float32) for r in ins).astype(out.dtype)
@@ -221,23 +272,23 @@
         return lax.ppermute(value, AXES, [(i, i ^ distance) for i in range(count)])
 
     order = list(range(depth - 1, -1, -1))
-    packed = pack(stash_values, jnp.concatenate([scales, value_grad]), n_tp, plane, order[:1], keys, core, sub, value_grad)
-    packed += pack(stash_values, scales, n_tp, plane, order[1:], keys, core, sub)
-    passed = {}
+    joined = jnp.concatenate([scales, value_grad])
+    packed = pack(stash_values, joined, n_tp, plane, order[:1], keys, core, sub, value_grad)
+    mine, theirs = pack(stash_values, scales, n_tp, plane, order[1:], keys, core, sub)
+    packed += merge(mine, send(theirs, core), sub)
+    terms = []
     for n, j in enumerate(order):
         own, *away = packed[n * len(keys):(n + 1) * len(keys)]
         arrived = [own] + [send(v, k) for k, v in zip(keys[1:], away)]
         if n == 0:
             gt = grads(arrived, n_tp, value_grad.shape[1], 2 * sub)
-        mine, theirs = matmul(gt, arrived, sub)
-        terms = [mine, send(theirs, core)]
-        if j:
-            low = j
-            terms += passed.pop(j, [])
-            value = join(*terms)
-            passed.setdefault(j ^ low, []).append(send(value, low * plane))
+            mine, theirs = matmul(gt, arrived, sub)
+            value = join(mine, send(theirs, core))
+            gts = [gt, send(gt, core)]
         else:
-            own, other, squares = totals(terms + passed.pop(0))
+            value = product(gts, arrived, jnp.bfloat16 if j else jnp.float32)
+        terms.append(send(value, j * plane) if j else value)
+    own, other, squares = totals(terms[::-1])
     other = send(other, 1)
     pieces = [squares]
     for group in [(core,), keys[1:], [j * plane for j in range(1, depth)]]:

time: 65.9 us -> 61.8 us (0.938)
  waiting for transfers between devices: 29 us -> 20.3 us
  starting transfers between devices: 31.2 us -> 34.4 us
  local copies, waits for them, and re-layouts: 0.01 us -> 2.31 us
  other arithmetic: 1.01 us -> 0.01 us
    ppermute x27 -> x26, waiting for transfers between devices: 29 us -> 20.3 us  [send(): return lax.ppermute(value, AXES, [(i, i ^ distance) for i in range(count)])]
    ppermute x27 -> x26, starting transfers between devices: 31.2 us -> 34.4 us  [send(): return lax.ppermute(value, AXES, [(i, i ^ distance) for i in range(count)])]
    unnamed x4 -> x6, local copies, waits for them, and re-layouts: 0.01 us -> 2.31 us
    pallas_call x0 -> x4, Pallas kernels: none -> 1 us  [the longest x3 0.9 us: product(): pl.pallas_call(product_kernel, out_shape=jax.ShapeDtypeStruct((columns, s...]
    concatenate x1, other arithmetic: 1 us -> 0.01 us  [fast_body(): joined = jnp.concatenate([scales, value_grad])]
    pallas_call x4 -> x1, Pallas kernels: 1.17 us -> 0.3 us  [matmul(): pl.pallas_call(functools.partial(matmul_kernel, sub), out_shape=[jax.Shap...]
  transfers between devices with their start and end apart: 27 -> 26, of which waited for: 15 -> 11; matrix products, arithmetic and copies ran while one was open for 0% -> 0% of each run, Pallas kernels for 3% -> 5%
where the time goes in v4:
time: 61.8 us; the launch traced here: 61.5 us
  starting transfers between devices  34.4 us (56%)
  waiting for transfers between devices  20.3 us (33%)
  Pallas kernels  4.41 us (7%)
  local copies, waits for them, and re-layouts  2.31 us (4%)
    ppermute x26, starting transfers between devices, send(): return lax.ppermute(value, AXES, [(i, i ^ distance) for i in range(count)])  34.4 us
    ppermute x26, waiting for transfers between devices, send(): return lax.ppermute(value, AXES, [(i, i ^ distance) for i in range(count)])  20.3 us
    unnamed x6, local copies, waits for them, and re-layouts  2.31 us
    pallas_call x2, Pallas kernels, pack(): pl.pallas_call(functools.partial(pack_kernel, n_tp, plane, planes, keys,...  2.01 us
  transfers between devices with their start and end apart: 26, of which 11 were waited for; matrix products, arithmetic and copies ran while one was open for 0% of the time, Pallas kernels for 5%

profile of v4, /device:TPU:0, one launch (start us, length us, event | category | flops | bytes accessed | tf_op | source)
XLA Modules:
  0.0 61.5 jit_solution(2720927295637844286)
XLA Ops:
  0.0 1.6 %copy-done = bf16[128,8192]{1,0:T(8,128)(2,1)S(1)} copy-done((bf16[128,8192]{1,0:T(8,128)(2,1)S(1)}, bf16[128,8192]{1,0:T(8,128)(2,1)}, u32[]{:S(2)}) %copy-start) | copy-done | bytes 2097176
  1.6 0.7 %copy-done.1 = bf16[128,64]{0,1:T(8,128)(2,1)S(1)} copy-done((bf16[128,64]{0,1:T(8,128)(2,1)S(1)}, bf16[128,64]{0,1:T(8,128)(2,1)}, u32[]{:S(2)}) %copy-start.1) | copy-done | bytes 16408
  2.3 0.6 pack.3
  2.9 0.6 collective-permute-start.4
  3.5 1.4 %pack.2 = (bf16[128,768]{1,0:T(8,128)(2,1)S(1)}, bf16[128,768]{1,0:T(8,128)(2,1)S(1)}, bf16[128,768]{1,0:T(8,128)(2,1)S(1)}, bf16[128,768]{1,0:T(8,128)(2,1)S(1)}) custom-call(bf16[128,8192]{1,0:T(8,128)(2,1)} %x_ref.3, bf16[320,128]{1,0:T(8,128)(2,1)S(1)} %pad_maximum_fusion.s_ref), custom_call_target="tpu_custom_call" | custom-call | flops 786432 | bytes 1572864 | tf_op jit(solution)/shard_map/pack/pallas_call | solution.py:78
  4.9 2.7 %collective-permute-start = (bf16[128,768]{1,0:T(8,128)(2,1)S(1)}, bf16[128,768]{1,0:T(8,128)(2,1)S(1)}, u32[]{:S(2)}, u32[]{:S(2)}) collective-permute-start(bf16[128,768]{1,0:T(8,128)(2,1)S(1)} %get-tuple-element.29), channel_id=1, source_target_pairs={{0,1},{1,0},{2,3},{3,2},{4,5},{5,4},{6,7},{7,6},{8,9},{9,8},{10,11... | collective-permute-start | bytes 589832 | tf_op jit(solution)/shard_map/ppermute | solution.py:272
  7.6 1.5 %collective-permute-start.1 = (bf16[128,768]{1,0:T(8,128)(2,1)S(1)}, bf16[128,768]{1,0:T(8,128)(2,1)S(1)}, u32[]{:S(2)}, u32[]{:S(2)}) collective-permute-start(bf16[128,768]{1,0:T(8,128)(2,1)S(1)} %get-tuple-element.30), channel_id=1, source_target_pairs={{0,4},{1,5},{2,6},{3,7},{4,0},{5,1},{6,2},{7,3},{8,12},{9,13},{10,... | collective-permute-start | bytes 589832 | tf_op jit(solution)/shard_map/ppermute | solution.py:272
  9.2 3.9 %collective-permute-done.refs_1_ = bf16[128,768]{1,0:T(8,128)(2,1)S(1)} collective-permute-done((bf16[128,768]{1,0:T(8,128)(2,1)S(1)}, bf16[128,768]{1,0:T(8,128)(2,1)S(1)}, u32[]{:S(2)}, u32[]{:S(2)}) %collective-permute-start) | collective-permute-done | bytes 196640 | tf_op jit(solution)/shard_map/ppermute | solution.py:272
  13.1 2.4 %collective-permute-done.1.refs_2_ = bf16[128,768]{1,0:T(8,128)(2,1)S(1)} collective-permute-done((bf16[128,768]{1,0:T(8,128)(2,1)S(1)}, bf16[128,768]{1,0:T(8,128)(2,1)S(1)}, u32[]{:S(2)}, u32[]{:S(2)}) %collective-permute-start.1) | collective-permute-done | bytes 196640 | tf_op jit(solution)/shard_map/ppermute | solution.py:272
  15.4 3.1 %collective-permute-done.2.refs_3_ = bf16[128,768]{1,0:T(8,128)(2,1)S(1)} collective-permute-done((bf16[128,768]{1,0:T(8,128)(2,1)S(1)}, bf16[128,768]{1,0:T(8,128)(2,1)S(1)}, u32[]{:S(2)}, u32[]{:S(2)}) %collective-permute-start.2) | collective-permute-done | bytes 196640 | tf_op jit(solution)/shard_map/ppermute | solution.py:272
  19.6 1.7 %collective-permute-start.8 = (bf16[256,256]{1,0:T(8,128)(2,1)S(1)}, bf16[256,256]{1,0:T(8,128)(2,1)S(1)}, u32[]{:S(2)}, u32[]{:S(2)}) collective-permute-start(bf16[256,256]{1,0:T(8,128)(2,1)S(1)} %get-tuple-element.39), channel_id=1, source_target_pairs={{0,1},{1,0},{2,3},{3,2},{4,5},{5,4},{6,7},{7,6},{8,9},{9,8},{10,11... | collective-permute-start | bytes 393224 | tf_op jit(solution)/shard_map/ppermute | solution.py:272
  21.4 1.5 %collective-permute-start.9 = (bf16[256,256]{1,0:T(8,128)(2,1)S(1)}, bf16[256,256]{1,0:T(8,128)(2,1)S(1)}, u32[]{:S(2)}, u32[]{:S(2)}) collective-permute-start(bf16[256,256]{1,0:T(8,128)(2,1)S(1)} %get-tuple-element.40), channel_id=1, source_target_pairs={{0,4},{1,5},{2,6},{3,7},{4,0},{5,1},{6,2},{7,3},{8,12},{9,13},{10,... | collective-permute-start | bytes 393224 | tf_op jit(solution)/shard_map/ppermute | solution.py:272
  23.2 1.7 %collective-permute-start.12 = (bf16[256,256]{1,0:T(8,128)(2,1)S(1)}, bf16[256,256]{1,0:T(8,128)(2,1)S(1)}, u32[]{:S(2)}, u32[]{:S(2)}) collective-permute-start(bf16[256,256]{1,0:T(8,128)(2,1)S(1)} %get-tuple-element.43), channel_id=1, source_target_pairs={{0,1},{1,0},{2,3},{3,2},{4,5},{5,4},{6,7},{7,6},{8,9},{9,8},{10,11... | collective-permute-start | bytes 393224 | tf_op jit(solution)/shard_map/ppermute | solution.py:272
  24.9 1.5 %collective-permute-start.13 = (bf16[256,256]{1,0:T(8,128)(2,1)S(1)}, bf16[256,256]{1,0:T(8,128)(2,1)S(1)}, u32[]{:S(2)}, u32[]{:S(2)}) collective-permute-start(bf16[256,256]{1,0:T(8,128)(2,1)S(1)} %get-tuple-element.44), channel_id=1, source_target_pairs={{0,4},{1,5},{2,6},{3,7},{4,0},{5,1},{6,2},{7,3},{8,12},{9,13},{10,... | collective-permute-start | bytes 393224 | tf_op jit(solution)/shard_map/ppermute | solution.py:272
  26.4 1.7 %collective-permute-start.14 = (bf16[256,256]{1,0:T(8,128)(2,1)S(1)}, bf16[256,256]{1,0:T(8,128)(2,1)S(1)}, u32[]{:S(2)}, u32[]{:S(2)}) collective-permute-start(bf16[256,256]{1,0:T(8,128)(2,1)S(1)} %get-tuple-element.45), channel_id=1, source_target_pairs={{0,5},{1,4},{2,7},{3,6},{4,1},{5,0},{6,3},{7,2},{8,13},{9,12},{10,... | collective-permute-start | bytes 393224 | tf_op jit(solution)/shard_map/ppermute | solution.py:272
  28.6 1.6 %collective-permute-done.10.refs_3_ = bf16[256,256]{1,0:T(8,128)(2,1)S(1)} collective-permute-done((bf16[256,256]{1,0:T(8,128)(2,1)S(1)}, bf16[256,256]{1,0:T(8,128)(2,1)S(1)}, u32[]{:S(2)}, u32[]{:S(2)}) %collective-permute-start.10) | collective-permute-done | bytes 131104 | tf_op jit(solution)/shard_map/ppermute | solution.py:272
  30.2 3.6 %collective-permute-start.17 = (bf16[256,256]{1,0:T(8,128)(2,1)S(1)}, bf16[256,256]{1,0:T(8,128)(2,1)S(1)}, u32[]{:S(2)}, u32[]{:S(2)}) collective-permute-start(bf16[256,256]{1,0:T(8,128)(2,1)S(1)} %join.1), channel_id=1, source_target_pairs={{0,24},{1,25},{2,26},{3,27},{4,28},{5,29},{6,30},{7,31},{8,16},{9,... | collective-permute-start | bytes 393224 | tf_op jit(solution)/shard_map/ppermute | solution.py:272
  34.1 1.9 %collective-permute-start.6 = (bf16[256,256]{1,0:T(8,128)(2,1)S(1)}, bf16[256,256]{1,0:T(8,128)(2,1)S(1)}, u32[]{:S(2)}, u32[]{:S(2)}) collective-permute-start(bf16[256,256]{1,0:T(8,128)(2,1)S(1)} %get-tuple-element.36), channel_id=1, source_target_pairs={{0,4},{1,5},{2,6},{3,7},{4,0},{5,1},{6,2},{7,3},{8,12},{9,13},{10,... | collective-permute-start | bytes 393224 | tf_op jit(solution)/shard_map/ppermute | solution.py:272
  36.0 1.5 %collective-permute-start.7 = (bf16[256,256]{1,0:T(8,128)(2,1)S(1)}, bf16[256,256]{1,0:T(8,128)(2,1)S(1)}, u32[]{:S(2)}, u32[]{:S(2)}) collective-permute-start(bf16[256,256]{1,0:T(8,128)(2,1)S(1)} %get-tuple-element.37), channel_id=1, source_target_pairs={{0,5},{1,4},{2,7},{3,6},{4,1},{5,0},{6,3},{7,2},{8,13},{9,12},{10,... | collective-permute-start | bytes 393224 | tf_op jit(solution)/shard_map/ppermute | solution.py:272
  37.8 2.6 %collective-permute-start.15 = (bf16[256,256]{1,0:T(8,128)(2,1)S(1)}, bf16[256,256]{1,0:T(8,128)(2,1)S(1)}, u32[]{:S(2)}, u32[]{:S(2)}) collective-permute-start(bf16[256,256]{1,0:T(8,128)(2,1)S(1)} %product.5), channel_id=1, source_target_pairs={{0,16},{1,17},{2,18},{3,19},{4,20},{5,21},{6,22},{7,23},{8,24},{9,... | collective-permute-start | bytes 393224 | tf_op jit(solution)/shard_map/ppermute | solution.py:272
  40.4 1.5 %collective-permute-done.7.refs_3_ = bf16[256,256]{1,0:T(8,128)(2,1)S(1)} collective-permute-done((bf16[256,256]{1,0:T(8,128)(2,1)S(1)}, bf16[256,256]{1,0:T(8,128)(2,1)S(1)}, u32[]{:S(2)}, u32[]{:S(2)}) %collective-permute-start.7) | collective-permute-done | bytes 131104 | tf_op jit(solution)/shard_map/ppermute | solution.py:272
  42.2 2.1 %collective-permute-done.11.refs_1_ = bf16[256,256]{1,0:T(8,128)(2,1)S(1)} collective-permute-done((bf16[256,256]{1,0:T(8,128)(2,1)S(1)}, bf16[256,256]{1,0:T(8,128)(2,1)S(1)}, u32[]{:S(2)}, u32[]{:S(2)}) %collective-permute-start.11) | collective-permute-done | bytes 131104 | tf_op jit(solution)/shard_map/ppermute | solution.py:272
  44.5 1.2 %collective-permute-done.19 = f32[8,128]{1,0:T(8,128)S(1)} collective-permute-done((f32[8,128]{1,0:T(8,128)S(1)}, f32[8,128]{1,0:T(8,128)S(1)}, u32[]{:S(2)}, u32[]{:S(2)}) %collective-permute-start.19) | collective-permute-done | bytes 4128 | tf_op jit(solution)/shard_map/ppermute | solution.py:272
  45.6 3.5 %collective-permute-start.22 = (f32[8,128]{1,0:T(8,128)S(1)}, f32[8,128]{1,0:T(8,128)S(1)}, u32[]{:S(2)}, u32[]{:S(2)}) collective-permute-start(f32[8,128]{1,0:T(8,128)S(1)} %add.12), channel_id=1, source_target_pairs={{0,5},{1,4},{2,7},{3,6},{4,1},{5,0},{6,3},{7,2},{8,13},{9,12},{10,... | collective-permute-start | bytes 12296 | tf_op jit(solution)/shard_map/ppermute | solution.py:272
  49.7 2.0 %collective-permute-start.18 = (f32[128,256]{1,0:T(8,128)S(1)}, f32[128,256]{1,0:T(8,128)S(1)}, u32[]{:S(2)}, u32[]{:S(2)}) collective-permute-start(f32[128,256]{1,0:T(8,128)S(1)} %get-tuple-element.49), channel_id=1, source_target_pairs={{0,1},{1,0},{2,3},{3,2},{4,5},{5,4},{6,7},{7,6},{8,9},{9,8},{10,11... | collective-permute-start | bytes 393224 | tf_op jit(solution)/shard_map/ppermute | solution.py:272
  51.7 1.0 %collective-permute-done.21 = f32[8,128]{1,0:T(8,128)S(1)} collective-permute-done((f32[8,128]{1,0:T(8,128)S(1)}, f32[8,128]{1,0:T(8,128)S(1)}, u32[]{:S(2)}, u32[]{:S(2)}) %collective-permute-start.21) | collective-permute-done | bytes 4128 | tf_op jit(solution)/shard_map/ppermute | solution.py:272
  52.7 0.6 collective-permute-done.20
  53.3 2.9 %collective-permute-start.25 = (f32[8,128]{1,0:T(8,128)S(1)}, f32[8,128]{1,0:T(8,128)S(1)}, u32[]{:S(2)}, u32[]{:S(2)}) collective-permute-start(f32[8,128]{1,0:T(8,128)S(1)} %add_add_fusion.refs_0_), channel_id=1, source_target_pairs={{0,24},{1,25},{2,26},{3,27},{4,28},{5,29},{6,30},{7,31},{8,16},{9,... | collective-permute-start | bytes 12296 | tf_op jit(solution)/shard_map/ppermute | solution.py:272
  56.2 1.5 %collective-permute-start.23 = (f32[8,128]{1,0:T(8,128)S(1)}, f32[8,128]{1,0:T(8,128)S(1)}, u32[]{:S(2)}, u32[]{:S(2)}) collective-permute-start(f32[8,128]{1,0:T(8,128)S(1)} %add_add_fusion.refs_0_), channel_id=1, source_target_pairs={{0,8},{1,9},{2,10},{3,11},{4,12},{5,13},{6,14},{7,15},{8,0},{9,1},... | collective-permute-start | bytes 12296 | tf_op jit(solution)/shard_map/ppermute | solution.py:272
  57.7 1.0 %collective-permute-done.25.refs_3_ = f32[8,128]{1,0:T(8,128)S(1)} collective-permute-done((f32[8,128]{1,0:T(8,128)S(1)}, f32[8,128]{1,0:T(8,128)S(1)}, u32[]{:S(2)}, u32[]{:S(2)}) %collective-permute-start.25) | collective-permute-done | bytes 4128 | tf_op jit(solution)/shard_map/ppermute | solution.py:272
  58.7 2.0 %collective-permute-done.24.refs_2_ = f32[8,128]{1,0:T(8,128)S(1)} collective-permute-done((f32[8,128]{1,0:T(8,128)S(1)}, f32[8,128]{1,0:T(8,128)S(1)}, u32[]{:S(2)}, u32[]{:S(2)}) %collective-permute-start.24) | collective-permute-done | bytes 4128 | tf_op jit(solution)/shard_map/ppermute | solution.py:272
  60.7 0.9 %clip.1 = f32[512,128]{1,0:T(8,128)} custom-call(f32[128,256]{1,0:T(8,128)S(1)} %get-tuple-element.48.own, f32[128,256]{1,0:T(8,128)S(1)} %collective-permute-done.18.other, f32[8,128]{1,0:T(8,128)S(1)} %add_add_fusion.refs_0_, f32[8,128]{1,0:T(8,128)S(1)} %collective-permute-done.23.refs_1_, f32[8,128]{1,0:T(8,128)S(1)} %collective-permute-done.24.refs_2_, ...), custom_call_target="tpu_custom_call" | custom-call | flops 131072 | bytes 524288 | tf_op jit(solution)/shard_map/clip/pallas_call | solution.py:240
  (40 shorter events, 3.7 us)
Async XLA Ops:
  0.0 1.6 %copy-start = (bf16[128,8192]{1,0:T(8,128)(2,1)S(1)}, bf16[128,8192]{1,0:T(8,128)(2,1)}, u32[]{:S(2)}) copy-start(bf16[128,8192]{1,0:T(8,128)(2,1)} %x_ref.3) | copy-start | bytes 6291460
  1.6 0.7 %copy-start.1 = (bf16[128,64]{0,1:T(8,128)(2,1)S(1)}, bf16[128,64]{0,1:T(8,128)(2,1)}, u32[]{:S(2)}) copy-start(bf16[128,64]{0,1:T(8,128)(2,1)} %param.4) | copy-start | bytes 49156
  2.3 1.2 %copy-start.2 = (bf16[256,128]{1,0:T(8,128)(2,1)S(1)}, bf16[256,128]{1,0:T(8,128)(2,1)}, u32[]{:S(2)}) copy-start(bf16[256,128]{1,0:T(8,128)(2,1)} %param.5) | copy-start | bytes 196612
  2.9 16.6 %collective-permute-start.4 = (bf16[128,3072]{1,0:T(8,128)(2,1)S(1)}, bf16[128,3072]{1,0:T(8,128)(2,1)S(1)}, u32[]{:S(2)}, u32[]{:S(2)}) collective-permute-start(bf16[128,3072]{1,0:T(8,128)(2,1)S(1)} %get-tuple-element.33), channel_id=1, source_target_pairs={{0,2},{1,3},{2,0},{3,1},{4,6},{5,7},{6,4},{7,5},{8,10},{9,11},{10,... | collective-permute-start | bytes 2359304 | tf_op jit(solution)/shard_map/ppermute | solution.py:272
  4.9 8.1 %collective-permute-start = (bf16[128,768]{1,0:T(8,128)(2,1)S(1)}, bf16[128,768]{1,0:T(8,128)(2,1)S(1)}, u32[]{:S(2)}, u32[]{:S(2)}) collective-permute-start(bf16[128,768]{1,0:T(8,128)(2,1)S(1)} %get-tuple-element.29), channel_id=1, source_target_pairs={{0,1},{1,0},{2,3},{3,2},{4,5},{5,4},{6,7},{7,6},{8,9},{9,8},{10,11... | collective-permute-start | bytes 589832 | tf_op jit(solution)/shard_map/ppermute | solution.py:272
  7.6 7.8 %collective-permute-start.1 = (bf16[128,768]{1,0:T(8,128)(2,1)S(1)}, bf16[128,768]{1,0:T(8,128)(2,1)S(1)}, u32[]{:S(2)}, u32[]{:S(2)}) collective-permute-start(bf16[128,768]{1,0:T(8,128)(2,1)S(1)} %get-tuple-element.30), channel_id=1, source_target_pairs={{0,4},{1,5},{2,6},{3,7},{4,0},{5,1},{6,2},{7,3},{8,12},{9,13},{10,... | collective-permute-start | bytes 589832 | tf_op jit(solution)/shard_map/ppermute | solution.py:272
  9.1 9.4 %collective-permute-start.2 = (bf16[128,768]{1,0:T(8,128)(2,1)S(1)}, bf16[128,768]{1,0:T(8,128)(2,1)S(1)}, u32[]{:S(2)}, u32[]{:S(2)}) collective-permute-start(bf16[128,768]{1,0:T(8,128)(2,1)S(1)} %get-tuple-element.31), channel_id=1, source_target_pairs={{0,5},{1,4},{2,7},{3,6},{4,1},{5,0},{6,3},{7,2},{8,13},{9,12},{10,... | collective-permute-start | bytes 589832 | tf_op jit(solution)/shard_map/ppermute | solution.py:272
  19.0 4.2 %collective-permute-start.16 = (f32[256,256]{1,0:T(8,128)S(1)}, f32[256,256]{1,0:T(8,128)S(1)}, u32[]{:S(2)}, u32[]{:S(2)}) collective-permute-start(f32[256,256]{1,0:T(8,128)S(1)} %get-tuple-element.47), channel_id=1, source_target_pairs={{0,2},{1,3},{2,0},{3,1},{4,6},{5,7},{6,4},{7,5},{8,10},{9,11},{10,... | collective-permute-start | bytes 786440 | tf_op jit(solution)/shard_map/ppermute | solution.py:272
  19.0 5.8 %collective-permute-start.3 = (bf16[256,512]{1,0:T(8,128)(2,1)S(1)}, bf16[256,512]{1,0:T(8,128)(2,1)S(1)}, u32[]{:S(2)}, u32[]{:S(2)}) collective-permute-start(bf16[256,512]{1,0:T(8,128)(2,1)S(1)} %grads.1.gt_a.gt_ref), channel_id=1, source_target_pairs={{0,2},{1,3},{2,0},{3,1},{4,6},{5,7},{6,4},{7,5},{8,10},{9,11},{10,... | collective-permute-start | bytes 786440 | tf_op jit(solution)/shard_map/ppermute | solution.py:272
  19.6 6.7 %collective-permute-start.8 = (bf16[256,256]{1,0:T(8,128)(2,1)S(1)}, bf16[256,256]{1,0:T(8,128)(2,1)S(1)}, u32[]{:S(2)}, u32[]{:S(2)}) collective-permute-start(bf16[256,256]{1,0:T(8,128)(2,1)S(1)} %get-tuple-element.39), channel_id=1, source_target_pairs={{0,1},{1,0},{2,3},{3,2},{4,5},{5,4},{6,7},{7,6},{8,9},{9,8},{10,11... | collective-permute-start | bytes 393224 | tf_op jit(solution)/shard_map/ppermute | solution.py:272
  21.4 6.7 %collective-permute-start.9 = (bf16[256,256]{1,0:T(8,128)(2,1)S(1)}, bf16[256,256]{1,0:T(8,128)(2,1)S(1)}, u32[]{:S(2)}, u32[]{:S(2)}) collective-permute-start(bf16[256,256]{1,0:T(8,128)(2,1)S(1)} %get-tuple-element.40), channel_id=1, source_target_pairs={{0,4},{1,5},{2,6},{3,7},{4,0},{5,1},{6,2},{7,3},{8,12},{9,13},{10,... | collective-permute-start | bytes 393224 | tf_op jit(solution)/shard_map/ppermute | solution.py:272
  22.9 7.3 %collective-permute-start.10 = (bf16[256,256]{1,0:T(8,128)(2,1)S(1)}, bf16[256,256]{1,0:T(8,128)(2,1)S(1)}, u32[]{:S(2)}, u32[]{:S(2)}) collective-permute-start(bf16[256,256]{1,0:T(8,128)(2,1)S(1)} %get-tuple-element.41), channel_id=1, source_target_pairs={{0,5},{1,4},{2,7},{3,6},{4,1},{5,0},{6,3},{7,2},{8,13},{9,12},{10,... | collective-permute-start | bytes 393224 | tf_op jit(solution)/shard_map/ppermute | solution.py:272
  23.2 10.9 %collective-permute-start.12 = (bf16[256,256]{1,0:T(8,128)(2,1)S(1)}, bf16[256,256]{1,0:T(8,128)(2,1)S(1)}, u32[]{:S(2)}, u32[]{:S(2)}) collective-permute-start(bf16[256,256]{1,0:T(8,128)(2,1)S(1)} %get-tuple-element.43), channel_id=1, source_target_pairs={{0,1},{1,0},{2,3},{3,2},{4,5},{5,4},{6,7},{7,6},{8,9},{9,8},{10,11... | collective-permute-start | bytes 393224 | tf_op jit(solution)/shard_map/ppermute | solution.py:272
  24.9 11.1 %collective-permute-start.13 = (bf16[256,256]{1,0:T(8,128)(2,1)S(1)}, bf16[256,256]{1,0:T(8,128)(2,1)S(1)}, u32[]{:S(2)}, u32[]{:S(2)}) collective-permute-start(bf16[256,256]{1,0:T(8,128)(2,1)S(1)} %get-tuple-element.44), channel_id=1, source_target_pairs={{0,4},{1,5},{2,6},{3,7},{4,0},{5,1},{6,2},{7,3},{8,12},{9,13},{10,... | collective-permute-start | bytes 393224 | tf_op jit(solution)/shard_map/ppermute | solution.py:272
  26.4 11.1 %collective-permute-start.14 = (bf16[256,256]{1,0:T(8,128)(2,1)S(1)}, bf16[256,256]{1,0:T(8,128)(2,1)S(1)}, u32[]{:S(2)}, u32[]{:S(2)}) collective-permute-start(bf16[256,256]{1,0:T(8,128)(2,1)S(1)} %get-tuple-element.45), channel_id=1, source_target_pairs={{0,5},{1,4},{2,7},{3,6},{4,1},{5,0},{6,3},{7,2},{8,13},{9,12},{10,... | collective-permute-start | bytes 393224 | tf_op jit(solution)/shard_map/ppermute | solution.py:272
  28.1 9.7 %collective-permute-start.5 = (bf16[256,256]{1,0:T(8,128)(2,1)S(1)}, bf16[256,256]{1,0:T(8,128)(2,1)S(1)}, u32[]{:S(2)}, u32[]{:S(2)}) collective-permute-start(bf16[256,256]{1,0:T(8,128)(2,1)S(1)} %get-tuple-element.35), channel_id=1, source_target_pairs={{0,1},{1,0},{2,3},{3,2},{4,5},{5,4},{6,7},{7,6},{8,9},{9,8},{10,11... | collective-permute-start | bytes 393224 | tf_op jit(solution)/shard_map/ppermute | solution.py:272
  30.2 12.0 %collective-permute-start.17 = (bf16[256,256]{1,0:T(8,128)(2,1)S(1)}, bf16[256,256]{1,0:T(8,128)(2,1)S(1)}, u32[]{:S(2)}, u32[]{:S(2)}) collective-permute-start(bf16[256,256]{1,0:T(8,128)(2,1)S(1)} %join.1), channel_id=1, source_target_pairs={{0,24},{1,25},{2,26},{3,27},{4,28},{5,29},{6,30},{7,31},{8,16},{9,... | collective-permute-start | bytes 393224 | tf_op jit(solution)/shard_map/ppermute | solution.py:272
  34.1 6.3 %collective-permute-start.6 = (bf16[256,256]{1,0:T(8,128)(2,1)S(1)}, bf16[256,256]{1,0:T(8,128)(2,1)S(1)}, u32[]{:S(2)}, u32[]{:S(2)}) collective-permute-start(bf16[256,256]{1,0:T(8,128)(2,1)S(1)} %get-tuple-element.36), channel_id=1, source_target_pairs={{0,4},{1,5},{2,6},{3,7},{4,0},{5,1},{6,2},{7,3},{8,12},{9,13},{10,... | collective-permute-start | bytes 393224 | tf_op jit(solution)/shard_map/ppermute | solution.py:272
  36.0 5.9 %collective-permute-start.7 = (bf16[256,256]{1,0:T(8,128)(2,1)S(1)}, bf16[256,256]{1,0:T(8,128)(2,1)S(1)}, u32[]{:S(2)}, u32[]{:S(2)}) collective-permute-start(bf16[256,256]{1,0:T(8,128)(2,1)S(1)} %get-tuple-element.37), channel_id=1, source_target_pairs={{0,5},{1,4},{2,7},{3,6},{4,1},{5,0},{6,3},{7,2},{8,13},{9,12},{10,... | collective-permute-start | bytes 393224 | tf_op jit(solution)/shard_map/ppermute | solution.py:272
  37.5 6.8 %collective-permute-start.11 = (bf16[256,256]{1,0:T(8,128)(2,1)S(1)}, bf16[256,256]{1,0:T(8,128)(2,1)S(1)}, u32[]{:S(2)}, u32[]{:S(2)}) collective-permute-start(bf16[256,256]{1,0:T(8,128)(2,1)S(1)} %product.4), channel_id=1, source_target_pairs={{0,8},{1,9},{2,10},{3,11},{4,12},{5,13},{6,14},{7,15},{8,0},{9,1},... | collective-permute-start | bytes 393224 | tf_op jit(solution)/shard_map/ppermute | solution.py:272
  37.8 6.5 %collective-permute-start.15 = (bf16[256,256]{1,0:T(8,128)(2,1)S(1)}, bf16[256,256]{1,0:T(8,128)(2,1)S(1)}, u32[]{:S(2)}, u32[]{:S(2)}) collective-permute-start(bf16[256,256]{1,0:T(8,128)(2,1)S(1)} %product.5), channel_id=1, source_target_pairs={{0,16},{1,17},{2,18},{3,19},{4,20},{5,21},{6,22},{7,23},{8,24},{9,... | collective-permute-start | bytes 393224 | tf_op jit(solution)/shard_map/ppermute | solution.py:272
  44.4 1.2 %collective-permute-start.19 = (f32[8,128]{1,0:T(8,128)S(1)}, f32[8,128]{1,0:T(8,128)S(1)}, u32[]{:S(2)}, u32[]{:S(2)}) collective-permute-start(f32[8,128]{1,0:T(8,128)S(1)} %get-tuple-element.50), channel_id=1, source_target_pairs={{0,2},{1,3},{2,0},{3,1},{4,6},{5,7},{6,4},{7,5},{8,10},{9,11},{10,... | collective-permute-start | bytes 12296 | tf_op jit(solution)/shard_map/ppermute | solution.py:272
  45.6 6.1 %collective-permute-start.22 = (f32[8,128]{1,0:T(8,128)S(1)}, f32[8,128]{1,0:T(8,128)S(1)}, u32[]{:S(2)}, u32[]{:S(2)}) collective-permute-start(f32[8,128]{1,0:T(8,128)S(1)} %add.12), channel_id=1, source_target_pairs={{0,5},{1,4},{2,7},{3,6},{4,1},{5,0},{6,3},{7,2},{8,13},{9,12},{10,... | collective-permute-start | bytes 12296 | tf_op jit(solution)/shard_map/ppermute | solution.py:272
  49.1 3.6 %collective-permute-start.21 = (f32[8,128]{1,0:T(8,128)S(1)}, f32[8,128]{1,0:T(8,128)S(1)}, u32[]{:S(2)}, u32[]{:S(2)}) collective-permute-start(f32[8,128]{1,0:T(8,128)S(1)} %add.12), channel_id=1, source_target_pairs={{0,4},{1,5},{2,6},{3,7},{4,0},{5,1},{6,2},{7,3},{8,12},{9,13},{10,... | collective-permute-start | bytes 12296 | tf_op jit(solution)/shard_map/ppermute | solution.py:272
  49.6 3.6 %collective-permute-start.20 = (f32[8,128]{1,0:T(8,128)S(1)}, f32[8,128]{1,0:T(8,128)S(1)}, u32[]{:S(2)}, u32[]{:S(2)}) collective-permute-start(f32[8,128]{1,0:T(8,128)S(1)} %add.12), channel_id=1, source_target_pairs={{0,1},{1,0},{2,3},{3,2},{4,5},{5,4},{6,7},{7,6},{8,9},{9,8},{10,11... | collective-permute-start | bytes 12296 | tf_op jit(solution)/shard_map/ppermute | solution.py:272
  49.7 11.0 %collective-permute-start.18 = (f32[128,256]{1,0:T(8,128)S(1)}, f32[128,256]{1,0:T(8,128)S(1)}, u32[]{:S(2)}, u32[]{:S(2)}) collective-permute-start(f32[128,256]{1,0:T(8,128)S(1)} %get-tuple-element.49), channel_id=1, source_target_pairs={{0,1},{1,0},{2,3},{3,2},{4,5},{5,4},{6,7},{7,6},{8,9},{9,8},{10,11... | collective-permute-start | bytes 393224 | tf_op jit(solution)/shard_map/ppermute | solution.py:272
  53.3 5.4 %collective-permute-start.25 = (f32[8,128]{1,0:T(8,128)S(1)}, f32[8,128]{1,0:T(8,128)S(1)}, u32[]{:S(2)}, u32[]{:S(2)}) collective-permute-start(f32[8,128]{1,0:T(8,128)S(1)} %add_add_fusion.refs_0_), channel_id=1, source_target_pairs={{0,24},{1,25},{2,26},{3,27},{4,28},{5,29},{6,30},{7,31},{8,16},{9,... | collective-permute-start | bytes 12296 | tf_op jit(solution)/shard_map/ppermute | solution.py:272
  56.2 4.5 %collective-permute-start.24 = (f32[8,128]{1,0:T(8,128)S(1)}, f32[8,128]{1,0:T(8,128)S(1)}, u32[]{:S(2)}, u32[]{:S(2)}) collective-permute-start(f32[8,128]{1,0:T(8,128)S(1)} %add_add_fusion.refs_0_), channel_id=1, source_target_pairs={{0,16},{1,17},{2,18},{3,19},{4,20},{5,21},{6,22},{7,23},{8,24},{9,... | collective-permute-start | bytes 12296 | tf_op jit(solution)/shard_map/ppermute | solution.py:272
  56.2 4.5 %collective-permute-start.23 = (f32[8,128]{1,0:T(8,128)S(1)}, f32[8,128]{1,0:T(8,128)S(1)}, u32[]{:S(2)}, u32[]{:S(2)}) collective-permute-start(f32[8,128]{1,0:T(8,128)S(1)} %add_add_fusion.refs_0_), channel_id=1, source_target_pairs={{0,8},{1,9},{2,10},{3,11},{4,12},{5,13},{6,14},{7,15},{8,0},{9,1},... | collective-permute-start | bytes 12296 | tf_op jit(solution)/shard_map/ppermute | solution.py:272

commit v5 on v4

--- a/solution.py
+++ b/solution.py
@@ -33,22 +33,13 @@
     index = lax.axis_index("dp") * n_tp + lax.axis_index("tp")
     base = 0
     if load:
-        *outs, x_vmem, sem = refs
+        g_ref, *outs = refs
         (j,) = planes
-        width = plane * sub
         base = lax.bitwise_xor(index, jnp.int32(j * plane)) // plane * plane
-        copy = pltpu.make_async_copy(
-            x_ref.at[:, pl.ds(pl.multiple_of(base * sub, width), width)], x_vmem, sem
-        )
-        copy.start()
-        rows = x_vmem.shape[0]
-        blocks = s_ref.shape[0] - n_tp * rows
+        rows, hd = x_ref.shape[0], g_ref.shape[1]
         for out in outs:
             for h in range(n_tp):
-                hd = s_ref.shape[1]
-                out[:, 2 * sub + h * hd:2 * sub + (h + 1) * hd] = s_ref[blocks + h * rows:blocks + (h + 1) * rows, :]
-        copy.wait()
-        x_ref, s_ref = x_vmem, s_ref.at[:blocks]
+                out[:, 2 * sub + h * hd:2 * sub + (h + 1) * hd] = g_ref[h * rows:(h + 1) * rows, :]
     else:
         outs = refs
     scales = s_ref[...]
@@ -65,26 +56,41 @@
                     outs[h][:, column:column + sub] = values
 
 
-def pack(x, scales, n_tp, plane, planes, keys, core, sub, *load):
+def load_kernel(n_tp, plane, width, j, x_ref, out, sem):
+    index = lax.axis_index("dp") * n_tp + lax.axis_index("tp")
+    base = lax.bitwise_xor(index, jnp.int32(j * plane)) // plane * width
+    copy = pltpu.make_async_copy(x_ref.at[:, pl.ds(pl.multiple_of(base, width), width)], out, sem)
+    copy.start()
+    copy.wait()
+
+
+def load_plane(x, n_tp, plane, width, j):
+    return pl.pallas_call(
+        functools.partial(load_kernel, n_tp, plane, width, j),
+        out_shape=jax.ShapeDtypeStruct((x.shape[0], width), x.dtype),
+        in_specs=[pl.BlockSpec(memory_space=pltpu.HBM)],
+        out_specs=VMEM,
+        scratch_shapes=[pltpu.SemaphoreType.DMA],
+        compiler_params=params(FIRST_LIMIT),
+        cost_estimate=cost(1000 * x.size, 4 * x.size),
+        name="load",
+    )(x)
+
+
+def pack(x, scales, n_tp, plane, planes, keys, core, sub, block, *load):
     rows = x.shape[0]
     extra = load[0].size // rows if load else 0
-    block = x.shape[1] // (scales.shape[0] - (load[0].shape[0] if load else 0))
     outs = len(keys) if load else 2
     width = 2 * sub + extra if load else len(planes) * len(keys) * sub
-    scratch = [
-        pltpu.VMEM((rows, plane * sub), x.dtype),
-        pltpu.SemaphoreType.DMA,
-    ]
     return pl.pallas_call(
         functools.partial(pack_kernel, n_tp, plane, planes, keys, core, sub, block, bool(load)),
         out_shape=[jax.ShapeDtypeStruct((rows, width), jnp.bfloat16)] * outs,
-        in_specs=[pl.BlockSpec(memory_space=pltpu.HBM) if load else VMEM, VMEM],
+        in_specs=[VMEM] * (2 + len(load)),
         out_specs=[VMEM] * outs,
-        scratch_shapes=scratch if load else [],
-        compiler_params=params(FIRST_LIMIT) if load else params(),
+        compiler_params=params(),
         cost_estimate=cost(2 * rows * width * outs, 4 * rows * width * outs),
         name="pack",
-    )(x, scales)
+    )(x, scales, *load)
 
 
 def merge_kernel(own, theirs, *outs):
@@ -272,9 +278,10 @@
         return lax.ppermute(value, AXES, [(i, i ^ distance) for i in range(count)])
 
     order = list(range(depth - 1, -1, -1))
-    joined = jnp.concatenate([scales, value_grad])
-    packed = pack(stash_values, joined, n_tp, plane, order[:1], keys, core, sub, value_grad)
-    mine, theirs = pack(stash_values, scales, n_tp, plane, order[1:], keys, core, sub)
+    block = width // scales.shape[0]
+    start = load_plane(stash_values, n_tp, plane, plane * sub, order[0])
+    packed = pack(start, scales, n_tp, plane, order[:1], keys, core, sub, block, value_grad)
+    mine, theirs = pack(stash_values, scales, n_tp, plane, order[1:], keys, core, sub, block)
     packed += merge(mine, send(theirs, core), sub)
     terms = []
     for n, j in enumerate(order):

time: 61.8 us -> 61.8 us (level)
    pallas_call x2, Pallas kernels: 2.01 us -> 0.93 us  [pack(): pl.pallas_call(functools.partial(pack_kernel, n_tp, plane, planes, keys,...]
    pallas_call x0 -> x1, Pallas kernels: none -> 1.05 us  [load_plane(): pl.pallas_call(functools.partial(load_kernel, n_tp, plane, width, j), out...]
    unnamed x6 -> x8, local copies, waits for them, and re-layouts: 2.31 us -> 2.32 us
where the time goes in v5:
time: 61.8 us; the launch traced here: 61.5 us
  starting transfers between devices  34.3 us (56%)
  waiting for transfers between devices  20.4 us (33%)
  Pallas kernels  4.37 us (7%)
  local copies, waits for them, and re-layouts  2.32 us (4%)
    ppermute x26, starting transfers between devices, send(): return lax.ppermute(value, AXES, [(i, i ^ distance) for i in range(count)])  34.3 us
    ppermute x26, waiting for transfers between devices, send(): return lax.ppermute(value, AXES, [(i, i ^ distance) for i in range(count)])  20.4 us
    unnamed x8, local copies, waits for them, and re-layouts  2.32 us
  transfers between devices with their start and end apart: 26, of which 11 were waited for; matrix products, arithmetic and copies ran while one was open for 0% of the time, Pallas kernels for 5%

profile of v5, /device:TPU:0, one launch (start us, length us, event | category | flops | bytes accessed | tf_op | source)
XLA Modules:
  0.0 61.5 jit_solution(1797320287987352379)
XLA Ops:
  0.0 1.6 %copy-done = bf16[128,8192]{1,0:T(8,128)(2,1)S(1)} copy-done((bf16[128,8192]{1,0:T(8,128)(2,1)S(1)}, bf16[128,8192]{1,0:T(8,128)(2,1)}, u32[]{:S(2)}) %copy-start) | copy-done | bytes 2097176
  1.6 0.7 %copy-done.1 = bf16[128,64]{0,1:T(8,128)(2,1)S(1)} copy-done((bf16[128,64]{0,1:T(8,128)(2,1)S(1)}, bf16[128,64]{0,1:T(8,128)(2,1)}, u32[]{:S(2)}) %copy-start.1) | copy-done | bytes 16408
  2.3 0.6 pack.3
  2.9 0.6 collective-permute-start.4
  3.5 1.0 %load.1.x_ref = bf16[128,2048]{1,0:T(8,128)(2,1)S(1)} custom-call(bf16[128,8192]{1,0:T(8,128)(2,1)} %x_ref.3), custom_call_target="tpu_custom_call" | custom-call | flops 1048576000 | bytes 4194304 | tf_op jit(solution)/shard_map/load/pallas_call | solution.py:68
  4.9 2.6 %collective-permute-start = (bf16[128,768]{1,0:T(8,128)(2,1)S(1)}, bf16[128,768]{1,0:T(8,128)(2,1)S(1)}, u32[]{:S(2)}, u32[]{:S(2)}) collective-permute-start(bf16[128,768]{1,0:T(8,128)(2,1)S(1)} %get-tuple-element.29), channel_id=1, source_target_pairs={{0,1},{1,0},{2,3},{3,2},{4,5},{5,4},{6,7},{7,6},{8,9},{9,8},{10,11... | collective-permute-start | bytes 589832 | tf_op jit(solution)/shard_map/ppermute | solution.py:278
  7.5 1.5 %collective-permute-start.1 = (bf16[128,768]{1,0:T(8,128)(2,1)S(1)}, bf16[128,768]{1,0:T(8,128)(2,1)S(1)}, u32[]{:S(2)}, u32[]{:S(2)}) collective-permute-start(bf16[128,768]{1,0:T(8,128)(2,1)S(1)} %get-tuple-element.30), channel_id=1, source_target_pairs={{0,4},{1,5},{2,6},{3,7},{4,0},{5,1},{6,2},{7,3},{8,12},{9,13},{10,... | collective-permute-start | bytes 589832 | tf_op jit(solution)/shard_map/ppermute | solution.py:278
  9.0 4.0 %collective-permute-done.refs_1_ = bf16[128,768]{1,0:T(8,128)(2,1)S(1)} collective-permute-done((bf16[128,768]{1,0:T(8,128)(2,1)S(1)}, bf16[128,768]{1,0:T(8,128)(2,1)S(1)}, u32[]{:S(2)}, u32[]{:S(2)}) %collective-permute-start) | collective-permute-done | bytes 196640 | tf_op jit(solution)/shard_map/ppermute | solution.py:278
  13.1 2.2 %collective-permute-done.1.refs_2_ = bf16[128,768]{1,0:T(8,128)(2,1)S(1)} collective-permute-done((bf16[128,768]{1,0:T(8,128)(2,1)S(1)}, bf16[128,768]{1,0:T(8,128)(2,1)S(1)}, u32[]{:S(2)}, u32[]{:S(2)}) %collective-permute-start.1) | collective-permute-done | bytes 196640 | tf_op jit(solution)/shard_map/ppermute | solution.py:278
  15.3 3.2 %collective-permute-done.2.refs_3_ = bf16[128,768]{1,0:T(8,128)(2,1)S(1)} collective-permute-done((bf16[128,768]{1,0:T(8,128)(2,1)S(1)}, bf16[128,768]{1,0:T(8,128)(2,1)S(1)}, u32[]{:S(2)}, u32[]{:S(2)}) %collective-permute-start.2) | collective-permute-done | bytes 196640 | tf_op jit(solution)/shard_map/ppermute | solution.py:278
  19.6 1.7 %collective-permute-start.8 = (bf16[256,256]{1,0:T(8,128)(2,1)S(1)}, bf16[256,256]{1,0:T(8,128)(2,1)S(1)}, u32[]{:S(2)}, u32[]{:S(2)}) collective-permute-start(bf16[256,256]{1,0:T(8,128)(2,1)S(1)} %get-tuple-element.39), channel_id=1, source_target_pairs={{0,1},{1,0},{2,3},{3,2},{4,5},{5,4},{6,7},{7,6},{8,9},{9,8},{10,11... | collective-permute-start | bytes 393224 | tf_op jit(solution)/shard_map/ppermute | solution.py:278
  21.4 1.5 %collective-permute-start.9 = (bf16[256,256]{1,0:T(8,128)(2,1)S(1)}, bf16[256,256]{1,0:T(8,128)(2,1)S(1)}, u32[]{:S(2)}, u32[]{:S(2)}) collective-permute-start(bf16[256,256]{1,0:T(8,128)(2,1)S(1)} %get-tuple-element.40), channel_id=1, source_target_pairs={{0,4},{1,5},{2,6},{3,7},{4,0},{5,1},{6,2},{7,3},{8,12},{9,13},{10,... | collective-permute-start | bytes 393224 | tf_op jit(solution)/shard_map/ppermute | solution.py:278
  23.2 1.7 %collective-permute-start.12 = (bf16[256,256]{1,0:T(8,128)(2,1)S(1)}, bf16[256,256]{1,0:T(8,128)(2,1)S(1)}, u32[]{:S(2)}, u32[]{:S(2)}) collective-permute-start(bf16[256,256]{1,0:T(8,128)(2,1)S(1)} %get-tuple-element.43), channel_id=1, source_target_pairs={{0,1},{1,0},{2,3},{3,2},{4,5},{5,4},{6,7},{7,6},{8,9},{9,8},{10,11... | collective-permute-start | bytes 393224 | tf_op jit(solution)/shard_map/ppermute | solution.py:278
  24.9 1.5 %collective-permute-start.13 = (bf16[256,256]{1,0:T(8,128)(2,1)S(1)}, bf16[256,256]{1,0:T(8,128)(2,1)S(1)}, u32[]{:S(2)}, u32[]{:S(2)}) collective-permute-start(bf16[256,256]{1,0:T(8,128)(2,1)S(1)} %get-tuple-element.44), channel_id=1, source_target_pairs={{0,4},{1,5},{2,6},{3,7},{4,0},{5,1},{6,2},{7,3},{8,12},{9,13},{10,... | collective-permute-start | bytes 393224 | tf_op jit(solution)/shard_map/ppermute | solution.py:278
  26.4 1.7 %collective-permute-start.14 = (bf16[256,256]{1,0:T(8,128)(2,1)S(1)}, bf16[256,256]{1,0:T(8,128)(2,1)S(1)}, u32[]{:S(2)}, u32[]{:S(2)}) collective-permute-start(bf16[256,256]{1,0:T(8,128)(2,1)S(1)} %get-tuple-element.45), channel_id=1, source_target_pairs={{0,5},{1,4},{2,7},{3,6},{4,1},{5,0},{6,3},{7,2},{8,13},{9,12},{10,... | collective-permute-start | bytes 393224 | tf_op jit(solution)/shard_map/ppermute | solution.py:278
  28.6 1.6 %collective-permute-done.10.refs_3_ = bf16[256,256]{1,0:T(8,128)(2,1)S(1)} collective-permute-done((bf16[256,256]{1,0:T(8,128)(2,1)S(1)}, bf16[256,256]{1,0:T(8,128)(2,1)S(1)}, u32[]{:S(2)}, u32[]{:S(2)}) %collective-permute-start.10) | collective-permute-done | bytes 131104 | tf_op jit(solution)/shard_map/ppermute | solution.py:278
  30.2 3.6 %collective-permute-start.17 = (bf16[256,256]{1,0:T(8,128)(2,1)S(1)}, bf16[256,256]{1,0:T(8,128)(2,1)S(1)}, u32[]{:S(2)}, u32[]{:S(2)}) collective-permute-start(bf16[256,256]{1,0:T(8,128)(2,1)S(1)} %join.1), channel_id=1, source_target_pairs={{0,24},{1,25},{2,26},{3,27},{4,28},{5,29},{6,30},{7,31},{8,16},{9,... | collective-permute-start | bytes 393224 | tf_op jit(solution)/shard_map/ppermute | solution.py:278
  34.1 1.9 %collective-permute-start.6 = (bf16[256,256]{1,0:T(8,128)(2,1)S(1)}, bf16[256,256]{1,0:T(8,128)(2,1)S(1)}, u32[]{:S(2)}, u32[]{:S(2)}) collective-permute-start(bf16[256,256]{1,0:T(8,128)(2,1)S(1)} %get-tuple-element.36), channel_id=1, source_target_pairs={{0,4},{1,5},{2,6},{3,7},{4,0},{5,1},{6,2},{7,3},{8,12},{9,13},{10,... | collective-permute-start | bytes 393224 | tf_op jit(solution)/shard_map/ppermute | solution.py:278
  36.0 1.5 %collective-permute-start.7 = (bf16[256,256]{1,0:T(8,128)(2,1)S(1)}, bf16[256,256]{1,0:T(8,128)(2,1)S(1)}, u32[]{:S(2)}, u32[]{:S(2)}) collective-permute-start(bf16[256,256]{1,0:T(8,128)(2,1)S(1)} %get-tuple-element.37), channel_id=1, source_target_pairs={{0,5},{1,4},{2,7},{3,6},{4,1},{5,0},{6,3},{7,2},{8,13},{9,12},{10,... | collective-permute-start | bytes 393224 | tf_op jit(solution)/shard_map/ppermute | solution.py:278
  37.8 2.6 %collective-permute-start.15 = (bf16[256,256]{1,0:T(8,128)(2,1)S(1)}, bf16[256,256]{1,0:T(8,128)(2,1)S(1)}, u32[]{:S(2)}, u32[]{:S(2)}) collective-permute-start(bf16[256,256]{1,0:T(8,128)(2,1)S(1)} %product.5), channel_id=1, source_target_pairs={{0,16},{1,17},{2,18},{3,19},{4,20},{5,21},{6,22},{7,23},{8,24},{9,... | collective-permute-start | bytes 393224 | tf_op jit(solution)/shard_map/ppermute | solution.py:278
  40.4 1.5 %collective-permute-done.7.refs_3_ = bf16[256,256]{1,0:T(8,128)(2,1)S(1)} collective-permute-done((bf16[256,256]{1,0:T(8,128)(2,1)S(1)}, bf16[256,256]{1,0:T(8,128)(2,1)S(1)}, u32[]{:S(2)}, u32[]{:S(2)}) %collective-permute-start.7) | collective-permute-done | bytes 131104 | tf_op jit(solution)/shard_map/ppermute | solution.py:278
  42.2 2.1 %collective-permute-done.11.refs_1_ = bf16[256,256]{1,0:T(8,128)(2,1)S(1)} collective-permute-done((bf16[256,256]{1,0:T(8,128)(2,1)S(1)}, bf16[256,256]{1,0:T(8,128)(2,1)S(1)}, u32[]{:S(2)}, u32[]{:S(2)}) %collective-permute-start.11) | collective-permute-done | bytes 131104 | tf_op jit(solution)/shard_map/ppermute | solution.py:278
  44.5 1.2 %collective-permute-done.19 = f32[8,128]{1,0:T(8,128)S(1)} collective-permute-done((f32[8,128]{1,0:T(8,128)S(1)}, f32[8,128]{1,0:T(8,128)S(1)}, u32[]{:S(2)}, u32[]{:S(2)}) %collective-permute-start.19) | collective-permute-done | bytes 4128 | tf_op jit(solution)/shard_map/ppermute | solution.py:278
  45.6 3.5 %collective-permute-start.22 = (f32[8,128]{1,0:T(8,128)S(1)}, f32[8,128]{1,0:T(8,128)S(1)}, u32[]{:S(2)}, u32[]{:S(2)}) collective-permute-start(f32[8,128]{1,0:T(8,128)S(1)} %add.12), channel_id=1, source_target_pairs={{0,5},{1,4},{2,7},{3,6},{4,1},{5,0},{6,3},{7,2},{8,13},{9,12},{10,... | collective-permute-start | bytes 12296 | tf_op jit(solution)/shard_map/ppermute | solution.py:278
  49.7 2.0 %collective-permute-start.18 = (f32[128,256]{1,0:T(8,128)S(1)}, f32[128,256]{1,0:T(8,128)S(1)}, u32[]{:S(2)}, u32[]{:S(2)}) collective-permute-start(f32[128,256]{1,0:T(8,128)S(1)} %get-tuple-element.49), channel_id=1, source_target_pairs={{0,1},{1,0},{2,3},{3,2},{4,5},{5,4},{6,7},{7,6},{8,9},{9,8},{10,11... | collective-permute-start | bytes 393224 | tf_op jit(solution)/shard_map/ppermute | solution.py:278
  51.7 1.0 %collective-permute-done.21 = f32[8,128]{1,0:T(8,128)S(1)} collective-permute-done((f32[8,128]{1,0:T(8,128)S(1)}, f32[8,128]{1,0:T(8,128)S(1)}, u32[]{:S(2)}, u32[]{:S(2)}) %collective-permute-start.21) | collective-permute-done | bytes 4128 | tf_op jit(solution)/shard_map/ppermute | solution.py:278
  52.7 0.6 collective-permute-done.20
  53.3 2.9 %collective-permute-start.25 = (f32[8,128]{1,0:T(8,128)S(1)}, f32[8,128]{1,0:T(8,128)S(1)}, u32[]{:S(2)}, u32[]{:S(2)}) collective-permute-start(f32[8,128]{1,0:T(8,128)S(1)} %add_add_fusion.refs_0_), channel_id=1, source_target_pairs={{0,24},{1,25},{2,26},{3,27},{4,28},{5,29},{6,30},{7,31},{8,16},{9,... | collective-permute-start | bytes 12296 | tf_op jit(solution)/shard_map/ppermute | solution.py:278
  56.2 1.5 %collective-permute-start.23 = (f32[8,128]{1,0:T(8,128)S(1)}, f32[8,128]{1,0:T(8,128)S(1)}, u32[]{:S(2)}, u32[]{:S(2)}) collective-permute-start(f32[8,128]{1,0:T(8,128)S(1)} %add_add_fusion.refs_0_), channel_id=1, source_target_pairs={{0,8},{1,9},{2,10},{3,11},{4,12},{5,13},{6,14},{7,15},{8,0},{9,1},... | collective-permute-start | bytes 12296 | tf_op jit(solution)/shard_map/ppermute | solution.py:278
  57.7 1.0 %collective-permute-done.25.refs_3_ = f32[8,128]{1,0:T(8,128)S(1)} collective-permute-done((f32[8,128]{1,0:T(8,128)S(1)}, f32[8,128]{1,0:T(8,128)S(1)}, u32[]{:S(2)}, u32[]{:S(2)}) %collective-permute-start.25) | collective-permute-done | bytes 4128 | tf_op jit(solution)/shard_map/ppermute | solution.py:278
  58.7 2.0 %collective-permute-done.24.refs_2_ = f32[8,128]{1,0:T(8,128)S(1)} collective-permute-done((f32[8,128]{1,0:T(8,128)S(1)}, f32[8,128]{1,0:T(8,128)S(1)}, u32[]{:S(2)}, u32[]{:S(2)}) %collective-permute-start.24) | collective-permute-done | bytes 4128 | tf_op jit(solution)/shard_map/ppermute | solution.py:278
  60.7 0.9 %clip.1 = f32[512,128]{1,0:T(8,128)} custom-call(f32[128,256]{1,0:T(8,128)S(1)} %get-tuple-element.48.own, f32[128,256]{1,0:T(8,128)S(1)} %collective-permute-done.18.other, f32[8,128]{1,0:T(8,128)S(1)} %add_add_fusion.refs_0_, f32[8,128]{1,0:T(8,128)S(1)} %collective-permute-done.23.refs_1_, f32[8,128]{1,0:T(8,128)S(1)} %collective-permute-done.24.refs_2_, ...), custom_call_target="tpu_custom_call" | custom-call | flops 131072 | bytes 524288 | tf_op jit(solution)/shard_map/clip/pallas_call | solution.py:246
  (42 shorter events, 4.0 us)
Async XLA Ops:
  0.0 1.6 %copy-start = (bf16[128,8192]{1,0:T(8,128)(2,1)S(1)}, bf16[128,8192]{1,0:T(8,128)(2,1)}, u32[]{:S(2)}) copy-start(bf16[128,8192]{1,0:T(8,128)(2,1)} %x_ref.3) | copy-start | bytes 6291460
  1.6 0.7 %copy-start.1 = (bf16[128,64]{0,1:T(8,128)(2,1)S(1)}, bf16[128,64]{0,1:T(8,128)(2,1)}, u32[]{:S(2)}) copy-start(bf16[128,64]{0,1:T(8,128)(2,1)} %param.4) | copy-start | bytes 49156
  2.9 1.6 %copy-start.2 = (bf16[128,64]{0,1:T(8,128)(2,1)S(1)}, bf16[128,64]{0,1:T(8,128)(2,1)}, u32[]{:S(2)}) copy-start(bf16[128,64]{0,1:T(8,128)(2,1)} %param.4) | copy-start | bytes 49156
  2.9 1.6 %copy-start.3 = (bf16[256,128]{1,0:T(8,128)(2,1)S(1)}, bf16[256,128]{1,0:T(8,128)(2,1)}, u32[]{:S(2)}) copy-start(bf16[256,128]{1,0:T(8,128)(2,1)} %refs_0_.1) | copy-start | bytes 196612
  2.9 16.6 %collective-permute-start.4 = (bf16[128,3072]{1,0:T(8,128)(2,1)S(1)}, bf16[128,3072]{1,0:T(8,128)(2,1)S(1)}, u32[]{:S(2)}, u32[]{:S(2)}) collective-permute-start(bf16[128,3072]{1,0:T(8,128)(2,1)S(1)} %get-tuple-element.33), channel_id=1, source_target_pairs={{0,2},{1,3},{2,0},{3,1},{4,6},{5,7},{6,4},{7,5},{8,10},{9,11},{10,... | collective-permute-start | bytes 2359304 | tf_op jit(solution)/shard_map/ppermute | solution.py:278
  4.9 8.1 %collective-permute-start = (bf16[128,768]{1,0:T(8,128)(2,1)S(1)}, bf16[128,768]{1,0:T(8,128)(2,1)S(1)}, u32[]{:S(2)}, u32[]{:S(2)}) collective-permute-start(bf16[128,768]{1,0:T(8,128)(2,1)S(1)} %get-tuple-element.29), channel_id=1, source_target_pairs={{0,1},{1,0},{2,3},{3,2},{4,5},{5,4},{6,7},{7,6},{8,9},{9,8},{10,11... | collective-permute-start | bytes 589832 | tf_op jit(solution)/shard_map/ppermute | solution.py:278
  7.5 7.8 %collective-permute-start.1 = (bf16[128,768]{1,0:T(8,128)(2,1)S(1)}, bf16[128,768]{1,0:T(8,128)(2,1)S(1)}, u32[]{:S(2)}, u32[]{:S(2)}) collective-permute-start(bf16[128,768]{1,0:T(8,128)(2,1)S(1)} %get-tuple-element.30), channel_id=1, source_target_pairs={{0,4},{1,5},{2,6},{3,7},{4,0},{5,1},{6,2},{7,3},{8,12},{9,13},{10,... | collective-permute-start | bytes 589832 | tf_op jit(solution)/shard_map/ppermute | solution.py:278
  9.0 9.5 %collective-permute-start.2 = (bf16[128,768]{1,0:T(8,128)(2,1)S(1)}, bf16[128,768]{1,0:T(8,128)(2,1)S(1)}, u32[]{:S(2)}, u32[]{:S(2)}) collective-permute-start(bf16[128,768]{1,0:T(8,128)(2,1)S(1)} %get-tuple-element.31), channel_id=1, source_target_pairs={{0,5},{1,4},{2,7},{3,6},{4,1},{5,0},{6,3},{7,2},{8,13},{9,12},{10,... | collective-permute-start | bytes 589832 | tf_op jit(solution)/shard_map/ppermute | solution.py:278
  19.0 4.2 %collective-permute-start.16 = (f32[256,256]{1,0:T(8,128)S(1)}, f32[256,256]{1,0:T(8,128)S(1)}, u32[]{:S(2)}, u32[]{:S(2)}) collective-permute-start(f32[256,256]{1,0:T(8,128)S(1)} %get-tuple-element.47), channel_id=1, source_target_pairs={{0,2},{1,3},{2,0},{3,1},{4,6},{5,7},{6,4},{7,5},{8,10},{9,11},{10,... | collective-permute-start | bytes 786440 | tf_op jit(solution)/shard_map/ppermute | solution.py:278
  19.0 5.8 %collective-permute-start.3 = (bf16[256,512]{1,0:T(8,128)(2,1)S(1)}, bf16[256,512]{1,0:T(8,128)(2,1)S(1)}, u32[]{:S(2)}, u32[]{:S(2)}) collective-permute-start(bf16[256,512]{1,0:T(8,128)(2,1)S(1)} %grads.1.gt_a.gt_ref), channel_id=1, source_target_pairs={{0,2},{1,3},{2,0},{3,1},{4,6},{5,7},{6,4},{7,5},{8,10},{9,11},{10,... | collective-permute-start | bytes 786440 | tf_op jit(solution)/shard_map/ppermute | solution.py:278
  19.6 6.7 %collective-permute-start.8 = (bf16[256,256]{1,0:T(8,128)(2,1)S(1)}, bf16[256,256]{1,0:T(8,128)(2,1)S(1)}, u32[]{:S(2)}, u32[]{:S(2)}) collective-permute-start(bf16[256,256]{1,0:T(8,128)(2,1)S(1)} %get-tuple-element.39), channel_id=1, source_target_pairs={{0,1},{1,0},{2,3},{3,2},{4,5},{5,4},{6,7},{7,6},{8,9},{9,8},{10,11... | collective-permute-start | bytes 393224 | tf_op jit(solution)/shard_map/ppermute | solution.py:278
  21.4 6.7 %collective-permute-start.9 = (bf16[256,256]{1,0:T(8,128)(2,1)S(1)}, bf16[256,256]{1,0:T(8,128)(2,1)S(1)}, u32[]{:S(2)}, u32[]{:S(2)}) collective-permute-start(bf16[256,256]{1,0:T(8,128)(2,1)S(1)} %get-tuple-element.40), channel_id=1, source_target_pairs={{0,4},{1,5},{2,6},{3,7},{4,0},{5,1},{6,2},{7,3},{8,12},{9,13},{10,... | collective-permute-start | bytes 393224 | tf_op jit(solution)/shard_map/ppermute | solution.py:278
  22.9 7.3 %collective-permute-start.10 = (bf16[256,256]{1,0:T(8,128)(2,1)S(1)}, bf16[256,256]{1,0:T(8,128)(2,1)S(1)}, u32[]{:S(2)}, u32[]{:S(2)}) collective-permute-start(bf16[256,256]{1,0:T(8,128)(2,1)S(1)} %get-tuple-element.41), channel_id=1, source_target_pairs={{0,5},{1,4},{2,7},{3,6},{4,1},{5,0},{6,3},{7,2},{8,13},{9,12},{10,... | collective-permute-start | bytes 393224 | tf_op jit(solution)/shard_map/ppermute | solution.py:278
  23.2 10.9 %collective-permute-start.12 = (bf16[256,256]{1,0:T(8,128)(2,1)S(1)}, bf16[256,256]{1,0:T(8,128)(2,1)S(1)}, u32[]{:S(2)}, u32[]{:S(2)}) collective-permute-start(bf16[256,256]{1,0:T(8,128)(2,1)S(1)} %get-tuple-element.43), channel_id=1, source_target_pairs={{0,1},{1,0},{2,3},{3,2},{4,5},{5,4},{6,7},{7,6},{8,9},{9,8},{10,11... | collective-permute-start | bytes 393224 | tf_op jit(solution)/shard_map/ppermute | solution.py:278
  24.9 11.1 %collective-permute-start.13 = (bf16[256,256]{1,0:T(8,128)(2,1)S(1)}, bf16[256,256]{1,0:T(8,128)(2,1)S(1)}, u32[]{:S(2)}, u32[]{:S(2)}) collective-permute-start(bf16[256,256]{1,0:T(8,128)(2,1)S(1)} %get-tuple-element.44), channel_id=1, source_target_pairs={{0,4},{1,5},{2,6},{3,7},{4,0},{5,1},{6,2},{7,3},{8,12},{9,13},{10,... | collective-permute-start | bytes 393224 | tf_op jit(solution)/shard_map/ppermute | solution.py:278
  26.4 11.1 %collective-permute-start.14 = (bf16[256,256]{1,0:T(8,128)(2,1)S(1)}, bf16[256,256]{1,0:T(8,128)(2,1)S(1)}, u32[]{:S(2)}, u32[]{:S(2)}) collective-permute-start(bf16[256,256]{1,0:T(8,128)(2,1)S(1)} %get-tuple-element.45), channel_id=1, source_target_pairs={{0,5},{1,4},{2,7},{3,6},{4,1},{5,0},{6,3},{7,2},{8,13},{9,12},{10,... | collective-permute-start | bytes 393224 | tf_op jit(solution)/shard_map/ppermute | solution.py:278
  28.1 9.7 %collective-permute-start.5 = (bf16[256,256]{1,0:T(8,128)(2,1)S(1)}, bf16[256,256]{1,0:T(8,128)(2,1)S(1)}, u32[]{:S(2)}, u32[]{:S(2)}) collective-permute-start(bf16[256,256]{1,0:T(8,128)(2,1)S(1)} %get-tuple-element.35), channel_id=1, source_target_pairs={{0,1},{1,0},{2,3},{3,2},{4,5},{5,4},{6,7},{7,6},{8,9},{9,8},{10,11... | collective-permute-start | bytes 393224 | tf_op jit(solution)/shard_map/ppermute | solution.py:278
  30.2 12.0 %collective-permute-start.17 = (bf16[256,256]{1,0:T(8,128)(2,1)S(1)}, bf16[256,256]{1,0:T(8,128)(2,1)S(1)}, u32[]{:S(2)}, u32[]{:S(2)}) collective-permute-start(bf16[256,256]{1,0:T(8,128)(2,1)S(1)} %join.1), channel_id=1, source_target_pairs={{0,24},{1,25},{2,26},{3,27},{4,28},{5,29},{6,30},{7,31},{8,16},{9,... | collective-permute-start | bytes 393224 | tf_op jit(solution)/shard_map/ppermute | solution.py:278
  34.1 6.3 %collective-permute-start.6 = (bf16[256,256]{1,0:T(8,128)(2,1)S(1)}, bf16[256,256]{1,0:T(8,128)(2,1)S(1)}, u32[]{:S(2)}, u32[]{:S(2)}) collective-permute-start(bf16[256,256]{1,0:T(8,128)(2,1)S(1)} %get-tuple-element.36), channel_id=1, source_target_pairs={{0,4},{1,5},{2,6},{3,7},{4,0},{5,1},{6,2},{7,3},{8,12},{9,13},{10,... | collective-permute-start | bytes 393224 | tf_op jit(solution)/shard_map/ppermute | solution.py:278
  36.0 5.9 %collective-permute-start.7 = (bf16[256,256]{1,0:T(8,128)(2,1)S(1)}, bf16[256,256]{1,0:T(8,128)(2,1)S(1)}, u32[]{:S(2)}, u32[]{:S(2)}) collective-permute-start(bf16[256,256]{1,0:T(8,128)(2,1)S(1)} %get-tuple-element.37), channel_id=1, source_target_pairs={{0,5},{1,4},{2,7},{3,6},{4,1},{5,0},{6,3},{7,2},{8,13},{9,12},{10,... | collective-permute-start | bytes 393224 | tf_op jit(solution)/shard_map/ppermute | solution.py:278
  37.5 6.8 %collective-permute-start.11 = (bf16[256,256]{1,0:T(8,128)(2,1)S(1)}, bf16[256,256]{1,0:T(8,128)(2,1)S(1)}, u32[]{:S(2)}, u32[]{:S(2)}) collective-permute-start(bf16[256,256]{1,0:T(8,128)(2,1)S(1)} %product.4), channel_id=1, source_target_pairs={{0,8},{1,9},{2,10},{3,11},{4,12},{5,13},{6,14},{7,15},{8,0},{9,1},... | collective-permute-start | bytes 393224 | tf_op jit(solution)/shard_map/ppermute | solution.py:278
  37.8 6.5 %collective-permute-start.15 = (bf16[256,256]{1,0:T(8,128)(2,1)S(1)}, bf16[256,256]{1,0:T(8,128)(2,1)S(1)}, u32[]{:S(2)}, u32[]{:S(2)}) collective-permute-start(bf16[256,256]{1,0:T(8,128)(2,1)S(1)} %product.5), channel_id=1, source_target_pairs={{0,16},{1,17},{2,18},{3,19},{4,20},{5,21},{6,22},{7,23},{8,24},{9,... | collective-permute-start | bytes 393224 | tf_op jit(solution)/shard_map/ppermute | solution.py:278
  44.4 1.2 %collective-permute-start.19 = (f32[8,128]{1,0:T(8,128)S(1)}, f32[8,128]{1,0:T(8,128)S(1)}, u32[]{:S(2)}, u32[]{:S(2)}) collective-permute-start(f32[8,128]{1,0:T(8,128)S(1)} %get-tuple-element.50), channel_id=1, source_target_pairs={{0,2},{1,3},{2,0},{3,1},{4,6},{5,7},{6,4},{7,5},{8,10},{9,11},{10,... | collective-permute-start | bytes 12296 | tf_op jit(solution)/shard_map/ppermute | solution.py:278
  45.6 6.1 %collective-permute-start.22 = (f32[8,128]{1,0:T(8,128)S(1)}, f32[8,128]{1,0:T(8,128)S(1)}, u32[]{:S(2)}, u32[]{:S(2)}) collective-permute-start(f32[8,128]{1,0:T(8,128)S(1)} %add.12), channel_id=1, source_target_pairs={{0,5},{1,4},{2,7},{3,6},{4,1},{5,0},{6,3},{7,2},{8,13},{9,12},{10,... | collective-permute-start | bytes 12296 | tf_op jit(solution)/shard_map/ppermute | solution.py:278
  49.1 3.6 %collective-permute-start.21 = (f32[8,128]{1,0:T(8,128)S(1)}, f32[8,128]{1,0:T(8,128)S(1)}, u32[]{:S(2)}, u32[]{:S(2)}) collective-permute-start(f32[8,128]{1,0:T(8,128)S(1)} %add.12), channel_id=1, source_target_pairs={{0,4},{1,5},{2,6},{3,7},{4,0},{5,1},{6,2},{7,3},{8,12},{9,13},{10,... | collective-permute-start | bytes 12296 | tf_op jit(solution)/shard_map/ppermute | solution.py:278
  49.6 3.6 %collective-permute-start.20 = (f32[8,128]{1,0:T(8,128)S(1)}, f32[8,128]{1,0:T(8,128)S(1)}, u32[]{:S(2)}, u32[]{:S(2)}) collective-permute-start(f32[8,128]{1,0:T(8,128)S(1)} %add.12), channel_id=1, source_target_pairs={{0,1},{1,0},{2,3},{3,2},{4,5},{5,4},{6,7},{7,6},{8,9},{9,8},{10,11... | collective-permute-start | bytes 12296 | tf_op jit(solution)/shard_map/ppermute | solution.py:278
  49.7 11.0 %collective-permute-start.18 = (f32[128,256]{1,0:T(8,128)S(1)}, f32[128,256]{1,0:T(8,128)S(1)}, u32[]{:S(2)}, u32[]{:S(2)}) collective-permute-start(f32[128,256]{1,0:T(8,128)S(1)} %get-tuple-element.49), channel_id=1, source_target_pairs={{0,1},{1,0},{2,3},{3,2},{4,5},{5,4},{6,7},{7,6},{8,9},{9,8},{10,11... | collective-permute-start | bytes 393224 | tf_op jit(solution)/shard_map/ppermute | solution.py:278
  53.3 5.4 %collective-permute-start.25 = (f32[8,128]{1,0:T(8,128)S(1)}, f32[8,128]{1,0:T(8,128)S(1)}, u32[]{:S(2)}, u32[]{:S(2)}) collective-permute-start(f32[8,128]{1,0:T(8,128)S(1)} %add_add_fusion.refs_0_), channel_id=1, source_target_pairs={{0,24},{1,25},{2,26},{3,27},{4,28},{5,29},{6,30},{7,31},{8,16},{9,... | collective-permute-start | bytes 12296 | tf_op jit(solution)/shard_map/ppermute | solution.py:278
  56.2 4.5 %collective-permute-start.24 = (f32[8,128]{1,0:T(8,128)S(1)}, f32[8,128]{1,0:T(8,128)S(1)}, u32[]{:S(2)}, u32[]{:S(2)}) collective-permute-start(f32[8,128]{1,0:T(8,128)S(1)} %add_add_fusion.refs_0_), channel_id=1, source_target_pairs={{0,16},{1,17},{2,18},{3,19},{4,20},{5,21},{6,22},{7,23},{8,24},{9,... | collective-permute-start | bytes 12296 | tf_op jit(solution)/shard_map/ppermute | solution.py:278
  56.2 4.5 %collective-permute-start.23 = (f32[8,128]{1,0:T(8,128)S(1)}, f32[8,128]{1,0:T(8,128)S(1)}, u32[]{:S(2)}, u32[]{:S(2)}) collective-permute-start(f32[8,128]{1,0:T(8,128)S(1)} %add_add_fusion.refs_0_), channel_id=1, source_target_pairs={{0,8},{1,9},{2,10},{3,11},{4,12},{5,13},{6,14},{7,15},{8,0},{9,1},... | collective-permute-start | bytes 12296 | tf_op jit(solution)/shard_map/ppermute | solution.py:278
